TPU v7x, 1024 devices: a whole 4x4x32 slice. The times are simulated.
1024 devices in a mesh: gx: 8 (over z_hi, x), gy: 8 (over y, core), gz: 16 (over z_lo).
Axes of the slice: x: 4, y: 4, z: 32 (z_hi: 2, z_lo: 16; z = z_hi * 16 + z_lo), core: 2. Of those that a mesh axis runs over, the one named last changes fastest.
Arguments:
- vorticity: float32 [3, 64, 128, 2048], P(None, 'gx', 'gy', 'gz'), may hold values from -6 to 6
- velocity: float32 [3, 64, 128, 2048], P(None, 'gx', 'gy', 'gz'), may hold values from -1 to 1
Outputs:
- vorticity_out: float32 [3, 64, 128, 2048], P(None, 'gx', 'gy', 'gz')
All inputs are finite; a program needn't handle non-finite values.
Results may differ from a plain program's by a relative error of at most 0.0003.
Values sent between devices are 32-bit elements; how exact they have to be, the bound alone decides.
No kernel may reach another device: no remote copies, remote signals or barrier semaphores. Data moves between devices by JAX's collectives and lax.ppermute only.
A program may use at most 32 MiB of HBM per device.

v0:
```python
import jax
import jax.numpy as jnp
from jax import lax
from jax.sharding import PartitionSpec as P

SUBSTEPS = 2


time_step = 0.5


def extended(cells, sides, width):
    for axis, dim in sides:
        count = lax.axis_size(axis)
        head = lax.slice_in_dim(cells, 0, width, axis=dim)
        tail = lax.slice_in_dim(cells, cells.shape[dim] - width, cells.shape[dim], axis=dim)
        cells = jnp.concatenate(
            [
                lax.ppermute(tail, axis, [(i, (i + 1) % count) for i in range(count)]),
                cells,
                lax.ppermute(head, axis, [((i + 1) % count, i) for i in range(count)]),
            ],
            axis=dim,
        )
    return cells


def kernel(distance):
    magnitude = jnp.abs(distance)
    near = 1.0 - 2.5 * magnitude * magnitude + 1.5 * magnitude * magnitude * magnitude
    far = 0.5 * (2.0 - magnitude) * (2.0 - magnitude) * (1.0 - magnitude)
    return jnp.where(magnitude < 1.0, near, jnp.where(magnitude < 2.0, far, 0.0))


def spread(current, displace, along):
    widened = None
    for offset in range(-2, 3):
        weighted = kernel(offset - displace) * current
        widths = [(0, 0), (0, 0), (0, 0), (0, 0)]
        widths[along] = (2 + offset, 2 - offset)
        padded = jnp.pad(weighted, widths)
        widened = padded if widened is None else widened + padded
    return widened


def derive(reach, along, length):

    def window(first):
        return lax.slice_in_dim(reach, first, first + length, axis=along)

    return (8.0 * (window(3) - window(1)) - (window(4) - window(0))) / 12.0


def add_edges(interior, leading, trailing, along, length):
    filler_shape = list(interior.shape)
    filler_shape[along] = length - 4
    filler = jnp.zeros(filler_shape, jnp.float32)
    return interior + jnp.concatenate([leading, filler, trailing], axis=along)


def settle(widened, received, along, length):
    interior = lax.slice_in_dim(widened, 2, length + 2, axis=along)
    leading = lax.slice_in_dim(received, 0, 2, axis=along)
    trailing = lax.slice_in_dim(received, 6, 8, axis=along)
    return add_edges(interior, leading, trailing, along, length)


def carry_later(border_strip, along):
    if along == 1:
        return extended(border_strip, (("gx", 1),), 2)
    if along == 2:
        return extended(border_strip, (("gy", 2),), 2)
    return extended(border_strip, (("gz", 3),), 2)


def carry_joined(border_strip, along):
    if along == 1:
        return extended(border_strip, (("gx", 1),), 2)
    if along == 2:
        return extended(border_strip, (("gy", 2),), 2)
    return extended(border_strip, (("gz", 3),), 2)


def edge_layers(widened, along, length):
    return jnp.concatenate(
        [
            lax.slice_in_dim(widened, 0, 2, axis=along),
            lax.slice_in_dim(widened, length + 2, length + 4, axis=along),
        ],
        axis=along,
    )


def local(vorticity, velocity):
    extents = vorticity.shape[1:]
    slopes = [None, None, None]
    current = vorticity
    for substep in range(SUBSTEPS):
        for along in (1, 2, 3):
            length = extents[along - 1]
            widened = spread(current, time_step * velocity[along - 1], along)
            ghosts = edge_layers(widened, along, length)
            if substep == 0:
                border = jnp.concatenate(
                    [
                        lax.slice_in_dim(velocity, 0, 2, axis=along),
                        lax.slice_in_dim(velocity, length - 2, length, axis=along),
                    ],
                    axis=along,
                )
                received = carry_joined(jnp.concatenate([ghosts, border], axis=0), along)
                moving = received[3:]
                reach = jnp.concatenate(
                    [
                        lax.slice_in_dim(moving, 0, 2, axis=along),
                        velocity,
                        lax.slice_in_dim(moving, 6, 8, axis=along),
                    ],
                    axis=along,
                )
                slopes[along - 1] = derive(reach, along, length)
                received = received[:3]
            else:
                received = carry_later(ghosts, along)
            current = settle(widened, received, along, length)
        stretch = current[0] * slopes[0] + current[1] * slopes[1] + current[2] * slopes[2]
        current = current + time_step * stretch
    return current


def solution(mesh):
    placed = (P(None, "gx", "gy", "gz"), P(None, "gx", "gy", "gz"))
    return jax.shard_map(
        local, mesh=mesh, in_specs=placed, out_specs=P(None, "gx", "gy", "gz"), check_vma=False
    )
```

profile of v0, /device:TPU:6, one launch (start us, length us, event | category | flops | bytes accessed | tf_op | source)
XLA Modules:
  0.0 168.0 jit_solution(1054620968516547204)
XLA Ops:
  0.0 1.5 fusion.20
  1.7 0.8 copy-done
  2.5 28.9 %collective-permute-start = (f32[6,2,16,128]{3,2,1,0:T(8,128)S(1)}, f32[6,2,16,128]{3,2,1,0:T(8,128)S(1)}, u32[]{:S(2)}, u32[]{:S(2)}) collective-permute-start(f32[6,2,16,128]{3,2,1,0:T(8,128)S(1)} %get-tuple-element.69), channel_id=1, source_target_pairs={{0,128},{128,256},{256,384},{384,512},{512,640},{640,768},{768,896... | collective-permute-start | bytes 294920 | tf_op jit(solution)/shard_map/ppermute | solution.py:19
  31.4 1.9 %collective-permute-start.1 = (f32[6,2,16,128]{3,2,1,0:T(8,128)S(1)}, f32[6,2,16,128]{3,2,1,0:T(8,128)S(1)}, u32[]{:S(2)}, u32[]{:S(2)}) collective-permute-start(f32[6,2,16,128]{3,2,1,0:T(8,128)S(1)} %get-tuple-element.70), channel_id=1, source_target_pairs={{128,0},{256,128},{384,256},{512,384},{640,512},{768,640},{896,768... | collective-permute-start | bytes 294920 | tf_op jit(solution)/shard_map/ppermute | solution.py:21
  33.4 0.1 fusion.118
  33.8 0.2 copy.82
  34.0 0.2 copy.83
  34.3 4.9 %collective-permute-done = f32[6,2,16,128]{3,2,1,0:T(8,128)S(1)} collective-permute-done((f32[6,2,16,128]{3,2,1,0:T(8,128)S(1)}, f32[6,2,16,128]{3,2,1,0:T(8,128)S(1)}, u32[]{:S(2)}, u32[]{:S(2)}) %collective-permute-start) | collective-permute-done | bytes 98336 | tf_op jit(solution)/shard_map/ppermute | solution.py:19
  39.2 25.0 %collective-permute-done.1 = f32[6,2,16,128]{3,2,1,0:T(8,128)S(1)} collective-permute-done((f32[6,2,16,128]{3,2,1,0:T(8,128)S(1)}, f32[6,2,16,128]{3,2,1,0:T(8,128)S(1)}, u32[]{:S(2)}, u32[]{:S(2)}) %collective-permute-start.1) | collective-permute-done | bytes 98336 | tf_op jit(solution)/shard_map/ppermute | solution.py:21
  64.2 0.1 broadcast_multiply_fusion.27
  64.5 0.1 pad_add_fusion.4
  64.7 2.9 %collective-permute-start.3 = (f32[6,8,2,128]{3,1,2,0:T(8,128)S(1)}, f32[6,8,2,128]{3,1,2,0:T(8,128)S(1)}, u32[]{:S(2)}, u32[]{:S(2)}) collective-permute-start(f32[6,8,2,128]{3,1,2,0:T(8,128)S(1)} %get-tuple-element.87), channel_id=1, source_target_pairs={{16,0},{32,16},{48,32},{64,48},{80,64},{96,80},{112,96},{0,112},{1... | collective-permute-start | bytes 147464 | tf_op jit(solution)/shard_map/ppermute | solution.py:21
  67.6 1.6 collective-permute-done.2
  69.3 0.1 collective-permute-done.3
  69.4 0.1 broadcast_multiply_fusion.1
  69.5 0.1 broadcast_multiply_fusion.29
  69.7 0.5 pad_add_fusion.1
  70.1 0.1 fusion.117
  70.2 0.2 copy.66
  70.4 0.2 copy.67
  70.7 11.3 %collective-permute-start.5 = (f32[6,8,16,2]{2,1,3,0:T(8,128)S(1)}, f32[6,8,16,2]{2,1,3,0:T(8,128)S(1)}, u32[]{:S(2)}, u32[]{:S(2)}) collective-permute-start(f32[6,8,16,2]{2,1,3,0:T(8,128)S(1)} %get-tuple-element.85), channel_id=1, source_target_pairs={{1,0},{2,1},{3,2},{4,3},{5,4},{6,5},{7,6},{8,7},{9,8},{10,9},{11,1... | collective-permute-start | bytes 18440 | tf_op jit(solution)/shard_map/ppermute | solution.py:21
  82.1 1.9 %collective-permute-start.4 = (f32[6,8,16,2]{2,1,3,0:T(8,128)S(1)}, f32[6,8,16,2]{2,1,3,0:T(8,128)S(1)}, u32[]{:S(2)}, u32[]{:S(2)}) collective-permute-start(f32[6,8,16,2]{2,1,3,0:T(8,128)S(1)} %get-tuple-element.84), channel_id=1, source_target_pairs={{0,1},{1,2},{2,3},{3,4},{4,5},{5,6},{6,7},{7,8},{8,9},{9,10},{10,1... | collective-permute-start | bytes 18440 | tf_op jit(solution)/shard_map/ppermute | solution.py:19
  84.0 1.8 %collective-permute-done.5 = f32[6,8,16,2]{2,1,3,0:T(8,128)S(1)} collective-permute-done((f32[6,8,16,2]{2,1,3,0:T(8,128)S(1)}, f32[6,8,16,2]{2,1,3,0:T(8,128)S(1)}, u32[]{:S(2)}, u32[]{:S(2)}) %collective-permute-start.5) | collective-permute-done | bytes 6176 | tf_op jit(solution)/shard_map/ppermute | solution.py:21
  85.8 0.2 copy.74
  86.0 18.9 %collective-permute-done.4 = f32[6,8,16,2]{2,1,3,0:T(8,128)S(1)} collective-permute-done((f32[6,8,16,2]{2,1,3,0:T(8,128)S(1)}, f32[6,8,16,2]{2,1,3,0:T(8,128)S(1)}, u32[]{:S(2)}, u32[]{:S(2)}) %collective-permute-start.4) | collective-permute-done | bytes 6176 | tf_op jit(solution)/shard_map/ppermute | solution.py:19
  105.0 0.2 copy.75
  105.2 0.2 copy.71
  105.4 0.2 copy.70
  105.7 0.2 slice_add_fusion.3
  105.9 0.4 broadcast_multiply_fusion.24
  106.4 1.9 %collective-permute-start.6 = (f32[3,2,16,128]{3,2,1,0:T(8,128)S(1)}, f32[3,2,16,128]{3,2,1,0:T(8,128)S(1)}, u32[]{:S(2)}, u32[]{:S(2)}) collective-permute-start(f32[3,2,16,128]{3,2,1,0:T(8,128)S(1)} %get-tuple-element.16), channel_id=1, source_target_pairs={{0,128},{128,256},{256,384},{384,512},{512,640},{640,768},{768,896... | collective-permute-start | bytes 147464 | tf_op jit(solution)/shard_map/ppermute | solution.py:19
  108.3 3.9 %collective-permute-start.7 = (f32[3,2,16,128]{3,2,1,0:T(8,128)S(1)}, f32[3,2,16,128]{3,2,1,0:T(8,128)S(1)}, u32[]{:S(2)}, u32[]{:S(2)}) collective-permute-start(f32[3,2,16,128]{3,2,1,0:T(8,128)S(1)} %get-tuple-element.17), channel_id=1, source_target_pairs={{128,0},{256,128},{384,256},{512,384},{640,512},{768,640},{896,768... | collective-permute-start | bytes 147464 | tf_op jit(solution)/shard_map/ppermute | solution.py:21
  112.4 22.5 %collective-permute-done.7 = f32[3,2,16,128]{3,2,1,0:T(8,128)S(1)} collective-permute-done((f32[3,2,16,128]{3,2,1,0:T(8,128)S(1)}, f32[3,2,16,128]{3,2,1,0:T(8,128)S(1)}, u32[]{:S(2)}, u32[]{:S(2)}) %collective-permute-start.7) | collective-permute-done | bytes 49184 | tf_op jit(solution)/shard_map/ppermute | solution.py:21
  134.8 0.1 broadcast_multiply_fusion.26
  135.1 1.4 collective-permute-start.9
  136.5 0.1 pad_add_fusion.2
  136.6 1.4 collective-permute-done.9
  138.0 2.9 %collective-permute-done.8 = f32[3,8,2,128]{3,1,2,0:T(8,128)S(1)} collective-permute-done((f32[3,8,2,128]{3,1,2,0:T(8,128)S(1)}, f32[3,8,2,128]{3,1,2,0:T(8,128)S(1)}, u32[]{:S(2)}, u32[]{:S(2)}) %collective-permute-start.8) | collective-permute-done | bytes 24608 | tf_op jit(solution)/shard_map/ppermute | solution.py:19
  141.0 0.1 broadcast_multiply_fusion
  141.1 0.1 broadcast_multiply_fusion.28
  141.2 0.5 pad_add_fusion
  141.7 0.1 fusion.116
  141.8 1.9 %collective-permute-start.10 = (f32[3,8,16,2]{3,2,1,0:T(8,128)S(1)}, f32[3,8,16,2]{3,2,1,0:T(8,128)S(1)}, u32[]{:S(2)}, u32[]{:S(2)}) collective-permute-start(f32[3,8,16,2]{3,2,1,0:T(8,128)S(1)} %get-tuple-element.22), channel_id=1, source_target_pairs={{0,1},{1,2},{2,3},{3,4},{4,5},{5,6},{6,7},{7,8},{8,9},{9,10},{10,1... | collective-permute-start | bytes 9224 | tf_op jit(solution)/shard_map/ppermute | solution.py:19
  143.7 20.1 %collective-permute-start.11 = (f32[3,8,16,2]{3,2,1,0:T(8,128)S(1)}, f32[3,8,16,2]{3,2,1,0:T(8,128)S(1)}, u32[]{:S(2)}, u32[]{:S(2)}) collective-permute-start(f32[3,8,16,2]{3,2,1,0:T(8,128)S(1)} %get-tuple-element.23), channel_id=1, source_target_pairs={{1,0},{2,1},{3,2},{4,3},{5,4},{6,5},{7,6},{8,7},{9,8},{10,9},{11,1... | collective-permute-start | bytes 9224 | tf_op jit(solution)/shard_map/ppermute | solution.py:21
  163.9 1.8 %collective-permute-done.10 = f32[3,8,16,2]{3,2,1,0:T(8,128)S(1)} collective-permute-done((f32[3,8,16,2]{3,2,1,0:T(8,128)S(1)}, f32[3,8,16,2]{3,2,1,0:T(8,128)S(1)}, u32[]{:S(2)}, u32[]{:S(2)}) %collective-permute-start.10) | collective-permute-done | bytes 3104 | tf_op jit(solution)/shard_map/ppermute | solution.py:19
  165.6 1.4 collective-permute-done.11
  167.0 0.2 slice_add_fusion
  167.2 0.8 multiply_add_fusion
  (50 shorter events, 1.2 us)
Async XLA Ops:
  0.0 1.5 copy-start.1
  1.5 0.9 copy-start
  2.5 36.7 %collective-permute-start = (f32[6,2,16,128]{3,2,1,0:T(8,128)S(1)}, f32[6,2,16,128]{3,2,1,0:T(8,128)S(1)}, u32[]{:S(2)}, u32[]{:S(2)}) collective-permute-start(f32[6,2,16,128]{3,2,1,0:T(8,128)S(1)} %get-tuple-element.69), channel_id=1, source_target_pairs={{0,128},{128,256},{256,384},{384,512},{512,640},{640,768},{768,896... | collective-permute-start | bytes 294920 | tf_op jit(solution)/shard_map/ppermute | solution.py:19
  31.4 32.8 %collective-permute-start.1 = (f32[6,2,16,128]{3,2,1,0:T(8,128)S(1)}, f32[6,2,16,128]{3,2,1,0:T(8,128)S(1)}, u32[]{:S(2)}, u32[]{:S(2)}) collective-permute-start(f32[6,2,16,128]{3,2,1,0:T(8,128)S(1)} %get-tuple-element.70), channel_id=1, source_target_pairs={{128,0},{256,128},{384,256},{512,384},{640,512},{768,640},{896,768... | collective-permute-start | bytes 294920 | tf_op jit(solution)/shard_map/ppermute | solution.py:21
  64.5 4.7 %collective-permute-start.2 = (f32[6,8,2,128]{3,1,2,0:T(8,128)S(1)}, f32[6,8,2,128]{3,1,2,0:T(8,128)S(1)}, u32[]{:S(2)}, u32[]{:S(2)}) collective-permute-start(f32[6,8,2,128]{3,1,2,0:T(8,128)S(1)} %get-tuple-element.86), channel_id=1, source_target_pairs={{0,16},{16,32},{32,48},{48,64},{64,80},{80,96},{96,112},{112,0},{1... | collective-permute-start | bytes 147464 | tf_op jit(solution)/shard_map/ppermute | solution.py:19
  64.7 4.7 %collective-permute-start.3 = (f32[6,8,2,128]{3,1,2,0:T(8,128)S(1)}, f32[6,8,2,128]{3,1,2,0:T(8,128)S(1)}, u32[]{:S(2)}, u32[]{:S(2)}) collective-permute-start(f32[6,8,2,128]{3,1,2,0:T(8,128)S(1)} %get-tuple-element.87), channel_id=1, source_target_pairs={{16,0},{32,16},{48,32},{64,48},{80,64},{96,80},{112,96},{0,112},{1... | collective-permute-start | bytes 147464 | tf_op jit(solution)/shard_map/ppermute | solution.py:21
  70.7 15.1 %collective-permute-start.5 = (f32[6,8,16,2]{2,1,3,0:T(8,128)S(1)}, f32[6,8,16,2]{2,1,3,0:T(8,128)S(1)}, u32[]{:S(2)}, u32[]{:S(2)}) collective-permute-start(f32[6,8,16,2]{2,1,3,0:T(8,128)S(1)} %get-tuple-element.85), channel_id=1, source_target_pairs={{1,0},{2,1},{3,2},{4,3},{5,4},{6,5},{7,6},{8,7},{9,8},{10,9},{11,1... | collective-permute-start | bytes 18440 | tf_op jit(solution)/shard_map/ppermute | solution.py:21
  82.1 22.9 %collective-permute-start.4 = (f32[6,8,16,2]{2,1,3,0:T(8,128)S(1)}, f32[6,8,16,2]{2,1,3,0:T(8,128)S(1)}, u32[]{:S(2)}, u32[]{:S(2)}) collective-permute-start(f32[6,8,16,2]{2,1,3,0:T(8,128)S(1)} %get-tuple-element.84), channel_id=1, source_target_pairs={{0,1},{1,2},{2,3},{3,4},{4,5},{5,6},{6,7},{7,8},{8,9},{9,10},{10,1... | collective-permute-start | bytes 18440 | tf_op jit(solution)/shard_map/ppermute | solution.py:19
  106.4 6.0 %collective-permute-start.6 = (f32[3,2,16,128]{3,2,1,0:T(8,128)S(1)}, f32[3,2,16,128]{3,2,1,0:T(8,128)S(1)}, u32[]{:S(2)}, u32[]{:S(2)}) collective-permute-start(f32[3,2,16,128]{3,2,1,0:T(8,128)S(1)} %get-tuple-element.16), channel_id=1, source_target_pairs={{0,128},{128,256},{256,384},{384,512},{512,640},{640,768},{768,896... | collective-permute-start | bytes 147464 | tf_op jit(solution)/shard_map/ppermute | solution.py:19
  108.3 26.5 %collective-permute-start.7 = (f32[3,2,16,128]{3,2,1,0:T(8,128)S(1)}, f32[3,2,16,128]{3,2,1,0:T(8,128)S(1)}, u32[]{:S(2)}, u32[]{:S(2)}) collective-permute-start(f32[3,2,16,128]{3,2,1,0:T(8,128)S(1)} %get-tuple-element.17), channel_id=1, source_target_pairs={{128,0},{256,128},{384,256},{512,384},{640,512},{768,640},{896,768... | collective-permute-start | bytes 147464 | tf_op jit(solution)/shard_map/ppermute | solution.py:21
  135.1 2.9 %collective-permute-start.9 = (f32[3,8,2,128]{3,1,2,0:T(8,128)S(1)}, f32[3,8,2,128]{3,1,2,0:T(8,128)S(1)}, u32[]{:S(2)}, u32[]{:S(2)}) collective-permute-start(f32[3,8,2,128]{3,1,2,0:T(8,128)S(1)} %copy.77), channel_id=1, source_target_pairs={{16,0},{32,16},{48,32},{64,48},{80,64},{96,80},{112,96},{0,112},{1... | collective-permute-start | bytes 73736 | tf_op jit(solution)/shard_map/ppermute | solution.py:21
  136.5 4.5 %collective-permute-start.8 = (f32[3,8,2,128]{3,1,2,0:T(8,128)S(1)}, f32[3,8,2,128]{3,1,2,0:T(8,128)S(1)}, u32[]{:S(2)}, u32[]{:S(2)}) collective-permute-start(f32[3,8,2,128]{3,1,2,0:T(8,128)S(1)} %copy.76), channel_id=1, source_target_pairs={{0,16},{16,32},{32,48},{48,64},{64,80},{80,96},{96,112},{112,0},{1... | collective-permute-start | bytes 73736 | tf_op jit(solution)/shard_map/ppermute | solution.py:19
  141.8 23.8 %collective-permute-start.10 = (f32[3,8,16,2]{3,2,1,0:T(8,128)S(1)}, f32[3,8,16,2]{3,2,1,0:T(8,128)S(1)}, u32[]{:S(2)}, u32[]{:S(2)}) collective-permute-start(f32[3,8,16,2]{3,2,1,0:T(8,128)S(1)} %get-tuple-element.22), channel_id=1, source_target_pairs={{0,1},{1,2},{2,3},{3,4},{4,5},{5,6},{6,7},{7,8},{8,9},{9,10},{10,1... | collective-permute-start | bytes 9224 | tf_op jit(solution)/shard_map/ppermute | solution.py:19
  143.7 23.3 %collective-permute-start.11 = (f32[3,8,16,2]{3,2,1,0:T(8,128)S(1)}, f32[3,8,16,2]{3,2,1,0:T(8,128)S(1)}, u32[]{:S(2)}, u32[]{:S(2)}) collective-permute-start(f32[3,8,16,2]{3,2,1,0:T(8,128)S(1)} %get-tuple-element.23), channel_id=1, source_target_pairs={{1,0},{2,1},{3,2},{4,3},{5,4},{6,5},{7,6},{8,7},{9,8},{10,9},{11,1... | collective-permute-start | bytes 9224 | tf_op jit(solution)/shard_map/ppermute | solution.py:21
where the time goes:
time: 168 us
  waiting for transfers between devices  82.4 us (49%)
  starting transfers between devices  76.3 us (45%)
  other arithmetic  5.56 us (3%)
  local copies, waits for them, and re-layouts  3.31 us (2%)
    ppermute x6, waiting for transfers between devices, extended(): lax.ppermute(head, axis, [((i + 1) % count, i) for i in range(count)])  52.2 us
    ppermute x6, starting transfers between devices, extended(): lax.ppermute(head, axis, [((i + 1) % count, i) for i in range(count)])  41.6 us
    ppermute x6, starting transfers between devices, extended(): lax.ppermute(tail, axis, [(i, (i + 1) % count) for i in range(count)])  34.7 us
    ppermute x6, waiting for transfers between devices, extended(): lax.ppermute(tail, axis, [(i, (i + 1) % count) for i in range(count)])  30.2 us
  transfers between devices with their start and end apart: 12, of which 12 were waited for; matrix products, arithmetic and copies ran while one was open for 1% of the time, Pallas kernels for 0%

commit v1 on v0

v1 whole, which is shorter than its diff:
```python
import jax
import jax.numpy as jnp
from jax import lax
from jax.experimental import pallas as pl
from jax.experimental.pallas import tpu as pltpu
from jax.sharding import PartitionSpec as P

AXES = ("gx", "gy", "gz")
HALF = 0.5


def flat_pairs(mesh, move):
    nx, ny, nz = (mesh.shape[a] for a in AXES)
    pairs = []
    for x in range(nx):
        for y in range(ny):
            for z in range(nz):
                to = move(x, y, z)
                if to is not None:
                    tx, ty, tz = to[0] % nx, to[1] % ny, to[2] % nz
                    pairs.append(((x * ny + y) * nz + z, (tx * ny + ty) * nz + tz))
    return pairs


def lanes_of(shape):
    return lax.broadcasted_iota(jnp.int32, shape, len(shape) - 1)


def rows_of(shape):
    return lax.broadcasted_iota(jnp.int32, shape, len(shape) - 2)


def roll(x, shift, axis):
    shift = shift % x.shape[axis]
    return x if shift == 0 else pltpu.roll(x, shift, axis)


def between(index, first, last):
    return (index >= first) & (index < last)


def pack_x(odd_ref, c_ref, v_ref, a_ref, b_ref):
    high = 4 * odd_ref[0]
    low = 4 - high
    for i in range(3):
        a_ref[i] = c_ref[i, pl.ds(high, 4)]
        a_ref[3 + i] = v_ref[i, pl.ds(high, 4)]
        b_ref[i] = c_ref[i, pl.ds(low, 4)]
        b_ref[3 + i] = v_ref[i, pl.ds(low, 4)]


def x_layer(slot, odd, c_ref, v_ref, lo_ref, hi_ref, field):
    if slot < 4:
        return lo_ref[field, slot]
    if slot < 12:
        return c_ref[field, slot - 4] if field < 3 else v_ref[field - 3, slot - 4]
    return hi_ref[field, slot - 12]


def pack_z(odd_ref, c_ref, v_ref, a_ref, b_ref, lo_ref, hi_ref, left_ref, right_ref):
    odd = odd_ref[0]

    @pl.when(odd == 1)
    def _():
        hi_ref[...] = a_ref[...]
        lo_ref[...] = b_ref[...]

    @pl.when(odd == 0)
    def _():
        hi_ref[...] = b_ref[...]
        lo_ref[...] = a_ref[...]

    lane = lanes_of((16, 128))
    for q in range(4):
        left = jnp.zeros((16, 128), jnp.float32)
        right = left
        for g in range(4):
            for field in range(6):
                at = 32 * g + 4 * field
                x = x_layer(4 * g + q, odd, c_ref, v_ref, lo_ref, hi_ref, field)
                here = between(lane, at, at + 4)
                left = jnp.where(here, roll(x, at, 1), left)
                right = jnp.where(here, roll(x, at + 4, 1), right)
        left_ref[q] = left
        right_ref[q] = right


def pack_y(c_ref, v_ref, lo_ref, hi_ref, zl_ref, zr_ref, down_ref, up_ref):
    upper = rows_of((8, 128)) < 4

    def join(first, second):
        down = jnp.where(upper, first[0:8], roll(second[0:8], 4, 0))
        up = jnp.where(upper, roll(first[8:16], 4, 0), second[8:16])
        return down, up

    for field in range(6):
        for s in range(8):
            pair = [x_layer(t, None, c_ref, v_ref, lo_ref, hi_ref, field) for t in (s, s + 8)]
            down_ref[8 * field + s], up_ref[8 * field + s] = join(*pair)
    for q in range(4):
        down_ref[48 + q], up_ref[48 + q] = join(zl_ref[q], zr_ref[q])


def weights(v):
    t = HALF * jnp.abs(v)
    ahead = v > 0.0
    u = 1.0 - t
    tt = t * t
    centre = 1.0 + tt * (1.5 * t - 2.5)
    near = t * (0.5 + t * (2.0 - 1.5 * t))
    tu = -0.5 * t * u
    behind = tu * u
    far = tu * t
    return (
        jnp.where(ahead, 0.0, far),
        jnp.where(ahead, behind, near),
        centre,
        jnp.where(ahead, near, behind),
        jnp.where(ahead, far, 0.0),
    )


def spread(c, w, axis):
    forth = roll(w[3] * c + roll(w[4] * c, 1, axis), 1, axis)
    back = roll(w[1] * c + roll(w[0] * c, -1, axis), -1, axis)
    return w[2] * c + forth + back


def slope_of(two_back, back, forth, two_forth):
    return (8.0 * (forth - back) - (two_forth - two_back)) * (1.0 / 12.0)


def slope_roll(v, axis):
    return slope_of(roll(v, 2, axis), roll(v, 1, axis), roll(v, -1, axis), roll(v, -2, axis))


def replicate(e):
    lane = lanes_of(e.shape)
    up1, up2 = roll(e, 32, 1), roll(e, 64, 1)
    dn1, dn2 = roll(e, -32, 1), roll(e, -64, 1)
    first, second = lane < 32, lane < 64
    return (
        jnp.where(first, e, jnp.where(second, up1, up2)),
        jnp.where(first, dn1, jnp.where(second, e, up1)),
        jnp.where(first, dn2, jnp.where(second, dn1, e)),
    )


def compute(
    c_ref, v_ref, lo_ref, hi_ref, zl_ref, zr_ref, above_ref, below_ref, out_ref,
    m_ref, ec_ref, ev_ref, ed_ref, x_ref, ex_ref, s_ref, es_ref, y_ref, ey_ref,
):
    upper = rows_of((8, 128)) < 4

    def halo(entry, second):
        above, below = above_ref[entry], below_ref[entry]
        if second:
            return jnp.where(upper, roll(above, 4, 0), below)
        return jnp.where(upper, above, roll(below, 4, 0))

    for field in range(6):
        for s in range(16):
            m_ref[field, s, 0:16] = x_layer(s, None, c_ref, v_ref, lo_ref, hi_ref, field)
            m_ref[field, s, 16:24] = halo(8 * field + s % 8, s >= 8)
    lane = lanes_of((24, 128))
    for s in range(16):
        g, q = s // 4, s % 4
        zl = jnp.concatenate([zl_ref[q], halo(48 + q, False)], axis=0)
        zr = jnp.concatenate([zr_ref[q], halo(48 + q, True)], axis=0)
        for kind, e_ref in ((0, ec_ref), (1, ev_ref)):
            e = jnp.zeros((24, 128), jnp.float32)
            for i in range(3):
                field = 3 * kind + i
                at = 32 * i
                held = 32 * g + 4 * field
                x = m_ref[field, s]
                e = jnp.where(between(lane, at, at + 4), roll(zl, at - held, 1), e)
                e = jnp.where(between(lane, at + 4, at + 16), roll(x, at + 4, 1), e)
                e = jnp.where(between(lane, at + 16, at + 28), roll(x, at + 28, 1), e)
                e = jnp.where(between(lane, at + 28, at + 32), roll(zr, at + 28 - held, 1), e)
            e_ref[s] = e
        for k, d in enumerate(replicate(ev_ref[s])):
            ed_ref[k, s] = d

    for s in range(2, 14):
        for i in range(3):
            around = [m_ref[3 + i, s + k] for k in (-2, -1, 1, 2)]
            s_ref[0, i, s] = slope_of(*around)
            v = m_ref[3 + i, s]
            s_ref[1, i, s] = slope_roll(v, 0)
            s_ref[2, i, s] = slope_roll(v, 1)
        around = [ev_ref[s + k] for k in (-2, -1, 1, 2)]
        es_ref[0, s] = slope_of(*around)
        v = ev_ref[s]
        es_ref[1, s] = slope_roll(v, 0)
        es_ref[2, s] = slope_roll(v, 1)

    def along_x(sources, v_of, stores, first, last):
        for tile in range(3):
            rows = slice(8 * tile, 8 * tile + 8)
            open_sums = {}
            for p in range(first - 2, last + 2):
                w = weights(v_of(p, rows))
                cs = [source(p, rows) for source in sources]
                for a in range(-2, 3):
                    to = p + a
                    if first <= to < last:
                        terms = [w[a + 2] * c for c in cs]
                        had = open_sums.get(to)
                        open_sums[to] = terms if had is None else [h + t for h, t in zip(had, terms)]
                done = open_sums.pop(p - 2, None)
                if done is not None:
                    for store, value in zip(stores, done):
                        store(p - 2, rows, value)

    def put(ref, *lead):
        def store(p, rows, value):
            ref[(*lead, p, rows)] = value
        return store

    def get(ref, *lead):
        return lambda p, rows: ref[(*lead, p, rows)]

    for substep in range(2):
        first, last = (2, 14) if substep == 0 else (4, 12)
        from_main = m_ref if substep == 0 else y_ref
        from_edge = ec_ref if substep == 0 else ey_ref
        along_x(
            [get(from_main, i) for i in range(3)], get(m_ref, 3),
            [put(x_ref, i) for i in range(3)], first, last,
        )
        along_x([get(from_edge)], get(ed_ref, 0), [put(ex_ref)], first, last)
        for s in range(first, last):
            w = weights(m_ref[4, s])
            cs = [spread(x_ref[i, s], w, 0) for i in range(3)]
            rows = 24 if substep == 0 else 16
            cs = [c[0:rows] for c in cs]
            w = weights(m_ref[5, s, 0:rows])
            cs = [spread(c, w, 1) for c in cs]
            new = []
            for i in range(3):
                stretch = sum(cs[j] * s_ref[j, i, s, 0:rows] for j in range(3))
                new.append(cs[i] + HALF * stretch)
            e = spread(ex_ref[s], weights(ed_ref[1, s]), 0)[0:rows]
            e = spread(e, weights(ed_ref[2, s, 0:rows]), 1)
            parts = replicate(e)
            e = e + HALF * sum(parts[j] * es_ref[j, s, 0:rows] for j in range(3))
            if substep == 0:
                for i in range(3):
                    y_ref[i, s] = new[i]
                ey_ref[s] = e
            else:
                lane16 = lanes_of((16, 128))
                for i in range(3):
                    value = jnp.where(lane16 < 4, roll(e, -(32 * i + 4), 1), new[i])
                    value = jnp.where(lane16 >= 124, roll(e, 100 - 32 * i, 1), value)
                    out_ref[i, s - 4] = value


def call(kernel, outs, scratch=(), scalars=0, operands=0):
    smem = pl.BlockSpec(memory_space=pltpu.SMEM)
    vmem = pl.BlockSpec(memory_space=pltpu.VMEM)
    shapes = [jax.ShapeDtypeStruct(o, jnp.float32) for o in outs]
    return pl.pallas_call(
        kernel,
        out_shape=shapes,
        in_specs=[smem] * scalars + [vmem] * operands,
        out_specs=[vmem] * len(outs),
        scratch_shapes=[pltpu.VMEM(s, jnp.float32) for s in scratch],
        name=kernel.__name__,
    )


def solution(mesh):
    step = 1
    across = flat_pairs(mesh, lambda x, y, z: (x + 1 if x % 2 else x - 1, y, z))
    other = flat_pairs(mesh, lambda x, y, z: (x - 1 if x % 2 else x + 1, y, z))
    y_up = flat_pairs(mesh, lambda x, y, z: (x, y + step, z))
    y_down = flat_pairs(mesh, lambda x, y, z: (x, y - step, z))
    z_up = flat_pairs(mesh, lambda x, y, z: (x, y, z + step))
    z_down = flat_pairs(mesh, lambda x, y, z: (x, y, z - step))

    def send(value, pairs):
        return lax.ppermute(value, AXES, pairs)

    def local(c, v):
        odd = (lax.axis_index("gx") % 2).astype(jnp.int32).reshape(1)
        layers = (6, 4, 16, 128)
        a, b = call(pack_x, [layers, layers], (), 1, 2)(odd, c, v)
        b = send(b, other)
        a = send(a, across)
        edge = (4, 16, 128)
        lo, hi, left, right = call(pack_z, [layers, layers, edge, edge], (), 1, 4)(odd, c, v, a, b)
        zl = send(right, z_up)
        zr = send(left, z_down)
        down, up = call(pack_y, [(52, 8, 128)] * 2, (), 0, 6)(c, v, lo, hi, zl, zr)
        above = send(down, y_down)
        below = send(up, y_up)
        block = (16, 24, 128)
        scratch = [
            (6, *block), block, block, (3, *block), (3, *block), block,
            (3, 3, *block), (3, *block), (3, *block), block,
        ]
        (out,) = call(compute, [(3, 8, 16, 128)], scratch, 0, 8)(c, v, lo, hi, zl, zr, above, below)
        return out

    placed = P(None, *AXES)
    return jax.shard_map(local, mesh=mesh, in_specs=(placed, placed), out_specs=placed, check_vma=False)
```

time: 168 us -> 124 us (0.74)
  the two profiles are of different devices: /device:TPU:6 before, /device:TPU:998 now
where the time goes in v1:
time: 124 us
  waiting for transfers between devices  61.4 us (50%)
  starting transfers between devices  36 us (29%)
  Pallas kernels  23.6 us (19%)
  local copies, waits for them, and re-layouts  2.67 us (2%)
    ppermute x6, waiting for transfers between devices, send(): return lax.ppermute(value, AXES, pairs)  61.4 us
    ppermute x6, starting transfers between devices, send(): return lax.ppermute(value, AXES, pairs)  36 us
    pallas_call x1, Pallas kernels, local(): call(compute, [(3, 8, 16, 128)], scratch, 0, 8)  17.4 us
    unnamed x12, local copies, waits for them, and re-layouts  2.67 us
  transfers between devices with their start and end apart: 6, of which 4 were waited for; matrix products, arithmetic and copies ran while one was open for 0% of the time, Pallas kernels for 0%

profile of v1, /device:TPU:998, one launch (start us, length us, event | category | flops | bytes accessed | tf_op | source)
XLA Modules:
  0.0 123.7 jit_solution(13365488605145691452)
XLA Ops:
  0.0 1.8 %pack_x.1 = (f32[6,4,16,128]{3,2,1,0:T(8,128)}, f32[6,4,16,128]{3,2,1,0:T(8,128)}) custom-call(s32[1]{0:T(128)} %bitcast.odd_ref, f32[3,8,16,128]{3,2,1,0:T(8,128)} %c_ref.7, f32[3,8,16,128]{3,2,1,0:T(8,128)} %v_ref.7), custom_call_target="tpu_custom_call" | custom-call | tf_op jit(solution)/shard_map/pack_x/pallas_call | solution.py:289
  1.8 12.2 %collective-permute-start = (f32[6,4,16,128]{3,2,1,0:T(8,128)}, f32[6,4,16,128]{3,2,1,0:T(8,128)S(1)}, u32[]{:S(2)}, u32[]{:S(2)}) collective-permute-start(f32[6,4,16,128]{3,2,1,0:T(8,128)} %get-tuple-element.13), channel_id=1, source_target_pairs={{0,896},{1,897},{2,898},{3,899},{4,900},{5,901},{6,902},{7,903},{8... | collective-permute-start | bytes 589832 | tf_op jit(solution)/shard_map/ppermute | solution.py:284
  14.0 1.9 %collective-permute-start.1 = (f32[6,4,16,128]{3,2,1,0:T(8,128)}, f32[6,4,16,128]{3,2,1,0:T(8,128)S(1)}, u32[]{:S(2)}, u32[]{:S(2)}) collective-permute-start(f32[6,4,16,128]{3,2,1,0:T(8,128)} %get-tuple-element.14), channel_id=1, source_target_pairs={{0,128},{1,129},{2,130},{3,131},{4,132},{5,133},{6,134},{7,135},{8... | collective-permute-start | bytes 589832 | tf_op jit(solution)/shard_map/ppermute | solution.py:284
  15.9 34.8 %collective-permute-done.a_ref = f32[6,4,16,128]{3,2,1,0:T(8,128)S(1)} collective-permute-done((f32[6,4,16,128]{3,2,1,0:T(8,128)}, f32[6,4,16,128]{3,2,1,0:T(8,128)S(1)}, u32[]{:S(2)}, u32[]{:S(2)}) %collective-permute-start) | collective-permute-done | bytes 196640 | tf_op jit(solution)/shard_map/ppermute | solution.py:284
  50.7 0.0 copy-start.2
  50.7 0.0 collective-permute-done.1.b_ref
  50.7 0.7 copy-done.2
  51.4 0.0 copy-start.3
  51.4 0.7 copy-done.3
  52.1 2.3 %pack_z.1 = (f32[6,4,16,128]{3,2,1,0:T(8,128)}, f32[6,4,16,128]{3,2,1,0:T(8,128)}, f32[4,16,128]{2,1,0:T(8,128)}, f32[4,16,128]{2,1,0:T(8,128)}) custom-call(s32[1]{0:T(128)} %bitcast.odd_ref, f32[3,8,16,128]{3,2,1,0:T(8,128)} %c_ref.7, f32[3,8,16,128]{3,2,1,0:T(8,128)} %v_ref.7, f32[6,4,16,128]{3,2,1,0:T(8,128)} %copy-done.2, f32[6,4,16,128]{3,2,1,0:T(8,128)} %copy-done.3), custom_call_target="tpu_custom_call" | custom-call | tf_op jit(solution)/shard_map/pack_z/pallas_call | solution.py:293
  54.4 19.4 %collective-permute-start.2 = (f32[4,16,128]{2,1,0:T(8,128)}, f32[4,16,128]{2,1,0:T(8,128)S(1)}, u32[]{:S(2)}, u32[]{:S(2)}) collective-permute-start(f32[4,16,128]{2,1,0:T(8,128)} %get-tuple-element.17), channel_id=1, source_target_pairs={{0,1},{1,2},{2,3},{3,4},{4,5},{5,6},{6,7},{7,8},{8,9},{9,10},{10,1... | collective-permute-start | bytes 98312 | tf_op jit(solution)/shard_map/ppermute | solution.py:284
  73.8 1.9 %collective-permute-start.3 = (f32[4,16,128]{2,1,0:T(8,128)}, f32[4,16,128]{2,1,0:T(8,128)S(1)}, u32[]{:S(2)}, u32[]{:S(2)}) collective-permute-start(f32[4,16,128]{2,1,0:T(8,128)} %get-tuple-element.18), channel_id=1, source_target_pairs={{0,15},{1,0},{2,1},{3,2},{4,3},{5,4},{6,5},{7,6},{8,7},{9,8},{10,9... | collective-permute-start | bytes 98312 | tf_op jit(solution)/shard_map/ppermute | solution.py:284
  75.8 0.0 collective-permute-done.2.zl_ref
  75.8 0.0 copy-start.4
  75.8 20.3 %collective-permute-done.3.zr_ref = f32[4,16,128]{2,1,0:T(8,128)S(1)} collective-permute-done((f32[4,16,128]{2,1,0:T(8,128)}, f32[4,16,128]{2,1,0:T(8,128)S(1)}, u32[]{:S(2)}, u32[]{:S(2)}) %collective-permute-start.3) | collective-permute-done | bytes 32800 | tf_op jit(solution)/shard_map/ppermute | solution.py:284
  96.1 0.0 copy-start.5
  96.1 0.0 copy-done.4
  96.1 0.6 copy-done.5
  96.7 2.0 %pack_y.1 = (f32[52,8,128]{2,1,0:T(8,128)}, f32[52,8,128]{2,1,0:T(8,128)}) custom-call(f32[3,8,16,128]{3,2,1,0:T(8,128)} %c_ref.7, f32[3,8,16,128]{3,2,1,0:T(8,128)} %v_ref.7, f32[6,4,16,128]{3,2,1,0:T(8,128)} %get-tuple-element.15.lo_ref, f32[6,4,16,128]{3,2,1,0:T(8,128)} %get-tuple-element.16.hi_ref, f32[4,16,128]{2,1,0:T(8,128)} %copy-done.4, ...), custom_call_target="tpu_custom_call" | custom-call | tf_op jit(solution)/shard_map/pack_y/pallas_call | solution.py:296
  98.7 0.0 collective-permute-start.4
  98.7 0.5 collective-permute-start.5
  99.2 3.2 %collective-permute-done.4.above_ref = f32[52,8,128]{2,1,0:T(8,128)S(1)} collective-permute-done((f32[52,8,128]{2,1,0:T(8,128)}, f32[52,8,128]{2,1,0:T(8,128)S(1)}, u32[]{:S(2)}, u32[]{:S(2)}) %collective-permute-start.4) | collective-permute-done | bytes 213024 | tf_op jit(solution)/shard_map/ppermute | solution.py:284
  102.4 0.0 copy-start
  102.4 3.2 %collective-permute-done.5.below_ref = f32[52,8,128]{2,1,0:T(8,128)S(1)} collective-permute-done((f32[52,8,128]{2,1,0:T(8,128)}, f32[52,8,128]{2,1,0:T(8,128)S(1)}, u32[]{:S(2)}, u32[]{:S(2)}) %collective-permute-start.5) | collective-permute-done | bytes 213024 | tf_op jit(solution)/shard_map/ppermute | solution.py:284
  105.6 0.0 copy-done
  105.6 0.0 copy-start.1
  105.6 0.7 copy-done.1
  106.3 17.4 %compute.1 = f32[3,8,16,128]{3,2,1,0:T(8,128)} custom-call(f32[3,8,16,128]{3,2,1,0:T(8,128)} %c_ref.7, f32[3,8,16,128]{3,2,1,0:T(8,128)} %v_ref.7, f32[6,4,16,128]{3,2,1,0:T(8,128)} %get-tuple-element.15.lo_ref, f32[6,4,16,128]{3,2,1,0:T(8,128)} %get-tuple-element.16.hi_ref, f32[4,16,128]{2,1,0:T(8,128)} %copy-done.4, f32[4,16,128]{2,1,0:T(8,128)} %copy-done.5, ...), custom_call_target="tpu_custom_call" | custom-call | tf_op jit(solution)/shard_map/compute/pallas_call | solution.py:304
Async XLA Ops:
  1.8 48.9 %collective-permute-start = (f32[6,4,16,128]{3,2,1,0:T(8,128)}, f32[6,4,16,128]{3,2,1,0:T(8,128)S(1)}, u32[]{:S(2)}, u32[]{:S(2)}) collective-permute-start(f32[6,4,16,128]{3,2,1,0:T(8,128)} %get-tuple-element.13), channel_id=1, source_target_pairs={{0,896},{1,897},{2,898},{3,899},{4,900},{5,901},{6,902},{7,903},{8... | collective-permute-start | bytes 589832 | tf_op jit(solution)/shard_map/ppermute | solution.py:284
  14.0 36.7 %collective-permute-start.1 = (f32[6,4,16,128]{3,2,1,0:T(8,128)}, f32[6,4,16,128]{3,2,1,0:T(8,128)S(1)}, u32[]{:S(2)}, u32[]{:S(2)}) collective-permute-start(f32[6,4,16,128]{3,2,1,0:T(8,128)} %get-tuple-element.14), channel_id=1, source_target_pairs={{0,128},{1,129},{2,130},{3,131},{4,132},{5,133},{6,134},{7,135},{8... | collective-permute-start | bytes 589832 | tf_op jit(solution)/shard_map/ppermute | solution.py:284
  50.7 0.7 copy-start.2
  51.4 0.7 copy-start.3
  54.4 21.3 %collective-permute-start.2 = (f32[4,16,128]{2,1,0:T(8,128)}, f32[4,16,128]{2,1,0:T(8,128)S(1)}, u32[]{:S(2)}, u32[]{:S(2)}) collective-permute-start(f32[4,16,128]{2,1,0:T(8,128)} %get-tuple-element.17), channel_id=1, source_target_pairs={{0,1},{1,2},{2,3},{3,4},{4,5},{5,6},{6,7},{7,8},{8,9},{9,10},{10,1... | collective-permute-start | bytes 98312 | tf_op jit(solution)/shard_map/ppermute | solution.py:284
  73.8 22.2 %collective-permute-start.3 = (f32[4,16,128]{2,1,0:T(8,128)}, f32[4,16,128]{2,1,0:T(8,128)S(1)}, u32[]{:S(2)}, u32[]{:S(2)}) collective-permute-start(f32[4,16,128]{2,1,0:T(8,128)} %get-tuple-element.18), channel_id=1, source_target_pairs={{0,15},{1,0},{2,1},{3,2},{4,3},{5,4},{6,5},{7,6},{8,7},{9,8},{10,9... | collective-permute-start | bytes 98312 | tf_op jit(solution)/shard_map/ppermute | solution.py:284
  75.8 20.3 %copy-start.4 = (f32[4,16,128]{2,1,0:T(8,128)}, f32[4,16,128]{2,1,0:T(8,128)S(1)}, u32[]{:S(2)}) copy-start(f32[4,16,128]{2,1,0:T(8,128)S(1)} %collective-permute-done.2.zl_ref) | copy-start | bytes 98308
  96.1 0.6 copy-start.5
  98.7 3.7 %collective-permute-start.4 = (f32[52,8,128]{2,1,0:T(8,128)}, f32[52,8,128]{2,1,0:T(8,128)S(1)}, u32[]{:S(2)}, u32[]{:S(2)}) collective-permute-start(f32[52,8,128]{2,1,0:T(8,128)} %get-tuple-element.19), channel_id=1, source_target_pairs={{0,112},{1,113},{2,114},{3,115},{4,116},{5,117},{6,118},{7,119},{8... | collective-permute-start | bytes 638984 | tf_op jit(solution)/shard_map/ppermute | solution.py:284
  98.7 6.9 %collective-permute-start.5 = (f32[52,8,128]{2,1,0:T(8,128)}, f32[52,8,128]{2,1,0:T(8,128)S(1)}, u32[]{:S(2)}, u32[]{:S(2)}) collective-permute-start(f32[52,8,128]{2,1,0:T(8,128)} %get-tuple-element.20), channel_id=1, source_target_pairs={{0,16},{1,17},{2,18},{3,19},{4,20},{5,21},{6,22},{7,23},{8,24},{9,... | collective-permute-start | bytes 638984 | tf_op jit(solution)/shard_map/ppermute | solution.py:284
  102.4 3.2 %copy-start = (f32[52,8,128]{2,1,0:T(8,128)}, f32[52,8,128]{2,1,0:T(8,128)S(1)}, u32[]{:S(2)}) copy-start(f32[52,8,128]{2,1,0:T(8,128)S(1)} %collective-permute-done.4.above_ref) | copy-start | bytes 638980
  105.6 0.7 copy-start.1

commit v2 on v1

v2 whole, which is shorter than its diff:
```python
import jax
import jax.numpy as jnp
from jax import lax
from jax.experimental import pallas as pl
from jax.experimental.pallas import tpu as pltpu
from jax.sharding import PartitionSpec as P

AXES = ("gx", "gy", "gz")
HALF = 0.5


def flat_pairs(mesh, move):
    nx, ny, nz = (mesh.shape[a] for a in AXES)
    pairs = []
    for x in range(nx):
        for y in range(ny):
            for z in range(nz):
                to = move(x, y, z)
                if to is not None:
                    tx, ty, tz = to[0] % nx, to[1] % ny, to[2] % nz
                    pairs.append(((x * ny + y) * nz + z, (tx * ny + ty) * nz + tz))
    return pairs


def lanes_of(shape):
    return lax.broadcasted_iota(jnp.int32, shape, len(shape) - 1)


def rows_of(shape):
    return lax.broadcasted_iota(jnp.int32, shape, len(shape) - 2)


def roll(x, shift, axis):
    shift = shift % x.shape[axis]
    return x if shift == 0 else pltpu.roll(x, shift, axis)


def between(index, first, last):
    return (index >= first) & (index < last)


def loop(first, last, body, unroll=1):
    def step(i, carry):
        body(i)
        return carry

    lax.fori_loop(first, last, step, 0, unroll=unroll)


def field_of(c_ref, v_ref, field):
    return (c_ref, field) if field < 3 else (v_ref, field - 3)


def pack_x(place_ref, c_ref, v_ref, a_ref, b_ref, edge_ref):
    high = 4 * place_ref[0]
    low = 4 - high
    shift = 4 * place_ref[1]

    def copy(q):
        for field in range(6):
            ref, i = field_of(c_ref, v_ref, field)
            a_ref[field, q] = ref[i, high + q]
            b_ref[field, q] = ref[i, low + q]
        lane = lanes_of((16, 128))
        edge = jnp.zeros((16, 128), jnp.float32)
        for g in (1, 2):
            for field in range(6):
                ref, i = field_of(c_ref, v_ref, field)
                at = 32 * g + 4 * field
                x = pltpu.roll(ref[i, 4 * (g - 1) + q], shift + at, 1)
                edge = jnp.where(between(lane, at, at + 4), x, edge)
        edge_ref[q] = edge

    loop(0, 4, copy)


def lower_upper(odd, a_ref, b_ref, field, q):
    a, b = a_ref[field, q], b_ref[field, q]
    return jnp.where(odd, b, a), jnp.where(odd, a, b)


def pack_z(place_ref, c_ref, v_ref, a_ref, b_ref, left_ref, right_ref):
    odd = place_ref[0] == 1

    def pack(q):
        lane = lanes_of((16, 128))
        left = jnp.zeros((16, 128), jnp.float32)
        right = left
        for field in range(6):
            ref, i = field_of(c_ref, v_ref, field)
            lo, hi = lower_upper(odd, a_ref, b_ref, field, q)
            for g, x in enumerate((lo, ref[i, q], ref[i, 4 + q], hi)):
                at = 32 * g + 4 * field
                here = between(lane, at, at + 4)
                left = jnp.where(here, roll(x, at, 1), left)
                right = jnp.where(here, roll(x, at + 4, 1), right)
        left_ref[q] = left
        right_ref[q] = right

    loop(0, 4, pack)


def pack_y(
    place_ref, c_ref, v_ref, a_ref, b_ref, zl_ref, zr_ref, wrap_ref, wrap_a_ref, wrap_b_ref,
    down_ref, up_ref, zl_out_ref, zr_out_ref,
):
    odd = place_ref[0] == 1
    first_end = place_ref[2] == 1
    last_end = place_ref[3] == 1
    upper = rows_of((8, 128)) < 4

    def join(entry, first, second):
        down_ref[entry] = jnp.where(upper, first[0:8], roll(second[0:8], 4, 0))
        up_ref[entry] = jnp.where(upper, roll(first[8:16], 4, 0), second[8:16])

    def pack(q):
        for field in range(6):
            ref, i = field_of(c_ref, v_ref, field)
            lo, hi = lower_upper(odd, a_ref, b_ref, field, q)
            near, far = ref[i, q], ref[i, 4 + q]
            join(8 * field + q, lo, far)
            join(8 * field + 4 + q, near, hi)
        lane = lanes_of((16, 128))
        wrap_a, wrap_b = roll(wrap_a_ref[q], 64, 1), roll(wrap_b_ref[q], 64, 1)
        lo, hi = jnp.where(odd, wrap_b, wrap_a), jnp.where(odd, wrap_a, wrap_b)
        wrap = jnp.where(lane < 32, lo, jnp.where(lane < 96, wrap_ref[q], hi))
        zl = jnp.where(first_end, wrap, zl_ref[q])
        zr = jnp.where(last_end, wrap, zr_ref[q])
        zl_out_ref[q] = zl
        zr_out_ref[q] = zr
        join(48 + q, zl, zr)

    loop(0, 4, pack)


def weights(v):
    t = HALF * jnp.abs(v)
    ahead = v > 0.0
    u = 1.0 - t
    tt = t * t
    centre = 1.0 + tt * (1.5 * t - 2.5)
    near = t * (0.5 + t * (2.0 - 1.5 * t))
    tu = -0.5 * t * u
    behind = tu * u
    far = tu * t
    return (
        jnp.where(ahead, 0.0, far),
        jnp.where(ahead, behind, near),
        centre,
        jnp.where(ahead, near, behind),
        jnp.where(ahead, far, 0.0),
    )


def spread(c, w, axis):
    near = roll(w[3] * c, 1, axis) + roll(w[1] * c, -1, axis)
    far = roll(w[4] * c, 2, axis) + roll(w[0] * c, -2, axis)
    return w[2] * c + near + far


def slope_of(two_back, back, forth, two_forth):
    return (8.0 * (forth - back) - (two_forth - two_back)) * (1.0 / 12.0)


def slope_roll(v, axis):
    return slope_of(roll(v, 2, axis), roll(v, 1, axis), roll(v, -1, axis), roll(v, -2, axis))


def replicate(e):
    lane = lanes_of(e.shape)
    up1, up2 = roll(e, 32, 1), roll(e, 64, 1)
    dn1, dn2 = roll(e, -32, 1), roll(e, -64, 1)
    first, second = lane < 32, lane < 64
    return (
        jnp.where(first, e, jnp.where(second, up1, up2)),
        jnp.where(first, dn1, jnp.where(second, e, up1)),
        jnp.where(first, dn2, jnp.where(second, dn1, e)),
    )


def compute(
    place_ref, c_ref, v_ref, a_ref, b_ref, zl_ref, zr_ref, above_ref, below_ref, out_ref,
    m_ref, ec_ref, ev_ref, ed_ref, x_ref, ex_ref, s_ref, es_ref,
):
    odd = place_ref[0] == 1
    upper = rows_of((8, 128)) < 4

    def halo(entry):
        above, below = above_ref[entry], below_ref[entry]
        first = jnp.where(upper, above, roll(below, 4, 0))
        return first, jnp.where(upper, roll(above, 4, 0), below)

    def widen(q):
        for field in range(6):
            ref, i = field_of(c_ref, v_ref, field)
            lo, hi = lower_upper(odd, a_ref, b_ref, field, q)
            m_ref[field, q, 0:16] = lo
            m_ref[field, 4 + q, 0:16] = ref[i, q]
            m_ref[field, 8 + q, 0:16] = ref[i, 4 + q]
            m_ref[field, 12 + q, 0:16] = hi
            m_ref[field, q, 16:24], m_ref[field, 8 + q, 16:24] = halo(8 * field + q)
            m_ref[field, 4 + q, 16:24], m_ref[field, 12 + q, 16:24] = halo(8 * field + 4 + q)

    loop(0, 4, widen)

    def edges(s):
        lane = lanes_of((24, 128))
        g, q = lax.shift_right_logical(s, 2), lax.bitwise_and(s, 3)
        zl_halo, zr_halo = halo(48 + q)
        zl = jnp.concatenate([zl_ref[q], zl_halo], axis=0)
        zr = jnp.concatenate([zr_ref[q], zr_halo], axis=0)
        back = 128 - 32 * g
        zl, zr = pltpu.roll(zl, back, 1), pltpu.roll(zr, back, 1)
        for kind, e_ref in ((0, ec_ref), (1, ev_ref)):
            e = jnp.zeros((24, 128), jnp.float32)
            for i in range(3):
                field = 3 * kind + i
                at = 32 * i
                x = m_ref[field, s]
                e = jnp.where(between(lane, at, at + 4), roll(zl, at - 4 * field, 1), e)
                e = jnp.where(between(lane, at + 4, at + 16), roll(x, at + 4, 1), e)
                e = jnp.where(between(lane, at + 16, at + 28), roll(x, at + 28, 1), e)
                e = jnp.where(between(lane, at + 28, at + 32), roll(zr, at + 28 - 4 * field, 1), e)
            e_ref[s] = e
        for k, d in enumerate(replicate(e)):
            ed_ref[k, s] = d

    loop(0, 16, edges, 2)

    def slopes(s):
        for i in range(3):
            v = m_ref[3 + i, s]
            s_ref[0, i, s] = slope_of(*[m_ref[3 + i, s + k] for k in (-2, -1, 1, 2)])
            s_ref[1, i, s] = slope_roll(v, 0)
            s_ref[2, i, s] = slope_roll(v, 1)
        v = ev_ref[s]
        es_ref[0, s] = slope_of(*[ev_ref[s + k] for k in (-2, -1, 1, 2)])
        es_ref[1, s] = slope_roll(v, 0)
        es_ref[2, s] = slope_roll(v, 1)

    loop(2, 14, slopes, 2)

    def along_x(sources, v_of, stores, rows):
        open_sums = {}
        for p in range(16):
            w = weights(v_of(p, rows))
            cs = [source(p, rows) for source in sources]
            for a in range(-2, 3):
                to = p + a
                if 2 <= to < 14:
                    terms = [w[a + 2] * c for c in cs]
                    had = open_sums.get(to)
                    open_sums[to] = terms if had is None else [h + t for h, t in zip(had, terms)]
            done = open_sums.pop(p - 2, None)
            if done is not None:
                for store, value in zip(stores, done):
                    store(p - 2, rows, value)

    def put(ref, *lead):
        def store(p, rows, value):
            ref[(*lead, p, rows)] = value
        return store

    def get(ref, *lead):
        return lambda p, rows: ref[(*lead, p, rows)]

    def tile_along_x(tile):
        rows = pl.ds(pl.multiple_of(8 * tile, 8), 8)
        along_x(
            [get(m_ref, i) for i in range(3)], get(m_ref, 3), [put(x_ref, i) for i in range(3)], rows
        )
        along_x([get(ec_ref)], get(ed_ref, 0), [put(ex_ref)], rows)

    def along_yz(s):
        w = weights(m_ref[4, s])
        cs = [spread(x_ref[i, s], w, 0) for i in range(3)]
        w = weights(m_ref[5, s])
        cs = [spread(c, w, 1) for c in cs]
        e = spread(ex_ref[s], weights(ed_ref[1, s]), 0)
        e = spread(e, weights(ed_ref[2, s]), 1)
        for i in range(3):
            stretch = sum(cs[j] * s_ref[j, i, s] for j in range(3))
            m_ref[i, s] = cs[i] + HALF * stretch
        parts = replicate(e)
        ec_ref[s] = e + HALF * sum(parts[j] * es_ref[j, s] for j in range(3))

    def substep(n):
        loop(0, 3, tile_along_x)
        loop(2, 14, along_yz, 2)

    loop(0, 2, substep)

    def finish(s):
        lane = lanes_of((16, 128))
        e = ec_ref[s + 4, 0:16]
        for i in range(3):
            value = jnp.where(lane < 4, roll(e, -(32 * i + 4), 1), m_ref[i, s + 4, 0:16])
            out_ref[i, s] = jnp.where(lane >= 124, roll(e, 100 - 32 * i, 1), value)

    loop(0, 8, finish, 2)


def call(kernel, outs, scratch=(), operands=0):
    smem = pl.BlockSpec(memory_space=pltpu.SMEM)
    vmem = pl.BlockSpec(memory_space=pltpu.VMEM)
    shapes = [jax.ShapeDtypeStruct(o, jnp.float32) for o in outs]
    return pl.pallas_call(
        kernel,
        out_shape=shapes,
        in_specs=[smem] + [vmem] * operands,
        out_specs=[vmem] * len(outs),
        scratch_shapes=[pltpu.VMEM(s, jnp.float32) for s in scratch],
        compiler_params=pltpu.CompilerParams(vmem_limit_bytes=16 * 1024 * 1024),
        name=kernel.__name__,
    )


def is_far(x):
    return x % 4 in (0, 3)


def solution(mesh):
    end = mesh.shape["gz"] - 1

    def across_of(x):
        return x + 1 if x % 2 else x - 1

    across = flat_pairs(mesh, lambda x, y, z: (across_of(x), y, z))
    other = flat_pairs(mesh, lambda x, y, z: (x - 1 if x % 2 else x + 1, y, z))
    y_up = flat_pairs(mesh, lambda x, y, z: (x, y + 1, z))
    y_down = flat_pairs(mesh, lambda x, y, z: (x, y - 1, z))
    z_up = flat_pairs(mesh, lambda x, y, z: (x, y, z + 1) if z < end else None)
    z_down = flat_pairs(mesh, lambda x, y, z: (x, y, z - 1) if z > 0 else None)
    ends = flat_pairs(mesh, lambda x, y, z: (x, y, end - z) if z in (0, end) else None)
    ends_other = flat_pairs(
        mesh, lambda x, y, z: (x - 1 if x % 2 else x + 1, y, z) if z in (0, end) else None
    )
    ends_across = flat_pairs(
        mesh,
        lambda x, y, z: (across_of(x), y, end - z if is_far(x) else z) if z in (0, end) else None,
    )

    def send(value, pairs):
        return lax.ppermute(value, AXES, pairs)

    def local(c, v):
        x, z = lax.axis_index("gx"), lax.axis_index("gz")
        place = jnp.stack([x % 2, (z > 0).astype(x.dtype), (z == 0).astype(x.dtype), (z == end).astype(x.dtype)])
        place = place.astype(jnp.int32)
        layers = (6, 4, 16, 128)
        edge = (4, 16, 128)
        a, b, own = call(pack_x, [layers, layers, edge], (), 2)(place, c, v)
        a = send(a, across)
        wrap = send(own, ends)
        b = send(b, other)
        wrap_b = send(wrap, ends_other)
        wrap_a = send(jnp.where((x % 4 == 0) | (x % 4 == 3), own, wrap), ends_across)
        left, right = call(pack_z, [edge, edge], (), 4)(place, c, v, a, b)
        zl = send(right, z_up)
        zr = send(left, z_down)
        down, up, zl, zr = call(pack_y, [(52, 8, 128)] * 2 + [edge] * 2, (), 9)(
            place, c, v, a, b, zl, zr, wrap, wrap_a, wrap_b
        )
        above = send(down, y_down)
        below = send(up, y_up)
        block = (16, 24, 128)
        scratch = [
            (6, *block), block, block, (3, *block), (3, *block), block, (3, 3, *block), (3, *block),
        ]
        (out,) = call(compute, [(3, 8, 16, 128)], scratch, 8)(place, c, v, a, b, zl, zr, above, below)
        return out

    placed = P(None, *AXES)
    return jax.shard_map(local, mesh=mesh, in_specs=(placed, placed), out_specs=placed, check_vma=False)
```

time: 124 us -> 104 us (0.84)
  the two profiles are of different devices: /device:TPU:998 before, /device:TPU:6 now
where the time goes in v2:
time: 104 us; the launch traced here: 103 us
  starting transfers between devices  52 us (50%)
  waiting for transfers between devices  36.9 us (35%)
  Pallas kernels  12.4 us (12%)
  local copies, waits for them, and re-layouts  1.86 us (2%)
    ppermute x9, starting transfers between devices, send(): return lax.ppermute(value, AXES, pairs)  52 us
    ppermute x9, waiting for transfers between devices, send(): return lax.ppermute(value, AXES, pairs)  36.9 us
    pallas_call x1, Pallas kernels, local(): call(compute, [(3, 8, 16, 128)], scratch, 8)  9.38 us
  transfers between devices with their start and end apart: 9, of which 5 were waited for; matrix products, arithmetic and copies ran while one was open for 0% of the time, Pallas kernels for 1%

profile of v2, /device:TPU:6, one launch (start us, length us, event | category | flops | bytes accessed | tf_op | source)
XLA Modules:
  0.0 103.4 jit_solution(2237179620273290957)
XLA Ops:
  0.0 0.1 pad_add_fusion.place_ref
  0.1 0.0 copy-start
  0.1 0.9 copy-done
  1.0 0.0 copy-start.2
  1.0 0.9 copy-done.2
  1.9 0.0 copy-start.1
  1.9 0.0 copy-start.3
  1.9 0.9 pack_x.1
  2.9 26.4 %collective-permute-start.4 = (f32[4,16,128]{2,1,0:T(8,128)S(1)}, f32[4,16,128]{2,1,0:T(8,128)S(1)}, u32[]{:S(2)}, u32[]{:S(2)}) collective-permute-start(f32[4,16,128]{2,1,0:T(8,128)S(1)} %get-tuple-element.18), channel_id=1, source_target_pairs={{0,15},{15,0},{16,31},{31,16},{32,47},{47,32},{48,63},{63,48},{64,... | collective-permute-start | bytes 98312 | tf_op jit(solution)/shard_map/ppermute | solution.py:344
  29.3 11.8 %collective-permute-start = (f32[6,4,16,128]{3,2,1,0:T(8,128)S(1)}, f32[6,4,16,128]{3,2,1,0:T(8,128)S(1)}, u32[]{:S(2)}, u32[]{:S(2)}) collective-permute-start(f32[6,4,16,128]{3,2,1,0:T(8,128)S(1)} %get-tuple-element.14), channel_id=1, source_target_pairs={{0,896},{1,897},{2,898},{3,899},{4,900},{5,901},{6,902},{7,903},{8... | collective-permute-start | bytes 589832 | tf_op jit(solution)/shard_map/ppermute | solution.py:344
  41.1 1.9 %collective-permute-start.1 = (f32[6,4,16,128]{3,2,1,0:T(8,128)S(1)}, f32[6,4,16,128]{3,2,1,0:T(8,128)S(1)}, u32[]{:S(2)}, u32[]{:S(2)}) collective-permute-start(f32[6,4,16,128]{3,2,1,0:T(8,128)S(1)} %get-tuple-element.15), channel_id=1, source_target_pairs={{0,128},{1,129},{2,130},{3,131},{4,132},{5,133},{6,134},{7,135},{8... | collective-permute-start | bytes 589832 | tf_op jit(solution)/shard_map/ppermute | solution.py:344
  43.0 0.0 collective-permute-done.4.wrap_ref
  43.0 1.9 %collective-permute-start.5 = (f32[4,16,128]{2,1,0:T(8,128)S(1)}, f32[4,16,128]{2,1,0:T(8,128)S(1)}, u32[]{:S(2)}, u32[]{:S(2)}) collective-permute-start(f32[4,16,128]{2,1,0:T(8,128)S(1)} %broadcast_select_fusion), channel_id=1, source_target_pairs={{0,911},{15,896},{16,927},{31,912},{32,943},{47,928},{48,959},{63,... | collective-permute-start | bytes 98312 | tf_op jit(solution)/shard_map/ppermute | solution.py:344
  45.0 6.1 %collective-permute-start.6 = (f32[4,16,128]{2,1,0:T(8,128)S(1)}, f32[4,16,128]{2,1,0:T(8,128)S(1)}, u32[]{:S(2)}, u32[]{:S(2)}) collective-permute-start(f32[4,16,128]{2,1,0:T(8,128)S(1)} %collective-permute-done.4.wrap_ref), channel_id=1, source_target_pairs={{0,128},{15,143},{16,144},{31,159},{32,160},{47,175},{48,176},{63,... | collective-permute-start | bytes 98312 | tf_op jit(solution)/shard_map/ppermute | solution.py:344
  51.0 26.0 %collective-permute-done.a_ref = f32[6,4,16,128]{3,2,1,0:T(8,128)S(1)} collective-permute-done((f32[6,4,16,128]{3,2,1,0:T(8,128)S(1)}, f32[6,4,16,128]{3,2,1,0:T(8,128)S(1)}, u32[]{:S(2)}, u32[]{:S(2)}) %collective-permute-start) | collective-permute-done | bytes 196640 | tf_op jit(solution)/shard_map/ppermute | solution.py:344
  77.0 0.0 collective-permute-done.1.b_ref
  77.0 0.0 copy-done.1
  77.0 0.0 copy-done.3
  77.0 1.2 %pack_z.1 = (f32[4,16,128]{2,1,0:T(8,128)S(1)}, f32[4,16,128]{2,1,0:T(8,128)S(1)}) custom-call(s32[4]{0:T(128)S(1)} %pad_add_fusion.place_ref, f32[3,8,16,128]{3,2,1,0:T(8,128)S(1)} %copy-done.1, f32[3,8,16,128]{3,2,1,0:T(8,128)S(1)} %copy-done.3, f32[6,4,16,128]{3,2,1,0:T(8,128)S(1)} %collective-permute-done.a_ref, ...), custom_call_target="tpu_custom_call" | custom-call | tf_op jit(solution)/shard_map/pack_z/pallas_call | solution.py:358
  78.2 1.3 %collective-permute-start.2 = (f32[4,16,128]{2,1,0:T(8,128)S(1)}, f32[4,16,128]{2,1,0:T(8,128)S(1)}, u32[]{:S(2)}, u32[]{:S(2)}) collective-permute-start(f32[4,16,128]{2,1,0:T(8,128)S(1)} %get-tuple-element.16), channel_id=1, source_target_pairs={{0,1},{1,2},{2,3},{3,4},{4,5},{5,6},{6,7},{7,8},{8,9},{9,10},{10,1... | collective-permute-start | bytes 98312 | tf_op jit(solution)/shard_map/ppermute | solution.py:344
  79.5 1.3 %collective-permute-start.3 = (f32[4,16,128]{2,1,0:T(8,128)S(1)}, f32[4,16,128]{2,1,0:T(8,128)S(1)}, u32[]{:S(2)}, u32[]{:S(2)}) collective-permute-start(f32[4,16,128]{2,1,0:T(8,128)S(1)} %get-tuple-element.17), channel_id=1, source_target_pairs={{1,0},{2,1},{3,2},{4,3},{5,4},{6,5},{7,6},{8,7},{9,8},{10,9},{11,1... | collective-permute-start | bytes 98312 | tf_op jit(solution)/shard_map/ppermute | solution.py:344
  80.8 0.0 collective-permute-done.5.wrap_a_ref
  80.8 0.0 collective-permute-done.6.wrap_b_ref
  80.8 0.3 collective-permute-done.2.zl_ref
  81.1 4.2 %collective-permute-done.3.zr_ref = f32[4,16,128]{2,1,0:T(8,128)S(1)} collective-permute-done((f32[4,16,128]{2,1,0:T(8,128)S(1)}, f32[4,16,128]{2,1,0:T(8,128)S(1)}, u32[]{:S(2)}, u32[]{:S(2)}) %collective-permute-start.3) | collective-permute-done | bytes 32800 | tf_op jit(solution)/shard_map/ppermute | solution.py:344
  85.3 0.9 pack_y.1
  86.2 1.3 %collective-permute-start.7 = (f32[52,8,128]{2,1,0:T(8,128)S(1)}, f32[52,8,128]{2,1,0:T(8,128)S(1)}, u32[]{:S(2)}, u32[]{:S(2)}) collective-permute-start(f32[52,8,128]{2,1,0:T(8,128)S(1)} %get-tuple-element.21), channel_id=1, source_target_pairs={{0,112},{1,113},{2,114},{3,115},{4,116},{5,117},{6,118},{7,119},{8... | collective-permute-start | bytes 638984 | tf_op jit(solution)/shard_map/ppermute | solution.py:344
  87.5 0.0 collective-permute-start.8
  87.5 3.4 %collective-permute-done.7.above_ref = f32[52,8,128]{2,1,0:T(8,128)S(1)} collective-permute-done((f32[52,8,128]{2,1,0:T(8,128)S(1)}, f32[52,8,128]{2,1,0:T(8,128)S(1)}, u32[]{:S(2)}, u32[]{:S(2)}) %collective-permute-start.7) | collective-permute-done | bytes 213024 | tf_op jit(solution)/shard_map/ppermute | solution.py:344
  90.9 3.1 %collective-permute-done.8.below_ref = f32[52,8,128]{2,1,0:T(8,128)S(1)} collective-permute-done((f32[52,8,128]{2,1,0:T(8,128)S(1)}, f32[52,8,128]{2,1,0:T(8,128)S(1)}, u32[]{:S(2)}, u32[]{:S(2)}) %collective-permute-start.8) | collective-permute-done | bytes 213024 | tf_op jit(solution)/shard_map/ppermute | solution.py:344
  94.0 9.4 %compute.1 = f32[3,8,16,128]{3,2,1,0:T(8,128)} custom-call(s32[4]{0:T(128)S(1)} %pad_add_fusion.place_ref, f32[3,8,16,128]{3,2,1,0:T(8,128)S(1)} %copy-done.1, f32[3,8,16,128]{3,2,1,0:T(8,128)S(1)} %copy-done.3, f32[6,4,16,128]{3,2,1,0:T(8,128)S(1)} %collective-permute-done.a_ref, f32[6,4,16,128]{3,2,1,0:T(8,128)S(1)} %collective-permute-done.1.b_ref, ...), custom_call_target="tpu_custom_call" | custom-call | tf_op jit(solution)/shard_map/compute/pallas_call | solution.py:370
  (1 shorter events, 0.0 us)
Async XLA Ops:
  0.1 0.9 copy-start
  1.0 0.9 copy-start.2
  1.9 75.1 %copy-start.1 = (f32[3,8,16,128]{3,2,1,0:T(8,128)S(1)}, f32[3,8,16,128]{3,2,1,0:T(8,128)}, u32[]{:S(2)}) copy-start(f32[3,8,16,128]{3,2,1,0:T(8,128)} %c_ref.7) | copy-start | bytes 589828
  1.9 75.1 %copy-start.3 = (f32[3,8,16,128]{3,2,1,0:T(8,128)S(1)}, f32[3,8,16,128]{3,2,1,0:T(8,128)}, u32[]{:S(2)}) copy-start(f32[3,8,16,128]{3,2,1,0:T(8,128)} %v_ref.7) | copy-start | bytes 589828
  2.9 40.1 %collective-permute-start.4 = (f32[4,16,128]{2,1,0:T(8,128)S(1)}, f32[4,16,128]{2,1,0:T(8,128)S(1)}, u32[]{:S(2)}, u32[]{:S(2)}) collective-permute-start(f32[4,16,128]{2,1,0:T(8,128)S(1)} %get-tuple-element.18), channel_id=1, source_target_pairs={{0,15},{15,0},{16,31},{31,16},{32,47},{47,32},{48,63},{63,48},{64,... | collective-permute-start | bytes 98312 | tf_op jit(solution)/shard_map/ppermute | solution.py:344
  29.3 47.7 %collective-permute-start = (f32[6,4,16,128]{3,2,1,0:T(8,128)S(1)}, f32[6,4,16,128]{3,2,1,0:T(8,128)S(1)}, u32[]{:S(2)}, u32[]{:S(2)}) collective-permute-start(f32[6,4,16,128]{3,2,1,0:T(8,128)S(1)} %get-tuple-element.14), channel_id=1, source_target_pairs={{0,896},{1,897},{2,898},{3,899},{4,900},{5,901},{6,902},{7,903},{8... | collective-permute-start | bytes 589832 | tf_op jit(solution)/shard_map/ppermute | solution.py:344
  41.1 35.9 %collective-permute-start.1 = (f32[6,4,16,128]{3,2,1,0:T(8,128)S(1)}, f32[6,4,16,128]{3,2,1,0:T(8,128)S(1)}, u32[]{:S(2)}, u32[]{:S(2)}) collective-permute-start(f32[6,4,16,128]{3,2,1,0:T(8,128)S(1)} %get-tuple-element.15), channel_id=1, source_target_pairs={{0,128},{1,129},{2,130},{3,131},{4,132},{5,133},{6,134},{7,135},{8... | collective-permute-start | bytes 589832 | tf_op jit(solution)/shard_map/ppermute | solution.py:344
  43.0 37.8 %collective-permute-start.5 = (f32[4,16,128]{2,1,0:T(8,128)S(1)}, f32[4,16,128]{2,1,0:T(8,128)S(1)}, u32[]{:S(2)}, u32[]{:S(2)}) collective-permute-start(f32[4,16,128]{2,1,0:T(8,128)S(1)} %broadcast_select_fusion), channel_id=1, source_target_pairs={{0,911},{15,896},{16,927},{31,912},{32,943},{47,928},{48,959},{63,... | collective-permute-start | bytes 98312 | tf_op jit(solution)/shard_map/ppermute | solution.py:344
  45.0 35.9 %collective-permute-start.6 = (f32[4,16,128]{2,1,0:T(8,128)S(1)}, f32[4,16,128]{2,1,0:T(8,128)S(1)}, u32[]{:S(2)}, u32[]{:S(2)}) collective-permute-start(f32[4,16,128]{2,1,0:T(8,128)S(1)} %collective-permute-done.4.wrap_ref), channel_id=1, source_target_pairs={{0,128},{15,143},{16,144},{31,159},{32,160},{47,175},{48,176},{63,... | collective-permute-start | bytes 98312 | tf_op jit(solution)/shard_map/ppermute | solution.py:344
  78.2 2.9 %collective-permute-start.2 = (f32[4,16,128]{2,1,0:T(8,128)S(1)}, f32[4,16,128]{2,1,0:T(8,128)S(1)}, u32[]{:S(2)}, u32[]{:S(2)}) collective-permute-start(f32[4,16,128]{2,1,0:T(8,128)S(1)} %get-tuple-element.16), channel_id=1, source_target_pairs={{0,1},{1,2},{2,3},{3,4},{4,5},{5,6},{6,7},{7,8},{8,9},{9,10},{10,1... | collective-permute-start | bytes 98312 | tf_op jit(solution)/shard_map/ppermute | solution.py:344
  79.5 5.8 %collective-permute-start.3 = (f32[4,16,128]{2,1,0:T(8,128)S(1)}, f32[4,16,128]{2,1,0:T(8,128)S(1)}, u32[]{:S(2)}, u32[]{:S(2)}) collective-permute-start(f32[4,16,128]{2,1,0:T(8,128)S(1)} %get-tuple-element.17), channel_id=1, source_target_pairs={{1,0},{2,1},{3,2},{4,3},{5,4},{6,5},{7,6},{8,7},{9,8},{10,9},{11,1... | collective-permute-start | bytes 98312 | tf_op jit(solution)/shard_map/ppermute | solution.py:344
  86.2 4.7 %collective-permute-start.7 = (f32[52,8,128]{2,1,0:T(8,128)S(1)}, f32[52,8,128]{2,1,0:T(8,128)S(1)}, u32[]{:S(2)}, u32[]{:S(2)}) collective-permute-start(f32[52,8,128]{2,1,0:T(8,128)S(1)} %get-tuple-element.21), channel_id=1, source_target_pairs={{0,112},{1,113},{2,114},{3,115},{4,116},{5,117},{6,118},{7,119},{8... | collective-permute-start | bytes 638984 | tf_op jit(solution)/shard_map/ppermute | solution.py:344
  87.5 6.5 %collective-permute-start.8 = (f32[52,8,128]{2,1,0:T(8,128)S(1)}, f32[52,8,128]{2,1,0:T(8,128)S(1)}, u32[]{:S(2)}, u32[]{:S(2)}) collective-permute-start(f32[52,8,128]{2,1,0:T(8,128)S(1)} %get-tuple-element.22), channel_id=1, source_target_pairs={{0,16},{1,17},{2,18},{3,19},{4,20},{5,21},{6,22},{7,23},{8,24},{9,... | collective-permute-start | bytes 638984 | tf_op jit(solution)/shard_map/ppermute | solution.py:344

commit v3 on v2

--- a/solution.py
+++ b/solution.py
@@ -4,6 +4,7 @@
 from jax.experimental import pallas as pl
 from jax.experimental.pallas import tpu as pltpu
 from jax.sharding import PartitionSpec as P
+
 
 AXES = ("gx", "gy", "gz")
 HALF = 0.5
@@ -51,7 +52,7 @@
     return (c_ref, field) if field < 3 else (v_ref, field - 3)
 
 
-def pack_x(place_ref, c_ref, v_ref, a_ref, b_ref, edge_ref):
+def pack_x(place_ref, c_ref, v_ref, ac_ref, av_ref, b_ref, edge_ref):
     high = 4 * place_ref[0]
     low = 4 - high
     shift = 4 * place_ref[1]
@@ -59,7 +60,8 @@
     def copy(q):
         for field in range(6):
             ref, i = field_of(c_ref, v_ref, field)
-            a_ref[field, q] = ref[i, high + q]
+            to, j = field_of(ac_ref, av_ref, field)
+            to[j, q] = ref[i, high + q]
             b_ref[field, q] = ref[i, low + q]
         lane = lanes_of((16, 128))
         edge = jnp.zeros((16, 128), jnp.float32)
@@ -74,12 +76,13 @@
     loop(0, 4, copy)
 
 
-def lower_upper(odd, a_ref, b_ref, field, q):
-    a, b = a_ref[field, q], b_ref[field, q]
+def lower_upper(odd, ac_ref, av_ref, b_ref, field, q):
+    ref, i = field_of(ac_ref, av_ref, field)
+    a, b = ref[i, q], b_ref[field, q]
     return jnp.where(odd, b, a), jnp.where(odd, a, b)
 
 
-def pack_z(place_ref, c_ref, v_ref, a_ref, b_ref, left_ref, right_ref):
+def pack_z(place_ref, c_ref, v_ref, ac_ref, av_ref, b_ref, left_ref, right_ref):
     odd = place_ref[0] == 1
 
     def pack(q):
@@ -88,7 +91,7 @@
         right = left
         for field in range(6):
             ref, i = field_of(c_ref, v_ref, field)
-            lo, hi = lower_upper(odd, a_ref, b_ref, field, q)
+            lo, hi = lower_upper(odd, ac_ref, av_ref, b_ref, field, q)
             for g, x in enumerate((lo, ref[i, q], ref[i, 4 + q], hi)):
                 at = 32 * g + 4 * field
                 here = between(lane, at, at + 4)
@@ -101,7 +104,7 @@
 
 
 def pack_y(
-    place_ref, c_ref, v_ref, a_ref, b_ref, zl_ref, zr_ref, wrap_ref, wrap_a_ref, wrap_b_ref,
+    place_ref, c_ref, v_ref, ac_ref, av_ref, b_ref, zl_ref, zr_ref, wrap_ref, wrap_a_ref, wrap_b_ref,
     down_ref, up_ref, zl_out_ref, zr_out_ref,
 ):
     odd = place_ref[0] == 1
@@ -116,7 +119,7 @@
     def pack(q):
         for field in range(6):
             ref, i = field_of(c_ref, v_ref, field)
-            lo, hi = lower_upper(odd, a_ref, b_ref, field, q)
+            lo, hi = lower_upper(odd, ac_ref, av_ref, b_ref, field, q)
             near, far = ref[i, q], ref[i, 4 + q]
             join(8 * field + q, lo, far)
             join(8 * field + 4 + q, near, hi)
@@ -179,7 +182,7 @@
 
 
 def compute(
-    place_ref, c_ref, v_ref, a_ref, b_ref, zl_ref, zr_ref, above_ref, below_ref, out_ref,
+    place_ref, c_ref, v_ref, ac_ref, av_ref, b_ref, zl_ref, zr_ref, above_ref, below_ref, out_ref,
     m_ref, ec_ref, ev_ref, ed_ref, x_ref, ex_ref, s_ref, es_ref,
 ):
     odd = place_ref[0] == 1
@@ -193,7 +196,7 @@
     def widen(q):
         for field in range(6):
             ref, i = field_of(c_ref, v_ref, field)
-            lo, hi = lower_upper(odd, a_ref, b_ref, field, q)
+            lo, hi = lower_upper(odd, ac_ref, av_ref, b_ref, field, q)
             m_ref[field, q, 0:16] = lo
             m_ref[field, 4 + q, 0:16] = ref[i, q]
             m_ref[field, 8 + q, 0:16] = ref[i, 4 + q]
@@ -259,6 +262,7 @@
     def put(ref, *lead):
         def store(p, rows, value):
             ref[(*lead, p, rows)] = value
+
         return store
 
     def get(ref, *lead):
@@ -311,7 +315,6 @@
         out_specs=[vmem] * len(outs),
         scratch_shapes=[pltpu.VMEM(s, jnp.float32) for s in scratch],
         compiler_params=pltpu.CompilerParams(vmem_limit_bytes=16 * 1024 * 1024),
-        name=kernel.__name__,
     )
 
 
@@ -325,15 +328,24 @@
     def across_of(x):
         return x + 1 if x % 2 else x - 1
 
+    def other_of(x):
+        return x - 1 if x % 2 else x + 1
+
     across = flat_pairs(mesh, lambda x, y, z: (across_of(x), y, z))
-    other = flat_pairs(mesh, lambda x, y, z: (x - 1 if x % 2 else x + 1, y, z))
+    other = flat_pairs(mesh, lambda x, y, z: (other_of(x), y, z))
+    aside = flat_pairs(mesh, lambda x, y, z: (other_of(x), y, z) if is_far(x) else None)
+    relay = flat_pairs(
+        mesh, lambda x, y, z: None if is_far(x) else (other_of(across_of(other_of(x))), y, z)
+    )
+    forward = flat_pairs(mesh, lambda x, y, z: None if is_far(x) else (other_of(x), y, z))
+    beside = flat_pairs(mesh, lambda x, y, z: None if is_far(x) else (across_of(x), y, z))
     y_up = flat_pairs(mesh, lambda x, y, z: (x, y + 1, z))
     y_down = flat_pairs(mesh, lambda x, y, z: (x, y - 1, z))
     z_up = flat_pairs(mesh, lambda x, y, z: (x, y, z + 1) if z < end else None)
     z_down = flat_pairs(mesh, lambda x, y, z: (x, y, z - 1) if z > 0 else None)
     ends = flat_pairs(mesh, lambda x, y, z: (x, y, end - z) if z in (0, end) else None)
     ends_other = flat_pairs(
-        mesh, lambda x, y, z: (x - 1 if x % 2 else x + 1, y, z) if z in (0, end) else None
+        mesh, lambda x, y, z: (other_of(x), y, z) if z in (0, end) else None
     )
     ends_across = flat_pairs(
         mesh,
@@ -347,19 +359,25 @@
         x, z = lax.axis_index("gx"), lax.axis_index("gz")
         place = jnp.stack([x % 2, (z > 0).astype(x.dtype), (z == 0).astype(x.dtype), (z == end).astype(x.dtype)])
         place = place.astype(jnp.int32)
+        far = (x % 4 == 0) | (x % 4 == 3)
         layers = (6, 4, 16, 128)
+        half = (3, 4, 16, 128)
         edge = (4, 16, 128)
-        a, b, own = call(pack_x, [layers, layers, edge], (), 2)(place, c, v)
-        a = send(a, across)
+        ac, av, b, own = call(pack_x, [half, half, layers, edge], (), 2)(place, c, v)
+        passed = send(av, aside)
+        ac = send(ac, across)
+        passed = send(passed, relay)
+        near_av = send(av, beside)
+        av = jnp.where(far, send(passed, forward), near_av)
         wrap = send(own, ends)
         b = send(b, other)
         wrap_b = send(wrap, ends_other)
-        wrap_a = send(jnp.where((x % 4 == 0) | (x % 4 == 3), own, wrap), ends_across)
-        left, right = call(pack_z, [edge, edge], (), 4)(place, c, v, a, b)
+        wrap_a = send(jnp.where(far, own, wrap), ends_across)
+        left, right = call(pack_z, [edge, edge], (), 5)(place, c, v, ac, av, b)
         zl = send(right, z_up)
         zr = send(left, z_down)
-        down, up, zl, zr = call(pack_y, [(52, 8, 128)] * 2 + [edge] * 2, (), 9)(
-            place, c, v, a, b, zl, zr, wrap, wrap_a, wrap_b
+        down, up, zl, zr = call(pack_y, [(52, 8, 128)] * 2 + [edge] * 2, (), 10)(
+            place, c, v, ac, av, b, zl, zr, wrap, wrap_a, wrap_b
         )
         above = send(down, y_down)
         below = send(up, y_up)
@@ -367,7 +385,7 @@
         scratch = [
             (6, *block), block, block, (3, *block), (3, *block), block, (3, 3, *block), (3, *block),
         ]
-        (out,) = call(compute, [(3, 8, 16, 128)], scratch, 8)(place, c, v, a, b, zl, zr, above, below)
+        (out,) = call(compute, [(3, 8, 16, 128)], scratch, 9)(place, c, v, ac, av, b, zl, zr, above, below)
         return out
 
     placed = P(None, *AXES)

time: 104 us -> 93.2 us (0.90)
  waiting for transfers between devices: 36.9 us -> 13.2 us
  starting transfers between devices: 52 us -> 65 us
    ppermute x9 -> x13, waiting for transfers between devices: 36.9 us -> 13.2 us  [send(): return lax.ppermute(value, AXES, pairs)]
    ppermute x9 -> x13, starting transfers between devices: 52 us -> 65 us  [send(): return lax.ppermute(value, AXES, pairs)]
  transfers between devices with their start and end apart: 9 -> 13, of which waited for: 5 -> 5; matrix products, arithmetic and copies ran while one was open for 0% -> 0% of each run, Pallas kernels for 1% -> 1%
where the time goes in v3:
time: 93.2 us; the launch traced here: 92.8 us
  starting transfers between devices  65 us (70%)
  waiting for transfers between devices  13.2 us (14%)
  Pallas kernels  12.4 us (13%)
  local copies, waits for them, and re-layouts  1.87 us (2%)
    ppermute x13, starting transfers between devices, send(): return lax.ppermute(value, AXES, pairs)  65 us
    ppermute x13, waiting for transfers between devices, send(): return lax.ppermute(value, AXES, pairs)  13.2 us
    pallas_call x1, Pallas kernels, local(): call(compute, [(3, 8, 16, 128)], scratch, 9)  9.38 us
    unnamed x8, local copies, waits for them, and re-layouts  1.87 us
  transfers between devices with their start and end apart: 13, of which 5 were waited for; matrix products, arithmetic and copies ran while one was open for 0% of the time, Pallas kernels for 1%

profile of v3, /device:TPU:6, one launch (start us, length us, event | category | flops | bytes accessed | tf_op | source)
XLA Modules:
  0.0 92.8 jit_solution(777966718597771378)
XLA Ops:
  0.0 0.1 pad_add_fusion.place_ref
  0.1 0.0 copy-start
  0.1 0.9 copy-done
  1.0 0.0 copy-start.2
  1.0 0.9 copy-done.2
  1.9 0.9 %shard_map.28 = (f32[3,4,16,128]{3,2,1,0:T(8,128)S(1)}, f32[3,4,16,128]{3,2,1,0:T(8,128)S(1)}, f32[6,4,16,128]{3,2,1,0:T(8,128)S(1)}, f32[4,16,128]{2,1,0:T(8,128)S(1)}) custom-call(s32[4]{0:T(128)S(1)} %pad_add_fusion.place_ref, f32[3,8,16,128]{3,2,1,0:T(8,128)S(1)} %copy-done, f32[3,8,16,128]{3,2,1,0:T(8,128)S(1)} %copy-done.2), custom_call_target="tpu_custom_call" | custom-call | tf_op jit(solution)/shard_map/pallas_call | solution.py:366
  2.9 2.7 %collective-permute-start.1 = (f32[3,4,16,128]{3,2,1,0:T(8,128)S(1)}, f32[3,4,16,128]{3,2,1,0:T(8,128)S(1)}, u32[]{:S(2)}, u32[]{:S(2)}) collective-permute-start(f32[3,4,16,128]{3,2,1,0:T(8,128)S(1)} %get-tuple-element.16), channel_id=1, source_target_pairs={{0,128},{1,129},{2,130},{3,131},{4,132},{5,133},{6,134},{7,135},{8... | collective-permute-start | bytes 294920 | tf_op jit(solution)/shard_map/ppermute | solution.py:356
  5.6 2.2 %collective-permute-done.1 = f32[3,4,16,128]{3,2,1,0:T(8,128)S(1)} collective-permute-done((f32[3,4,16,128]{3,2,1,0:T(8,128)S(1)}, f32[3,4,16,128]{3,2,1,0:T(8,128)S(1)}, u32[]{:S(2)}, u32[]{:S(2)}) %collective-permute-start.1) | collective-permute-done | bytes 98336 | tf_op jit(solution)/shard_map/ppermute | solution.py:356
  7.8 0.7 collective-permute-start.2
  8.5 26.4 %collective-permute-start.8 = (f32[4,16,128]{2,1,0:T(8,128)S(1)}, f32[4,16,128]{2,1,0:T(8,128)S(1)}, u32[]{:S(2)}, u32[]{:S(2)}) collective-permute-start(f32[4,16,128]{2,1,0:T(8,128)S(1)} %get-tuple-element.20), channel_id=1, source_target_pairs={{0,15},{15,0},{16,31},{31,16},{32,47},{47,32},{48,63},{63,48},{64,... | collective-permute-start | bytes 98312 | tf_op jit(solution)/shard_map/ppermute | solution.py:356
  34.9 0.7 collective-permute-start.4
  35.6 12.4 %collective-permute-start = (f32[3,4,16,128]{3,2,1,0:T(8,128)S(1)}, f32[3,4,16,128]{3,2,1,0:T(8,128)S(1)}, u32[]{:S(2)}, u32[]{:S(2)}) collective-permute-start(f32[3,4,16,128]{3,2,1,0:T(8,128)S(1)} %get-tuple-element.15), channel_id=1, source_target_pairs={{0,896},{1,897},{2,898},{3,899},{4,900},{5,901},{6,902},{7,903},{8... | collective-permute-start | bytes 294920 | tf_op jit(solution)/shard_map/ppermute | solution.py:356
  48.0 8.2 %collective-permute-start.5 = (f32[6,4,16,128]{3,2,1,0:T(8,128)S(1)}, f32[6,4,16,128]{3,2,1,0:T(8,128)S(1)}, u32[]{:S(2)}, u32[]{:S(2)}) collective-permute-start(f32[6,4,16,128]{3,2,1,0:T(8,128)S(1)} %get-tuple-element.17), channel_id=1, source_target_pairs={{0,128},{1,129},{2,130},{3,131},{4,132},{5,133},{6,134},{7,135},{8... | collective-permute-start | bytes 589832 | tf_op jit(solution)/shard_map/ppermute | solution.py:356
  56.2 0.0 copy-start.1
  56.3 0.0 copy-start.3
  56.3 0.0 collective-permute-done.2
  56.3 1.4 %collective-permute-start.3 = (f32[3,4,16,128]{3,2,1,0:T(8,128)S(1)}, f32[3,4,16,128]{3,2,1,0:T(8,128)S(1)}, u32[]{:S(2)}, u32[]{:S(2)}) collective-permute-start(f32[3,4,16,128]{3,2,1,0:T(8,128)S(1)} %collective-permute-done.2), channel_id=1, source_target_pairs={{128,0},{129,1},{130,2},{131,3},{132,4},{133,5},{134,6},{135,7},{1... | collective-permute-start | bytes 294920 | tf_op jit(solution)/shard_map/ppermute | solution.py:356
  57.7 0.0 collective-permute-done.8.wrap_ref
  57.7 1.9 %collective-permute-start.9 = (f32[4,16,128]{2,1,0:T(8,128)S(1)}, f32[4,16,128]{2,1,0:T(8,128)S(1)}, u32[]{:S(2)}, u32[]{:S(2)}) collective-permute-start(f32[4,16,128]{2,1,0:T(8,128)S(1)} %broadcast_select_fusion.1), channel_id=1, source_target_pairs={{0,911},{15,896},{16,927},{31,912},{32,943},{47,928},{48,959},{63,... | collective-permute-start | bytes 98312 | tf_op jit(solution)/shard_map/ppermute | solution.py:356
  59.7 0.0 collective-permute-done.4
  59.7 6.8 %collective-permute-start.10 = (f32[4,16,128]{2,1,0:T(8,128)S(1)}, f32[4,16,128]{2,1,0:T(8,128)S(1)}, u32[]{:S(2)}, u32[]{:S(2)}) collective-permute-start(f32[4,16,128]{2,1,0:T(8,128)S(1)} %collective-permute-done.8.wrap_ref), channel_id=1, source_target_pairs={{0,128},{15,143},{16,144},{31,159},{32,160},{47,175},{48,176},{63,... | collective-permute-start | bytes 98312 | tf_op jit(solution)/shard_map/ppermute | solution.py:356
  66.5 0.0 collective-permute-done.3
  66.6 0.0 collective-permute-done.ac_ref
  66.6 0.0 collective-permute-done.5.b_ref
  66.6 0.0 copy-done.1
  66.6 0.0 copy-done.3
  66.6 1.2 %shard_map.29 = (f32[4,16,128]{2,1,0:T(8,128)S(1)}, f32[4,16,128]{2,1,0:T(8,128)S(1)}) custom-call(s32[4]{0:T(128)S(1)} %pad_add_fusion.place_ref, f32[3,8,16,128]{3,2,1,0:T(8,128)S(1)} %copy-done.1, f32[3,8,16,128]{3,2,1,0:T(8,128)S(1)} %copy-done.3, f32[3,4,16,128]{3,2,1,0:T(8,128)S(1)} %collective-permute-done.ac_ref, ...), custom_call_target="tpu_custom_call" | custom-call | tf_op jit(solution)/shard_map/pallas_call | solution.py:376
  67.8 1.3 %collective-permute-start.6 = (f32[4,16,128]{2,1,0:T(8,128)S(1)}, f32[4,16,128]{2,1,0:T(8,128)S(1)}, u32[]{:S(2)}, u32[]{:S(2)}) collective-permute-start(f32[4,16,128]{2,1,0:T(8,128)S(1)} %get-tuple-element.18), channel_id=1, source_target_pairs={{0,1},{1,2},{2,3},{3,4},{4,5},{5,6},{6,7},{7,8},{8,9},{9,10},{10,1... | collective-permute-start | bytes 98312 | tf_op jit(solution)/shard_map/ppermute | solution.py:356
  69.1 1.3 %collective-permute-start.7 = (f32[4,16,128]{2,1,0:T(8,128)S(1)}, f32[4,16,128]{2,1,0:T(8,128)S(1)}, u32[]{:S(2)}, u32[]{:S(2)}) collective-permute-start(f32[4,16,128]{2,1,0:T(8,128)S(1)} %get-tuple-element.19), channel_id=1, source_target_pairs={{1,0},{2,1},{3,2},{4,3},{5,4},{6,5},{7,6},{8,7},{9,8},{10,9},{11,1... | collective-permute-start | bytes 98312 | tf_op jit(solution)/shard_map/ppermute | solution.py:356
  70.4 0.0 collective-permute-done.9.wrap_a_ref
  70.4 0.0 collective-permute-done.10.wrap_b_ref
  70.5 0.3 collective-permute-done.6.zl_ref
  70.7 4.2 %collective-permute-done.7.zr_ref = f32[4,16,128]{2,1,0:T(8,128)S(1)} collective-permute-done((f32[4,16,128]{2,1,0:T(8,128)S(1)}, f32[4,16,128]{2,1,0:T(8,128)S(1)}, u32[]{:S(2)}, u32[]{:S(2)}) %collective-permute-start.7) | collective-permute-done | bytes 32800 | tf_op jit(solution)/shard_map/ppermute | solution.py:356
  74.9 0.9 shard_map.30
  75.8 1.1 %collective-permute-start.11 = (f32[52,8,128]{2,1,0:T(8,128)S(1)}, f32[52,8,128]{2,1,0:T(8,128)S(1)}, u32[]{:S(2)}, u32[]{:S(2)}) collective-permute-start(f32[52,8,128]{2,1,0:T(8,128)S(1)} %get-tuple-element.23), channel_id=1, source_target_pairs={{0,112},{1,113},{2,114},{3,115},{4,116},{5,117},{6,118},{7,119},{8... | collective-permute-start | bytes 638984 | tf_op jit(solution)/shard_map/ppermute | solution.py:356
  76.9 0.0 collective-permute-start.12
  76.9 3.4 %collective-permute-done.11.above_ref = f32[52,8,128]{2,1,0:T(8,128)S(1)} collective-permute-done((f32[52,8,128]{2,1,0:T(8,128)S(1)}, f32[52,8,128]{2,1,0:T(8,128)S(1)}, u32[]{:S(2)}, u32[]{:S(2)}) %collective-permute-start.11) | collective-permute-done | bytes 213024 | tf_op jit(solution)/shard_map/ppermute | solution.py:356
  80.3 3.1 %collective-permute-done.12.below_ref = f32[52,8,128]{2,1,0:T(8,128)S(1)} collective-permute-done((f32[52,8,128]{2,1,0:T(8,128)S(1)}, f32[52,8,128]{2,1,0:T(8,128)S(1)}, u32[]{:S(2)}, u32[]{:S(2)}) %collective-permute-start.12) | collective-permute-done | bytes 213024 | tf_op jit(solution)/shard_map/ppermute | solution.py:356
  83.4 9.4 %shard_map.31 = f32[3,8,16,128]{3,2,1,0:T(8,128)} custom-call(s32[4]{0:T(128)S(1)} %pad_add_fusion.place_ref, f32[3,8,16,128]{3,2,1,0:T(8,128)S(1)} %copy-done.1, f32[3,8,16,128]{3,2,1,0:T(8,128)S(1)} %copy-done.3, f32[3,4,16,128]{3,2,1,0:T(8,128)S(1)} %collective-permute-done.ac_ref, f32[3,4,16,128]{3,2,1,0:T(8,128)S(1)} %broadcast_select_fusion.av_ref, ...), custom_call_target="tpu_custom_call" | custom-call | tf_op jit(solution)/shard_map/pallas_call | solution.py:388
  (2 shorter events, 0.0 us)
Async XLA Ops:
  0.1 0.9 %copy-start = (f32[3,8,16,128]{3,2,1,0:T(8,128)S(1)}, f32[3,8,16,128]{3,2,1,0:T(8,128)}, u32[]{:S(2)}) copy-start(f32[3,8,16,128]{3,2,1,0:T(8,128)} %c_ref.7) | copy-start | bytes 589828
  1.0 0.9 copy-start.2
  2.9 4.9 %collective-permute-start.1 = (f32[3,4,16,128]{3,2,1,0:T(8,128)S(1)}, f32[3,4,16,128]{3,2,1,0:T(8,128)S(1)}, u32[]{:S(2)}, u32[]{:S(2)}) collective-permute-start(f32[3,4,16,128]{3,2,1,0:T(8,128)S(1)} %get-tuple-element.16), channel_id=1, source_target_pairs={{0,128},{1,129},{2,130},{3,131},{4,132},{5,133},{6,134},{7,135},{8... | collective-permute-start | bytes 294920 | tf_op jit(solution)/shard_map/ppermute | solution.py:356
  7.8 48.5 %collective-permute-start.2 = (f32[3,4,16,128]{3,2,1,0:T(8,128)S(1)}, f32[3,4,16,128]{3,2,1,0:T(8,128)S(1)}, u32[]{:S(2)}, u32[]{:S(2)}) collective-permute-start(f32[3,4,16,128]{3,2,1,0:T(8,128)S(1)} %collective-permute-done.1), channel_id=1, source_target_pairs={{128,768},{129,769},{130,770},{131,771},{132,772},{133,773},{134,7... | collective-permute-start | bytes 294920 | tf_op jit(solution)/shard_map/ppermute | solution.py:356
  8.5 49.2 %collective-permute-start.8 = (f32[4,16,128]{2,1,0:T(8,128)S(1)}, f32[4,16,128]{2,1,0:T(8,128)S(1)}, u32[]{:S(2)}, u32[]{:S(2)}) collective-permute-start(f32[4,16,128]{2,1,0:T(8,128)S(1)} %get-tuple-element.20), channel_id=1, source_target_pairs={{0,15},{15,0},{16,31},{31,16},{32,47},{47,32},{48,63},{63,48},{64,... | collective-permute-start | bytes 98312 | tf_op jit(solution)/shard_map/ppermute | solution.py:356
  34.9 24.8 %collective-permute-start.4 = (f32[3,4,16,128]{3,2,1,0:T(8,128)S(1)}, f32[3,4,16,128]{3,2,1,0:T(8,128)S(1)}, u32[]{:S(2)}, u32[]{:S(2)}) collective-permute-start(f32[3,4,16,128]{3,2,1,0:T(8,128)S(1)} %get-tuple-element.16), channel_id=1, source_target_pairs={{128,256},{129,257},{130,258},{131,259},{132,260},{133,261},{134,2... | collective-permute-start | bytes 294920 | tf_op jit(solution)/shard_map/ppermute | solution.py:356
  35.6 31.0 %collective-permute-start = (f32[3,4,16,128]{3,2,1,0:T(8,128)S(1)}, f32[3,4,16,128]{3,2,1,0:T(8,128)S(1)}, u32[]{:S(2)}, u32[]{:S(2)}) collective-permute-start(f32[3,4,16,128]{3,2,1,0:T(8,128)S(1)} %get-tuple-element.15), channel_id=1, source_target_pairs={{0,896},{1,897},{2,898},{3,899},{4,900},{5,901},{6,902},{7,903},{8... | collective-permute-start | bytes 294920 | tf_op jit(solution)/shard_map/ppermute | solution.py:356
  48.0 18.6 %collective-permute-start.5 = (f32[6,4,16,128]{3,2,1,0:T(8,128)S(1)}, f32[6,4,16,128]{3,2,1,0:T(8,128)S(1)}, u32[]{:S(2)}, u32[]{:S(2)}) collective-permute-start(f32[6,4,16,128]{3,2,1,0:T(8,128)S(1)} %get-tuple-element.17), channel_id=1, source_target_pairs={{0,128},{1,129},{2,130},{3,131},{4,132},{5,133},{6,134},{7,135},{8... | collective-permute-start | bytes 589832 | tf_op jit(solution)/shard_map/ppermute | solution.py:356
  56.2 10.3 %copy-start.1 = (f32[3,8,16,128]{3,2,1,0:T(8,128)S(1)}, f32[3,8,16,128]{3,2,1,0:T(8,128)}, u32[]{:S(2)}) copy-start(f32[3,8,16,128]{3,2,1,0:T(8,128)} %c_ref.7) | copy-start | bytes 589828
  56.3 10.3 %copy-start.3 = (f32[3,8,16,128]{3,2,1,0:T(8,128)S(1)}, f32[3,8,16,128]{3,2,1,0:T(8,128)}, u32[]{:S(2)}) copy-start(f32[3,8,16,128]{3,2,1,0:T(8,128)} %v_ref.7) | copy-start | bytes 589828
  56.3 10.3 %collective-permute-start.3 = (f32[3,4,16,128]{3,2,1,0:T(8,128)S(1)}, f32[3,4,16,128]{3,2,1,0:T(8,128)S(1)}, u32[]{:S(2)}, u32[]{:S(2)}) collective-permute-start(f32[3,4,16,128]{3,2,1,0:T(8,128)S(1)} %collective-permute-done.2), channel_id=1, source_target_pairs={{128,0},{129,1},{130,2},{131,3},{132,4},{133,5},{134,6},{135,7},{1... | collective-permute-start | bytes 294920 | tf_op jit(solution)/shard_map/ppermute | solution.py:356
  57.7 12.7 %collective-permute-start.9 = (f32[4,16,128]{2,1,0:T(8,128)S(1)}, f32[4,16,128]{2,1,0:T(8,128)S(1)}, u32[]{:S(2)}, u32[]{:S(2)}) collective-permute-start(f32[4,16,128]{2,1,0:T(8,128)S(1)} %broadcast_select_fusion.1), channel_id=1, source_target_pairs={{0,911},{15,896},{16,927},{31,912},{32,943},{47,928},{48,959},{63,... | collective-permute-start | bytes 98312 | tf_op jit(solution)/shard_map/ppermute | solution.py:356
  59.7 10.8 %collective-permute-start.10 = (f32[4,16,128]{2,1,0:T(8,128)S(1)}, f32[4,16,128]{2,1,0:T(8,128)S(1)}, u32[]{:S(2)}, u32[]{:S(2)}) collective-permute-start(f32[4,16,128]{2,1,0:T(8,128)S(1)} %collective-permute-done.8.wrap_ref), channel_id=1, source_target_pairs={{0,128},{15,143},{16,144},{31,159},{32,160},{47,175},{48,176},{63,... | collective-permute-start | bytes 98312 | tf_op jit(solution)/shard_map/ppermute | solution.py:356
  67.8 2.9 %collective-permute-start.6 = (f32[4,16,128]{2,1,0:T(8,128)S(1)}, f32[4,16,128]{2,1,0:T(8,128)S(1)}, u32[]{:S(2)}, u32[]{:S(2)}) collective-permute-start(f32[4,16,128]{2,1,0:T(8,128)S(1)} %get-tuple-element.18), channel_id=1, source_target_pairs={{0,1},{1,2},{2,3},{3,4},{4,5},{5,6},{6,7},{7,8},{8,9},{9,10},{10,1... | collective-permute-start | bytes 98312 | tf_op jit(solution)/shard_map/ppermute | solution.py:356
  69.1 5.8 %collective-permute-start.7 = (f32[4,16,128]{2,1,0:T(8,128)S(1)}, f32[4,16,128]{2,1,0:T(8,128)S(1)}, u32[]{:S(2)}, u32[]{:S(2)}) collective-permute-start(f32[4,16,128]{2,1,0:T(8,128)S(1)} %get-tuple-element.19), channel_id=1, source_target_pairs={{1,0},{2,1},{3,2},{4,3},{5,4},{6,5},{7,6},{8,7},{9,8},{10,9},{11,1... | collective-permute-start | bytes 98312 | tf_op jit(solution)/shard_map/ppermute | solution.py:356
  75.8 4.4 %collective-permute-start.11 = (f32[52,8,128]{2,1,0:T(8,128)S(1)}, f32[52,8,128]{2,1,0:T(8,128)S(1)}, u32[]{:S(2)}, u32[]{:S(2)}) collective-permute-start(f32[52,8,128]{2,1,0:T(8,128)S(1)} %get-tuple-element.23), channel_id=1, source_target_pairs={{0,112},{1,113},{2,114},{3,115},{4,116},{5,117},{6,118},{7,119},{8... | collective-permute-start | bytes 638984 | tf_op jit(solution)/shard_map/ppermute | solution.py:356
  76.9 6.5 %collective-permute-start.12 = (f32[52,8,128]{2,1,0:T(8,128)S(1)}, f32[52,8,128]{2,1,0:T(8,128)S(1)}, u32[]{:S(2)}, u32[]{:S(2)}) collective-permute-start(f32[52,8,128]{2,1,0:T(8,128)S(1)} %get-tuple-element.24), channel_id=1, source_target_pairs={{0,16},{1,17},{2,18},{3,19},{4,20},{5,21},{6,22},{7,23},{8,24},{9,... | collective-permute-start | bytes 638984 | tf_op jit(solution)/shard_map/ppermute | solution.py:356

commit v4 on v3

--- a/solution.py
+++ b/solution.py
@@ -52,7 +52,14 @@
     return (c_ref, field) if field < 3 else (v_ref, field - 3)
 
 
-def pack_x(place_ref, c_ref, v_ref, ac_ref, av_ref, b_ref, edge_ref):
+def pack_x(place_ref, c_in, v_in, c_ref, v_ref, ac_ref, av_ref, b_ref, edge_ref, sems):
+    fetches = [
+        pltpu.make_async_copy(c_in, c_ref, sems.at[0]), pltpu.make_async_copy(v_in, v_ref, sems.at[1])
+    ]
+    for fetch in fetches:
+        fetch.start()
+    for fetch in fetches:
+        fetch.wait()
     high = 4 * place_ref[0]
     low = 4 - high
     shift = 4 * place_ref[1]
@@ -304,16 +311,18 @@
     loop(0, 8, finish, 2)
 
 
-def call(kernel, outs, scratch=(), operands=0):
+def call(kernel, outs, scratch=(), operands=0, sems=0):
     smem = pl.BlockSpec(memory_space=pltpu.SMEM)
     vmem = pl.BlockSpec(memory_space=pltpu.VMEM)
+    space = pl.BlockSpec(memory_space=pltpu.HBM) if sems else vmem
     shapes = [jax.ShapeDtypeStruct(o, jnp.float32) for o in outs]
     return pl.pallas_call(
         kernel,
         out_shape=shapes,
-        in_specs=[smem] + [vmem] * operands,
+        in_specs=[smem] + [space] * operands,
         out_specs=[vmem] * len(outs),
-        scratch_shapes=[pltpu.VMEM(s, jnp.float32) for s in scratch],
+        scratch_shapes=[pltpu.VMEM(s, jnp.float32) for s in scratch]
+        + ([pltpu.SemaphoreType.DMA((sems,))] if sems else []),
         compiler_params=pltpu.CompilerParams(vmem_limit_bytes=16 * 1024 * 1024),
     )
 
@@ -363,7 +372,10 @@
         layers = (6, 4, 16, 128)
         half = (3, 4, 16, 128)
         edge = (4, 16, 128)
-        ac, av, b, own = call(pack_x, [half, half, layers, edge], (), 2)(place, c, v)
+        own_block = (3, 8, 16, 128)
+        c, v, ac, av, b, own = call(
+            pack_x, [own_block, own_block, half, half, layers, edge], (), 2, 2
+        )(place, c, v)
         passed = send(av, aside)
         ac = send(ac, across)
         passed = send(passed, relay)
@@ -372,7 +384,8 @@
         wrap = send(own, ends)
         b = send(b, other)
         wrap_b = send(wrap, ends_other)
-        wrap_a = send(jnp.where(far, own, wrap), ends_across)
+        picked = jnp.where(far, own, wrap)
+        wrap_a = send(picked, ends_across)
         left, right = call(pack_z, [edge, edge], (), 5)(place, c, v, ac, av, b)
         zl = send(right, z_up)
         zr = send(left, z_down)

time: 93.2 us -> 93.7 us (level)
  no operation moved by 1% of the time
where the time goes in v4:
time: 93.7 us; the launch traced here: 93.3 us
  starting transfers between devices  65 us (69%)
  waiting for transfers between devices  13.2 us (14%)
  Pallas kernels  13 us (14%)
  local copies, waits for them, and re-layouts  1.85 us (2%)
    ppermute x13, starting transfers between devices, send(): return lax.ppermute(value, AXES, pairs)  65 us
    ppermute x13, waiting for transfers between devices, send(): return lax.ppermute(value, AXES, pairs)  13.2 us
    pallas_call x1, Pallas kernels, local(): call(compute, [(3, 8, 16, 128)], scratch, 9)  9.38 us
  transfers between devices with their start and end apart: 13, of which 5 were waited for; matrix products, arithmetic and copies ran while one was open for 0% of the time, Pallas kernels for 1%

profile of v4, /device:TPU:6, one launch (start us, length us, event | category | flops | bytes accessed | tf_op | source)
XLA Modules:
  0.0 93.3 jit_solution(11889138239254744374)
XLA Ops:
  0.0 0.1 pad_add_fusion.place_ref
  0.1 0.0 copy-start
  0.1 0.9 copy-done
  1.0 0.0 copy-start.1
  1.0 0.9 copy-done.1
  1.9 1.5 %shard_map.28 = (f32[3,8,16,128]{3,2,1,0:T(8,128)S(1)}, f32[3,8,16,128]{3,2,1,0:T(8,128)S(1)}, f32[3,4,16,128]{3,2,1,0:T(8,128)S(1)}, f32[3,4,16,128]{3,2,1,0:T(...) custom-call(s32[4]{0:T(128)S(1)} %pad_add_fusion.place_ref, f32[3,8,16,128]{3,2,1,0:T(8,128)S(1)} %copy-done, ...), custom_call_target="tpu_custom_call" | custom-call | tf_op jit(solution)/shard_map/pallas_call | solution.py:376
  3.4 2.7 %collective-permute-start.1 = (f32[3,4,16,128]{3,2,1,0:T(8,128)S(1)}, f32[3,4,16,128]{3,2,1,0:T(8,128)S(1)}, u32[]{:S(2)}, u32[]{:S(2)}) collective-permute-start(f32[3,4,16,128]{3,2,1,0:T(8,128)S(1)} %get-tuple-element.20), channel_id=1, source_target_pairs={{0,128},{1,129},{2,130},{3,131},{4,132},{5,133},{6,134},{7,135},{8... | collective-permute-start | bytes 294920 | tf_op jit(solution)/shard_map/ppermute | solution.py:365
  6.2 2.2 %collective-permute-done.1 = f32[3,4,16,128]{3,2,1,0:T(8,128)S(1)} collective-permute-done((f32[3,4,16,128]{3,2,1,0:T(8,128)S(1)}, f32[3,4,16,128]{3,2,1,0:T(8,128)S(1)}, u32[]{:S(2)}, u32[]{:S(2)}) %collective-permute-start.1) | collective-permute-done | bytes 98336 | tf_op jit(solution)/shard_map/ppermute | solution.py:365
  8.4 0.7 collective-permute-start.2
  9.0 26.4 %collective-permute-start.8 = (f32[4,16,128]{2,1,0:T(8,128)S(1)}, f32[4,16,128]{2,1,0:T(8,128)S(1)}, u32[]{:S(2)}, u32[]{:S(2)}) collective-permute-start(f32[4,16,128]{2,1,0:T(8,128)S(1)} %get-tuple-element.24), channel_id=1, source_target_pairs={{0,15},{15,0},{16,31},{31,16},{32,47},{47,32},{48,63},{63,48},{64,... | collective-permute-start | bytes 98312 | tf_op jit(solution)/shard_map/ppermute | solution.py:365
  35.4 0.7 collective-permute-start.4
  36.1 12.4 %collective-permute-start = (f32[3,4,16,128]{3,2,1,0:T(8,128)S(1)}, f32[3,4,16,128]{3,2,1,0:T(8,128)S(1)}, u32[]{:S(2)}, u32[]{:S(2)}) collective-permute-start(f32[3,4,16,128]{3,2,1,0:T(8,128)S(1)} %get-tuple-element.19), channel_id=1, source_target_pairs={{0,896},{1,897},{2,898},{3,899},{4,900},{5,901},{6,902},{7,903},{8... | collective-permute-start | bytes 294920 | tf_op jit(solution)/shard_map/ppermute | solution.py:365
  48.5 8.2 %collective-permute-start.5 = (f32[6,4,16,128]{3,2,1,0:T(8,128)S(1)}, f32[6,4,16,128]{3,2,1,0:T(8,128)S(1)}, u32[]{:S(2)}, u32[]{:S(2)}) collective-permute-start(f32[6,4,16,128]{3,2,1,0:T(8,128)S(1)} %get-tuple-element.21), channel_id=1, source_target_pairs={{0,128},{1,129},{2,130},{3,131},{4,132},{5,133},{6,134},{7,135},{8... | collective-permute-start | bytes 589832 | tf_op jit(solution)/shard_map/ppermute | solution.py:365
  56.8 0.0 collective-permute-done.2
  56.8 1.3 %collective-permute-start.3 = (f32[3,4,16,128]{3,2,1,0:T(8,128)S(1)}, f32[3,4,16,128]{3,2,1,0:T(8,128)S(1)}, u32[]{:S(2)}, u32[]{:S(2)}) collective-permute-start(f32[3,4,16,128]{3,2,1,0:T(8,128)S(1)} %collective-permute-done.2), channel_id=1, source_target_pairs={{128,0},{129,1},{130,2},{131,3},{132,4},{133,5},{134,6},{135,7},{1... | collective-permute-start | bytes 294920 | tf_op jit(solution)/shard_map/ppermute | solution.py:365
  58.1 0.0 collective-permute-done.8.wrap_ref
  58.1 1.9 %collective-permute-start.9 = (f32[4,16,128]{2,1,0:T(8,128)S(1)}, f32[4,16,128]{2,1,0:T(8,128)S(1)}, u32[]{:S(2)}, u32[]{:S(2)}) collective-permute-start(f32[4,16,128]{2,1,0:T(8,128)S(1)} %broadcast_select_fusion.1), channel_id=1, source_target_pairs={{0,911},{15,896},{16,927},{31,912},{32,943},{47,928},{48,959},{63,... | collective-permute-start | bytes 98312 | tf_op jit(solution)/shard_map/ppermute | solution.py:365
  60.1 0.0 collective-permute-done.4
  60.1 7.1 %collective-permute-start.10 = (f32[4,16,128]{2,1,0:T(8,128)S(1)}, f32[4,16,128]{2,1,0:T(8,128)S(1)}, u32[]{:S(2)}, u32[]{:S(2)}) collective-permute-start(f32[4,16,128]{2,1,0:T(8,128)S(1)} %collective-permute-done.8.wrap_ref), channel_id=1, source_target_pairs={{0,128},{15,143},{16,144},{31,159},{32,160},{47,175},{48,176},{63,... | collective-permute-start | bytes 98312 | tf_op jit(solution)/shard_map/ppermute | solution.py:365
  67.1 0.0 collective-permute-done.3
  67.2 0.0 collective-permute-done.ac_ref
  67.2 0.0 collective-permute-done.5.b_ref
  67.2 1.2 %shard_map.29 = (f32[4,16,128]{2,1,0:T(8,128)S(1)}, f32[4,16,128]{2,1,0:T(8,128)S(1)}) custom-call(s32[4]{0:T(128)S(1)} %pad_add_fusion.place_ref, f32[3,8,16,128]{3,2,1,0:T(8,128)S(1)} %get-tuple-element.17.c_ref, f32[3,8,16,128]{3,2,1,0:T(8,128)S(1)} %get-tuple-element.18.v_ref, f32[3,4,16,128]{3,2,1,0:T(8,128)S(1)} %collective-permute-done.ac_ref, ...), custom_call_target="tpu_custom_call" | custom-call | tf_op jit(solution)/shard_map/pallas_call | solution.py:389
  68.4 1.3 %collective-permute-start.6 = (f32[4,16,128]{2,1,0:T(8,128)S(1)}, f32[4,16,128]{2,1,0:T(8,128)S(1)}, u32[]{:S(2)}, u32[]{:S(2)}) collective-permute-start(f32[4,16,128]{2,1,0:T(8,128)S(1)} %get-tuple-element.22), channel_id=1, source_target_pairs={{0,1},{1,2},{2,3},{3,4},{4,5},{5,6},{6,7},{7,8},{8,9},{9,10},{10,1... | collective-permute-start | bytes 98312 | tf_op jit(solution)/shard_map/ppermute | solution.py:365
  69.7 1.3 %collective-permute-start.7 = (f32[4,16,128]{2,1,0:T(8,128)S(1)}, f32[4,16,128]{2,1,0:T(8,128)S(1)}, u32[]{:S(2)}, u32[]{:S(2)}) collective-permute-start(f32[4,16,128]{2,1,0:T(8,128)S(1)} %get-tuple-element.23), channel_id=1, source_target_pairs={{1,0},{2,1},{3,2},{4,3},{5,4},{6,5},{7,6},{8,7},{9,8},{10,9},{11,1... | collective-permute-start | bytes 98312 | tf_op jit(solution)/shard_map/ppermute | solution.py:365
  71.0 0.0 collective-permute-done.9.wrap_a_ref
  71.0 0.0 collective-permute-done.10.wrap_b_ref
  71.1 0.3 collective-permute-done.6.zl_ref
  71.3 4.2 %collective-permute-done.7.zr_ref = f32[4,16,128]{2,1,0:T(8,128)S(1)} collective-permute-done((f32[4,16,128]{2,1,0:T(8,128)S(1)}, f32[4,16,128]{2,1,0:T(8,128)S(1)}, u32[]{:S(2)}, u32[]{:S(2)}) %collective-permute-start.7) | collective-permute-done | bytes 32800 | tf_op jit(solution)/shard_map/ppermute | solution.py:365
  75.5 0.9 shard_map.30
  76.4 1.0 %collective-permute-start.11 = (f32[52,8,128]{2,1,0:T(8,128)S(1)}, f32[52,8,128]{2,1,0:T(8,128)S(1)}, u32[]{:S(2)}, u32[]{:S(2)}) collective-permute-start(f32[52,8,128]{2,1,0:T(8,128)S(1)} %get-tuple-element.27), channel_id=1, source_target_pairs={{0,112},{1,113},{2,114},{3,115},{4,116},{5,117},{6,118},{7,119},{8... | collective-permute-start | bytes 638984 | tf_op jit(solution)/shard_map/ppermute | solution.py:365
  77.4 0.0 collective-permute-start.12
  77.4 3.4 %collective-permute-done.11.above_ref = f32[52,8,128]{2,1,0:T(8,128)S(1)} collective-permute-done((f32[52,8,128]{2,1,0:T(8,128)S(1)}, f32[52,8,128]{2,1,0:T(8,128)S(1)}, u32[]{:S(2)}, u32[]{:S(2)}) %collective-permute-start.11) | collective-permute-done | bytes 213024 | tf_op jit(solution)/shard_map/ppermute | solution.py:365
  80.8 3.1 %collective-permute-done.12.below_ref = f32[52,8,128]{2,1,0:T(8,128)S(1)} collective-permute-done((f32[52,8,128]{2,1,0:T(8,128)S(1)}, f32[52,8,128]{2,1,0:T(8,128)S(1)}, u32[]{:S(2)}, u32[]{:S(2)}) %collective-permute-start.12) | collective-permute-done | bytes 213024 | tf_op jit(solution)/shard_map/ppermute | solution.py:365
  83.9 9.4 %shard_map.31 = f32[3,8,16,128]{3,2,1,0:T(8,128)} custom-call(s32[4]{0:T(128)S(1)} %pad_add_fusion.place_ref, f32[3,8,16,128]{3,2,1,0:T(8,128)S(1)} %get-tuple-element.17.c_ref, f32[3,8,16,128]{3,2,1,0:T(8,128)S(1)} %get-tuple-element.18.v_ref, f32[3,4,16,128]{3,2,1,0:T(8,128)S(1)} %collective-permute-done.ac_ref, ...), custom_call_target="tpu_custom_call" | custom-call | tf_op jit(solution)/shard_map/pallas_call | solution.py:401
  (2 shorter events, 0.0 us)
Async XLA Ops:
  0.1 0.9 copy-start
  1.0 0.9 copy-start.1
  3.4 4.9 %collective-permute-start.1 = (f32[3,4,16,128]{3,2,1,0:T(8,128)S(1)}, f32[3,4,16,128]{3,2,1,0:T(8,128)S(1)}, u32[]{:S(2)}, u32[]{:S(2)}) collective-permute-start(f32[3,4,16,128]{3,2,1,0:T(8,128)S(1)} %get-tuple-element.20), channel_id=1, source_target_pairs={{0,128},{1,129},{2,130},{3,131},{4,132},{5,133},{6,134},{7,135},{8... | collective-permute-start | bytes 294920 | tf_op jit(solution)/shard_map/ppermute | solution.py:365
  8.4 48.4 %collective-permute-start.2 = (f32[3,4,16,128]{3,2,1,0:T(8,128)S(1)}, f32[3,4,16,128]{3,2,1,0:T(8,128)S(1)}, u32[]{:S(2)}, u32[]{:S(2)}) collective-permute-start(f32[3,4,16,128]{3,2,1,0:T(8,128)S(1)} %collective-permute-done.1), channel_id=1, source_target_pairs={{128,768},{129,769},{130,770},{131,771},{132,772},{133,773},{134,7... | collective-permute-start | bytes 294920 | tf_op jit(solution)/shard_map/ppermute | solution.py:365
  9.0 49.1 %collective-permute-start.8 = (f32[4,16,128]{2,1,0:T(8,128)S(1)}, f32[4,16,128]{2,1,0:T(8,128)S(1)}, u32[]{:S(2)}, u32[]{:S(2)}) collective-permute-start(f32[4,16,128]{2,1,0:T(8,128)S(1)} %get-tuple-element.24), channel_id=1, source_target_pairs={{0,15},{15,0},{16,31},{31,16},{32,47},{47,32},{48,63},{63,48},{64,... | collective-permute-start | bytes 98312 | tf_op jit(solution)/shard_map/ppermute | solution.py:365
  35.4 24.6 %collective-permute-start.4 = (f32[3,4,16,128]{3,2,1,0:T(8,128)S(1)}, f32[3,4,16,128]{3,2,1,0:T(8,128)S(1)}, u32[]{:S(2)}, u32[]{:S(2)}) collective-permute-start(f32[3,4,16,128]{3,2,1,0:T(8,128)S(1)} %get-tuple-element.20), channel_id=1, source_target_pairs={{128,256},{129,257},{130,258},{131,259},{132,260},{133,261},{134,2... | collective-permute-start | bytes 294920 | tf_op jit(solution)/shard_map/ppermute | solution.py:365
  36.1 31.1 %collective-permute-start = (f32[3,4,16,128]{3,2,1,0:T(8,128)S(1)}, f32[3,4,16,128]{3,2,1,0:T(8,128)S(1)}, u32[]{:S(2)}, u32[]{:S(2)}) collective-permute-start(f32[3,4,16,128]{3,2,1,0:T(8,128)S(1)} %get-tuple-element.19), channel_id=1, source_target_pairs={{0,896},{1,897},{2,898},{3,899},{4,900},{5,901},{6,902},{7,903},{8... | collective-permute-start | bytes 294920 | tf_op jit(solution)/shard_map/ppermute | solution.py:365
  48.5 18.6 %collective-permute-start.5 = (f32[6,4,16,128]{3,2,1,0:T(8,128)S(1)}, f32[6,4,16,128]{3,2,1,0:T(8,128)S(1)}, u32[]{:S(2)}, u32[]{:S(2)}) collective-permute-start(f32[6,4,16,128]{3,2,1,0:T(8,128)S(1)} %get-tuple-element.21), channel_id=1, source_target_pairs={{0,128},{1,129},{2,130},{3,131},{4,132},{5,133},{6,134},{7,135},{8... | collective-permute-start | bytes 589832 | tf_op jit(solution)/shard_map/ppermute | solution.py:365
  56.8 10.4 %collective-permute-start.3 = (f32[3,4,16,128]{3,2,1,0:T(8,128)S(1)}, f32[3,4,16,128]{3,2,1,0:T(8,128)S(1)}, u32[]{:S(2)}, u32[]{:S(2)}) collective-permute-start(f32[3,4,16,128]{3,2,1,0:T(8,128)S(1)} %collective-permute-done.2), channel_id=1, source_target_pairs={{128,0},{129,1},{130,2},{131,3},{132,4},{133,5},{134,6},{135,7},{1... | collective-permute-start | bytes 294920 | tf_op jit(solution)/shard_map/ppermute | solution.py:365
  58.1 12.9 %collective-permute-start.9 = (f32[4,16,128]{2,1,0:T(8,128)S(1)}, f32[4,16,128]{2,1,0:T(8,128)S(1)}, u32[]{:S(2)}, u32[]{:S(2)}) collective-permute-start(f32[4,16,128]{2,1,0:T(8,128)S(1)} %broadcast_select_fusion.1), channel_id=1, source_target_pairs={{0,911},{15,896},{16,927},{31,912},{32,943},{47,928},{48,959},{63,... | collective-permute-start | bytes 98312 | tf_op jit(solution)/shard_map/ppermute | solution.py:365
  60.1 11.0 %collective-permute-start.10 = (f32[4,16,128]{2,1,0:T(8,128)S(1)}, f32[4,16,128]{2,1,0:T(8,128)S(1)}, u32[]{:S(2)}, u32[]{:S(2)}) collective-permute-start(f32[4,16,128]{2,1,0:T(8,128)S(1)} %collective-permute-done.8.wrap_ref), channel_id=1, source_target_pairs={{0,128},{15,143},{16,144},{31,159},{32,160},{47,175},{48,176},{63,... | collective-permute-start | bytes 98312 | tf_op jit(solution)/shard_map/ppermute | solution.py:365
  68.4 2.9 %collective-permute-start.6 = (f32[4,16,128]{2,1,0:T(8,128)S(1)}, f32[4,16,128]{2,1,0:T(8,128)S(1)}, u32[]{:S(2)}, u32[]{:S(2)}) collective-permute-start(f32[4,16,128]{2,1,0:T(8,128)S(1)} %get-tuple-element.22), channel_id=1, source_target_pairs={{0,1},{1,2},{2,3},{3,4},{4,5},{5,6},{6,7},{7,8},{8,9},{9,10},{10,1... | collective-permute-start | bytes 98312 | tf_op jit(solution)/shard_map/ppermute | solution.py:365
  69.7 5.8 %collective-permute-start.7 = (f32[4,16,128]{2,1,0:T(8,128)S(1)}, f32[4,16,128]{2,1,0:T(8,128)S(1)}, u32[]{:S(2)}, u32[]{:S(2)}) collective-permute-start(f32[4,16,128]{2,1,0:T(8,128)S(1)} %get-tuple-element.23), channel_id=1, source_target_pairs={{1,0},{2,1},{3,2},{4,3},{5,4},{6,5},{7,6},{8,7},{9,8},{10,9},{11,1... | collective-permute-start | bytes 98312 | tf_op jit(solution)/shard_map/ppermute | solution.py:365
  76.4 4.4 %collective-permute-start.11 = (f32[52,8,128]{2,1,0:T(8,128)S(1)}, f32[52,8,128]{2,1,0:T(8,128)S(1)}, u32[]{:S(2)}, u32[]{:S(2)}) collective-permute-start(f32[52,8,128]{2,1,0:T(8,128)S(1)} %get-tuple-element.27), channel_id=1, source_target_pairs={{0,112},{1,113},{2,114},{3,115},{4,116},{5,117},{6,118},{7,119},{8... | collective-permute-start | bytes 638984 | tf_op jit(solution)/shard_map/ppermute | solution.py:365
  77.4 6.5 %collective-permute-start.12 = (f32[52,8,128]{2,1,0:T(8,128)S(1)}, f32[52,8,128]{2,1,0:T(8,128)S(1)}, u32[]{:S(2)}, u32[]{:S(2)}) collective-permute-start(f32[52,8,128]{2,1,0:T(8,128)S(1)} %get-tuple-element.28), channel_id=1, source_target_pairs={{0,16},{1,17},{2,18},{3,19},{4,20},{5,21},{6,22},{7,23},{8,24},{9,... | collective-permute-start | bytes 638984 | tf_op jit(solution)/shard_map/ppermute | solution.py:365

commit v5 on v3

--- a/solution.py
+++ b/solution.py
@@ -61,7 +61,7 @@
         for field in range(6):
             ref, i = field_of(c_ref, v_ref, field)
             to, j = field_of(ac_ref, av_ref, field)
-            to[j, q] = ref[i, high + q]
+            to[4 * j + q] = ref[i, high + q]
             b_ref[field, q] = ref[i, low + q]
         lane = lanes_of((16, 128))
         edge = jnp.zeros((16, 128), jnp.float32)
@@ -74,16 +74,22 @@
         edge_ref[q] = edge
 
     loop(0, 4, copy)
+    for q in range(2):
+        ac_ref[12 + q] = edge_ref[q] + roll(edge_ref[q + 2], 64, 1)
 
 
 def lower_upper(odd, ac_ref, av_ref, b_ref, field, q):
     ref, i = field_of(ac_ref, av_ref, field)
-    a, b = ref[i, q], b_ref[field, q]
+    a, b = ref[4 * i + q], b_ref[field, q]
     return jnp.where(odd, b, a), jnp.where(odd, a, b)
 
 
-def pack_z(place_ref, c_ref, v_ref, ac_ref, av_ref, b_ref, left_ref, right_ref):
+def pack_z(
+    place_ref, c_ref, v_ref, ac_ref, av_ref, b_ref, end_ref, end_a_ref, end_b_ref, left_ref, right_ref
+):
     odd = place_ref[0] == 1
+    first_end = place_ref[2] == 1
+    last_end = place_ref[3] == 1
 
     def pack(q):
         lane = lanes_of((16, 128))
@@ -97,19 +103,23 @@
                 here = between(lane, at, at + 4)
                 left = jnp.where(here, roll(x, at, 1), left)
                 right = jnp.where(here, roll(x, at + 4, 1), right)
-        left_ref[q] = left
-        right_ref[q] = right
+        turn = 64 * lax.shift_right_logical(q, 1)
+        base, a, b = (
+            pltpu.roll(ref[lax.bitwise_and(q, 1)], turn, 1) for ref in (end_ref, end_a_ref, end_b_ref)
+        )
+        a, b = roll(a, 64, 1), roll(b, 64, 1)
+        lo, hi = jnp.where(odd, a, b), jnp.where(odd, b, a)
+        end = jnp.where(lane < 32, lo, jnp.where(lane < 96, base, hi))
+        left_ref[q] = jnp.where(first_end, end, left)
+        right_ref[q] = jnp.where(last_end, end, right)
 
     loop(0, 4, pack)
 
 
 def pack_y(
-    place_ref, c_ref, v_ref, ac_ref, av_ref, b_ref, zl_ref, zr_ref, wrap_ref, wrap_a_ref, wrap_b_ref,
-    down_ref, up_ref, zl_out_ref, zr_out_ref,
+    place_ref, c_ref, v_ref, ac_ref, av_ref, b_ref, zl_ref, zr_ref, down_ref, up_ref
 ):
     odd = place_ref[0] == 1
-    first_end = place_ref[2] == 1
-    last_end = place_ref[3] == 1
     upper = rows_of((8, 128)) < 4
 
     def join(entry, first, second):
@@ -123,15 +133,7 @@
             near, far = ref[i, q], ref[i, 4 + q]
             join(8 * field + q, lo, far)
             join(8 * field + 4 + q, near, hi)
-        lane = lanes_of((16, 128))
-        wrap_a, wrap_b = roll(wrap_a_ref[q], 64, 1), roll(wrap_b_ref[q], 64, 1)
-        lo, hi = jnp.where(odd, wrap_b, wrap_a), jnp.where(odd, wrap_a, wrap_b)
-        wrap = jnp.where(lane < 32, lo, jnp.where(lane < 96, wrap_ref[q], hi))
-        zl = jnp.where(first_end, wrap, zl_ref[q])
-        zr = jnp.where(last_end, wrap, zr_ref[q])
-        zl_out_ref[q] = zl
-        zr_out_ref[q] = zr
-        join(48 + q, zl, zr)
+        join(48 + q, zl_ref[q], zr_ref[q])
 
     loop(0, 4, pack)
 
@@ -337,20 +339,12 @@
     relay = flat_pairs(
         mesh, lambda x, y, z: None if is_far(x) else (other_of(across_of(other_of(x))), y, z)
     )
-    forward = flat_pairs(mesh, lambda x, y, z: None if is_far(x) else (other_of(x), y, z))
     beside = flat_pairs(mesh, lambda x, y, z: None if is_far(x) else (across_of(x), y, z))
     y_up = flat_pairs(mesh, lambda x, y, z: (x, y + 1, z))
     y_down = flat_pairs(mesh, lambda x, y, z: (x, y - 1, z))
-    z_up = flat_pairs(mesh, lambda x, y, z: (x, y, z + 1) if z < end else None)
-    z_down = flat_pairs(mesh, lambda x, y, z: (x, y, z - 1) if z > 0 else None)
-    ends = flat_pairs(mesh, lambda x, y, z: (x, y, end - z) if z in (0, end) else None)
-    ends_other = flat_pairs(
-        mesh, lambda x, y, z: (other_of(x), y, z) if z in (0, end) else None
-    )
-    ends_across = flat_pairs(
-        mesh,
-        lambda x, y, z: (across_of(x), y, end - z if is_far(x) else z) if z in (0, end) else None,
-    )
+    last_x = mesh.shape["gx"] - 1
+    z_up = flat_pairs(mesh, lambda x, y, z: (x if z < end else last_x - x, y, z + 1))
+    z_down = flat_pairs(mesh, lambda x, y, z: (x if z > 0 else last_x - x, y, z - 1))
 
     def send(value, pairs):
         return lax.ppermute(value, AXES, pairs)
@@ -361,24 +355,24 @@
         place = place.astype(jnp.int32)
         far = (x % 4 == 0) | (x % 4 == 3)
         layers = (6, 4, 16, 128)
-        half = (3, 4, 16, 128)
         edge = (4, 16, 128)
-        ac, av, b, own = call(pack_x, [half, half, layers, edge], (), 2)(place, c, v)
+        ac, av, b, _ = call(pack_x, [(14, 16, 128), (12, 16, 128), layers, edge], (), 2)(place, c, v)
+        own_end = ac[12:]
         passed = send(av, aside)
         ac = send(ac, across)
-        passed = send(passed, relay)
+        passed = send(jnp.concatenate([passed, own_end]), relay)
         near_av = send(av, beside)
-        av = jnp.where(far, send(passed, forward), near_av)
-        wrap = send(own, ends)
         b = send(b, other)
-        wrap_b = send(wrap, ends_other)
-        wrap_a = send(jnp.where(far, own, wrap), ends_across)
-        left, right = call(pack_z, [edge, edge], (), 5)(place, c, v, ac, av, b)
+        held = jnp.where(far, ac, passed)
+        forwarded = send(held, other)
+        end_a = jnp.where(far, own_end, send(passed[12:], beside))
+        av = jnp.where(far, forwarded[:12], near_av)
+        left, right = call(pack_z, [edge, edge], (), 8)(
+            place, c, v, ac, av, b, held[12:], end_a, forwarded[12:]
+        )
         zl = send(right, z_up)
         zr = send(left, z_down)
-        down, up, zl, zr = call(pack_y, [(52, 8, 128)] * 2 + [edge] * 2, (), 10)(
-            place, c, v, ac, av, b, zl, zr, wrap, wrap_a, wrap_b
-        )
+        down, up = call(pack_y, [(52, 8, 128)] * 2, (), 7)(place, c, v, ac, av, b, zl, zr)
         above = send(down, y_down)
         below = send(up, y_up)
         block = (16, 24, 128)

time: 93.2 us -> 96.6 us (1.036)
  starting transfers between devices: 65 us -> 67.3 us
    ppermute x13 -> x11, starting transfers between devices: 65 us -> 67.3 us  [send(): return lax.ppermute(value, AXES, pairs)]
    ppermute x13 -> x11, waiting for transfers between devices: 13.2 us -> 13 us  [send(): return lax.ppermute(value, AXES, pairs)]
  transfers between devices with their start and end apart: 13 -> 11, of which waited for: 5 -> 5; matrix products, arithmetic and copies ran while one was open for 0% -> 0% of each run, Pallas kernels for 1% -> 0%
where the time goes in v5:
time: 96.6 us; the launch traced here: 95.4 us
  starting transfers between devices  67.3 us (70%)
  waiting for transfers between devices  13 us (13%)
  Pallas kernels  12.9 us (13%)
  local copies, waits for them, and re-layouts  1.88 us (2%)
    ppermute x11, starting transfers between devices, send(): return lax.ppermute(value, AXES, pairs)  67.3 us
    ppermute x11, waiting for transfers between devices, send(): return lax.ppermute(value, AXES, pairs)  13 us
    pallas_call x1, Pallas kernels, local(): call(compute, [(3, 8, 16, 128)], scratch, 9)  9.38 us
  transfers between devices with their start and end apart: 11, of which 5 were waited for; matrix products, arithmetic and copies ran while one was open for 0% of the time, Pallas kernels for 0%

profile of v5, /device:TPU:6, one launch (start us, length us, event | category | flops | bytes accessed | tf_op | source)
XLA Modules:
  0.0 95.4 jit_solution(16979836643569028666)
XLA Ops:
  0.0 0.1 pad_add_fusion.place_ref
  0.1 0.0 copy-start
  0.1 0.9 copy-done
  1.0 0.0 copy-start.2
  1.0 0.9 copy-done.2
  1.9 1.6 %shard_map.28 = (f32[14,16,128]{2,1,0:T(8,128)S(1)}, f32[12,16,128]{2,1,0:T(8,128)S(1)}, f32[6,4,16,128]{3,2,1,0:T(8,128)S(1)}, f32[4,16,128]{2,1,0:T(8,128)}) custom-call(s32[4]{0:T(128)S(1)} %pad_add_fusion.place_ref, f32[3,8,16,128]{3,2,1,0:T(8,128)S(1)} %copy-done, f32[3,8,16,128]{3,2,1,0:T(8,128)S(1)} %copy-done.2), custom_call_target="tpu_custom_call" | custom-call | tf_op jit(solution)/shard_map/pallas_call | solution.py:359
  3.5 2.7 %collective-permute-start.1 = (f32[12,16,128]{2,1,0:T(8,128)S(1)}, f32[12,16,128]{2,1,0:T(8,128)S(1)}, u32[]{:S(2)}, u32[]{:S(2)}) collective-permute-start(f32[12,16,128]{2,1,0:T(8,128)S(1)} %get-tuple-element.13), channel_id=1, source_target_pairs={{0,128},{1,129},{2,130},{3,131},{4,132},{5,133},{6,134},{7,135},{8... | collective-permute-start | bytes 294920 | tf_op jit(solution)/shard_map/ppermute | solution.py:350
  6.2 2.2 %collective-permute-done.1 = f32[12,16,128]{2,1,0:T(8,128)S(1)} collective-permute-done((f32[12,16,128]{2,1,0:T(8,128)S(1)}, f32[12,16,128]{2,1,0:T(8,128)S(1)}, u32[]{:S(2)}, u32[]{:S(2)}) %collective-permute-start.1) | collective-permute-done | bytes 98336 | tf_op jit(solution)/shard_map/ppermute | solution.py:350
  8.4 0.7 collective-permute-start.2
  9.1 29.6 %collective-permute-start = (f32[14,16,128]{2,1,0:T(8,128)S(1)}, f32[14,16,128]{2,1,0:T(8,128)S(1)}, u32[]{:S(2)}, u32[]{:S(2)}) collective-permute-start(f32[14,16,128]{2,1,0:T(8,128)S(1)} %get-tuple-element.12), channel_id=1, source_target_pairs={{0,896},{1,897},{2,898},{3,899},{4,900},{5,901},{6,902},{7,903},{8... | collective-permute-start | bytes 344072 | tf_op jit(solution)/shard_map/ppermute | solution.py:350
  38.7 0.7 collective-permute-start.4
  39.3 8.2 %collective-permute-start.5 = (f32[6,4,16,128]{3,2,1,0:T(8,128)S(1)}, f32[6,4,16,128]{3,2,1,0:T(8,128)S(1)}, u32[]{:S(2)}, u32[]{:S(2)}) collective-permute-start(f32[6,4,16,128]{3,2,1,0:T(8,128)S(1)} %get-tuple-element.14), channel_id=1, source_target_pairs={{0,128},{1,129},{2,130},{3,131},{4,132},{5,133},{6,134},{7,135},{8... | collective-permute-start | bytes 589832 | tf_op jit(solution)/shard_map/ppermute | solution.py:350
  47.6 0.0 collective-permute-done.2
  47.6 0.7 collective-permute-start.6
  48.3 0.0 collective-permute-done.ac_ref
  48.3 0.0 copy-start.3
  48.3 0.0 copy-start.1
  48.3 11.6 %collective-permute-start.3 = (f32[14,16,128]{2,1,0:T(8,128)S(1)}, f32[14,16,128]{2,1,0:T(8,128)S(1)}, u32[]{:S(2)}, u32[]{:S(2)}) collective-permute-start(f32[14,16,128]{2,1,0:T(8,128)S(1)} %broadcast_select_fusion), channel_id=1, source_target_pairs={{0,128},{1,129},{2,130},{3,131},{4,132},{5,133},{6,134},{7,135},{8... | collective-permute-start | bytes 344072 | tf_op jit(solution)/shard_map/ppermute | solution.py:350
  60.0 0.0 collective-permute-done.6
  60.0 2.7 %collective-permute-done.3 = f32[14,16,128]{2,1,0:T(8,128)S(1)} collective-permute-done((f32[14,16,128]{2,1,0:T(8,128)S(1)}, f32[14,16,128]{2,1,0:T(8,128)S(1)}, u32[]{:S(2)}, u32[]{:S(2)}) %collective-permute-start.3) | collective-permute-done | bytes 114720 | tf_op jit(solution)/shard_map/ppermute | solution.py:350
  62.7 0.0 collective-permute-done.4
  62.7 0.0 collective-permute-done.5.b_ref
  62.8 0.0 copy-done.3
  62.8 0.0 copy-done.1
  62.8 1.3 %shard_map.29 = (f32[4,16,128]{2,1,0:T(8,128)S(1)}, f32[4,16,128]{2,1,0:T(8,128)S(1)}) custom-call(s32[4]{0:T(128)S(1)} %pad_add_fusion.place_ref, f32[3,8,16,128]{3,2,1,0:T(8,128)S(1)} %copy-done.1, f32[3,8,16,128]{3,2,1,0:T(8,128)S(1)} %copy-done.3, f32[14,16,128]{2,1,0:T(8,128)S(1)} %collective-permute-done.ac_ref, ...), custom_call_target="tpu_custom_call" | custom-call | tf_op jit(solution)/shard_map/pallas_call | solution.py:370
  64.1 4.3 %collective-permute-start.7 = (f32[4,16,128]{2,1,0:T(8,128)S(1)}, f32[4,16,128]{2,1,0:T(8,128)S(1)}, u32[]{:S(2)}, u32[]{:S(2)}) collective-permute-start(f32[4,16,128]{2,1,0:T(8,128)S(1)} %get-tuple-element.15), channel_id=1, source_target_pairs={{0,1},{1,2},{2,3},{3,4},{4,5},{5,6},{6,7},{7,8},{8,9},{9,10},{10,1... | collective-permute-start | bytes 98312 | tf_op jit(solution)/shard_map/ppermute | solution.py:350
  68.4 8.1 %collective-permute-start.8 = (f32[4,16,128]{2,1,0:T(8,128)S(1)}, f32[4,16,128]{2,1,0:T(8,128)S(1)}, u32[]{:S(2)}, u32[]{:S(2)}) collective-permute-start(f32[4,16,128]{2,1,0:T(8,128)S(1)} %get-tuple-element.16), channel_id=1, source_target_pairs={{0,911},{1,0},{2,1},{3,2},{4,3},{5,4},{6,5},{7,6},{8,7},{9,8},{10,... | collective-permute-start | bytes 98312 | tf_op jit(solution)/shard_map/ppermute | solution.py:350
  76.5 0.0 collective-permute-done.7.zl_ref
  76.5 1.6 %collective-permute-done.8.zr_ref = f32[4,16,128]{2,1,0:T(8,128)S(1)} collective-permute-done((f32[4,16,128]{2,1,0:T(8,128)S(1)}, f32[4,16,128]{2,1,0:T(8,128)S(1)}, u32[]{:S(2)}, u32[]{:S(2)}) %collective-permute-start.8) | collective-permute-done | bytes 32800 | tf_op jit(solution)/shard_map/ppermute | solution.py:350
  78.0 0.6 shard_map.30
  78.7 0.8 collective-permute-start.9
  79.5 0.0 collective-permute-start.10
  79.5 3.4 %collective-permute-done.9.above_ref = f32[52,8,128]{2,1,0:T(8,128)S(1)} collective-permute-done((f32[52,8,128]{2,1,0:T(8,128)S(1)}, f32[52,8,128]{2,1,0:T(8,128)S(1)}, u32[]{:S(2)}, u32[]{:S(2)}) %collective-permute-start.9) | collective-permute-done | bytes 213024 | tf_op jit(solution)/shard_map/ppermute | solution.py:350
  82.9 3.1 %collective-permute-done.10.below_ref = f32[52,8,128]{2,1,0:T(8,128)S(1)} collective-permute-done((f32[52,8,128]{2,1,0:T(8,128)S(1)}, f32[52,8,128]{2,1,0:T(8,128)S(1)}, u32[]{:S(2)}, u32[]{:S(2)}) %collective-permute-start.10) | collective-permute-done | bytes 213024 | tf_op jit(solution)/shard_map/ppermute | solution.py:350
  86.0 9.4 %shard_map.31 = f32[3,8,16,128]{3,2,1,0:T(8,128)} custom-call(s32[4]{0:T(128)S(1)} %pad_add_fusion.place_ref, f32[3,8,16,128]{3,2,1,0:T(8,128)S(1)} %copy-done.1, f32[3,8,16,128]{3,2,1,0:T(8,128)S(1)} %copy-done.3, f32[14,16,128]{2,1,0:T(8,128)S(1)} %collective-permute-done.ac_ref, f32[12,16,128]{2,1,0:T(8,128)S(1)} %slice_select_fusion.av_ref, ...), custom_call_target="tpu_custom_call" | custom-call | tf_op jit(solution)/shard_map/pallas_call | solution.py:382
  (8 shorter events, 0.1 us)
Async XLA Ops:
  0.1 0.9 copy-start
  1.0 0.9 copy-start.2
  3.5 4.9 %collective-permute-start.1 = (f32[12,16,128]{2,1,0:T(8,128)S(1)}, f32[12,16,128]{2,1,0:T(8,128)S(1)}, u32[]{:S(2)}, u32[]{:S(2)}) collective-permute-start(f32[12,16,128]{2,1,0:T(8,128)S(1)} %get-tuple-element.13), channel_id=1, source_target_pairs={{0,128},{1,129},{2,130},{3,131},{4,132},{5,133},{6,134},{7,135},{8... | collective-permute-start | bytes 294920 | tf_op jit(solution)/shard_map/ppermute | solution.py:350
  8.4 39.2 %collective-permute-start.2 = (f32[14,16,128]{2,1,0:T(8,128)S(1)}, f32[14,16,128]{2,1,0:T(8,128)S(1)}, u32[]{:S(2)}, u32[]{:S(2)}) collective-permute-start(f32[14,16,128]{2,1,0:T(8,128)S(1)} %pad_maximum_fusion), channel_id=1, source_target_pairs={{128,768},{129,769},{130,770},{131,771},{132,772},{133,773},{134,7... | collective-permute-start | bytes 344072 | tf_op jit(solution)/shard_map/ppermute | solution.py:350
  9.1 39.2 %collective-permute-start = (f32[14,16,128]{2,1,0:T(8,128)S(1)}, f32[14,16,128]{2,1,0:T(8,128)S(1)}, u32[]{:S(2)}, u32[]{:S(2)}) collective-permute-start(f32[14,16,128]{2,1,0:T(8,128)S(1)} %get-tuple-element.12), channel_id=1, source_target_pairs={{0,896},{1,897},{2,898},{3,899},{4,900},{5,901},{6,902},{7,903},{8... | collective-permute-start | bytes 344072 | tf_op jit(solution)/shard_map/ppermute | solution.py:350
  38.7 24.1 %collective-permute-start.4 = (f32[12,16,128]{2,1,0:T(8,128)S(1)}, f32[12,16,128]{2,1,0:T(8,128)S(1)}, u32[]{:S(2)}, u32[]{:S(2)}) collective-permute-start(f32[12,16,128]{2,1,0:T(8,128)S(1)} %get-tuple-element.13), channel_id=1, source_target_pairs={{128,256},{129,257},{130,258},{131,259},{132,260},{133,261},{134,2... | collective-permute-start | bytes 294920 | tf_op jit(solution)/shard_map/ppermute | solution.py:350
  39.3 23.4 %collective-permute-start.5 = (f32[6,4,16,128]{3,2,1,0:T(8,128)S(1)}, f32[6,4,16,128]{3,2,1,0:T(8,128)S(1)}, u32[]{:S(2)}, u32[]{:S(2)}) collective-permute-start(f32[6,4,16,128]{3,2,1,0:T(8,128)S(1)} %get-tuple-element.14), channel_id=1, source_target_pairs={{0,128},{1,129},{2,130},{3,131},{4,132},{5,133},{6,134},{7,135},{8... | collective-permute-start | bytes 589832 | tf_op jit(solution)/shard_map/ppermute | solution.py:350
  47.6 12.4 %collective-permute-start.6 = (f32[2,16,128]{2,1,0:T(8,128)S(1)}, f32[2,16,128]{2,1,0:T(8,128)S(1)}, u32[]{:S(2)}, u32[]{:S(2)}) collective-permute-start(f32[2,16,128]{2,1,0:T(8,128)S(1)} %slice.22), channel_id=1, source_target_pairs={{128,256},{129,257},{130,258},{131,259},{132,260},{133,261},{134,2... | collective-permute-start | bytes 49160 | tf_op jit(solution)/shard_map/ppermute | solution.py:350
  48.3 14.5 %copy-start.3 = (f32[3,8,16,128]{3,2,1,0:T(8,128)S(1)}, f32[3,8,16,128]{3,2,1,0:T(8,128)}, u32[]{:S(2)}) copy-start(f32[3,8,16,128]{3,2,1,0:T(8,128)} %v_ref.7) | copy-start | bytes 589828
  48.3 14.4 %copy-start.1 = (f32[3,8,16,128]{3,2,1,0:T(8,128)S(1)}, f32[3,8,16,128]{3,2,1,0:T(8,128)}, u32[]{:S(2)}) copy-start(f32[3,8,16,128]{3,2,1,0:T(8,128)} %c_ref.7) | copy-start | bytes 589828
  48.3 14.4 %collective-permute-start.3 = (f32[14,16,128]{2,1,0:T(8,128)S(1)}, f32[14,16,128]{2,1,0:T(8,128)S(1)}, u32[]{:S(2)}, u32[]{:S(2)}) collective-permute-start(f32[14,16,128]{2,1,0:T(8,128)S(1)} %broadcast_select_fusion), channel_id=1, source_target_pairs={{0,128},{1,129},{2,130},{3,131},{4,132},{5,133},{6,134},{7,135},{8... | collective-permute-start | bytes 344072 | tf_op jit(solution)/shard_map/ppermute | solution.py:350
  64.1 12.4 %collective-permute-start.7 = (f32[4,16,128]{2,1,0:T(8,128)S(1)}, f32[4,16,128]{2,1,0:T(8,128)S(1)}, u32[]{:S(2)}, u32[]{:S(2)}) collective-permute-start(f32[4,16,128]{2,1,0:T(8,128)S(1)} %get-tuple-element.15), channel_id=1, source_target_pairs={{0,1},{1,2},{2,3},{3,4},{4,5},{5,6},{6,7},{7,8},{8,9},{9,10},{10,1... | collective-permute-start | bytes 98312 | tf_op jit(solution)/shard_map/ppermute | solution.py:350
  68.4 9.7 %collective-permute-start.8 = (f32[4,16,128]{2,1,0:T(8,128)S(1)}, f32[4,16,128]{2,1,0:T(8,128)S(1)}, u32[]{:S(2)}, u32[]{:S(2)}) collective-permute-start(f32[4,16,128]{2,1,0:T(8,128)S(1)} %get-tuple-element.16), channel_id=1, source_target_pairs={{0,911},{1,0},{2,1},{3,2},{4,3},{5,4},{6,5},{7,6},{8,7},{9,8},{10,... | collective-permute-start | bytes 98312 | tf_op jit(solution)/shard_map/ppermute | solution.py:350
  78.7 4.2 %collective-permute-start.9 = (f32[52,8,128]{2,1,0:T(8,128)S(1)}, f32[52,8,128]{2,1,0:T(8,128)S(1)}, u32[]{:S(2)}, u32[]{:S(2)}) collective-permute-start(f32[52,8,128]{2,1,0:T(8,128)S(1)} %get-tuple-element.17), channel_id=1, source_target_pairs={{0,112},{1,113},{2,114},{3,115},{4,116},{5,117},{6,118},{7,119},{8... | collective-permute-start | bytes 638984 | tf_op jit(solution)/shard_map/ppermute | solution.py:350
  79.5 6.5 %collective-permute-start.10 = (f32[52,8,128]{2,1,0:T(8,128)S(1)}, f32[52,8,128]{2,1,0:T(8,128)S(1)}, u32[]{:S(2)}, u32[]{:S(2)}) collective-permute-start(f32[52,8,128]{2,1,0:T(8,128)S(1)} %get-tuple-element.18), channel_id=1, source_target_pairs={{0,16},{1,17},{2,18},{3,19},{4,20},{5,21},{6,22},{7,23},{8,24},{9,... | collective-permute-start | bytes 638984 | tf_op jit(solution)/shard_map/ppermute | solution.py:350

commit v6 on v5

--- a/solution.py
+++ b/solution.py
@@ -8,6 +8,9 @@
 
 AXES = ("gx", "gy", "gz")
 HALF = 0.5
+DIRECT = 4
+STRIPS = 4 * DIRECT
+RELAYED = 24 - STRIPS
 
 
 def flat_pairs(mesh, move):
@@ -52,6 +55,10 @@
     return (c_ref, field) if field < 3 else (v_ref, field - 3)
 
 
+def across_field(ac_ref, av_ref, field):
+    return (ac_ref, field) if field < DIRECT else (av_ref, field - DIRECT)
+
+
 def pack_x(place_ref, c_ref, v_ref, ac_ref, av_ref, b_ref, edge_ref):
     high = 4 * place_ref[0]
     low = 4 - high
@@ -60,7 +67,7 @@
     def copy(q):
         for field in range(6):
             ref, i = field_of(c_ref, v_ref, field)
-            to, j = field_of(ac_ref, av_ref, field)
+            to, j = across_field(ac_ref, av_ref, field)
             to[4 * j + q] = ref[i, high + q]
             b_ref[field, q] = ref[i, low + q]
         lane = lanes_of((16, 128))
@@ -75,11 +82,11 @@
 
     loop(0, 4, copy)
     for q in range(2):
-        ac_ref[12 + q] = edge_ref[q] + roll(edge_ref[q + 2], 64, 1)
+        ac_ref[STRIPS + q] = edge_ref[q] + roll(edge_ref[q + 2], 64, 1)
 
 
 def lower_upper(odd, ac_ref, av_ref, b_ref, field, q):
-    ref, i = field_of(ac_ref, av_ref, field)
+    ref, i = across_field(ac_ref, av_ref, field)
     a, b = ref[4 * i + q], b_ref[field, q]
     return jnp.where(odd, b, a), jnp.where(odd, a, b)
 
@@ -356,19 +363,20 @@
         far = (x % 4 == 0) | (x % 4 == 3)
         layers = (6, 4, 16, 128)
         edge = (4, 16, 128)
-        ac, av, b, _ = call(pack_x, [(14, 16, 128), (12, 16, 128), layers, edge], (), 2)(place, c, v)
-        own_end = ac[12:]
+        shapes = [(STRIPS + 2, 16, 128), (RELAYED, 16, 128), layers, edge]
+        ac, av, b, _ = call(pack_x, shapes, (), 2)(place, c, v)
+        own_end = ac[STRIPS:]
         passed = send(av, aside)
         ac = send(ac, across)
         passed = send(jnp.concatenate([passed, own_end]), relay)
         near_av = send(av, beside)
         b = send(b, other)
-        held = jnp.where(far, ac, passed)
+        held = jnp.where(far, ac[STRIPS - RELAYED :], passed)
         forwarded = send(held, other)
-        end_a = jnp.where(far, own_end, send(passed[12:], beside))
-        av = jnp.where(far, forwarded[:12], near_av)
+        end_a = jnp.where(far, own_end, send(passed[RELAYED:], beside))
+        av = jnp.where(far, forwarded[:RELAYED], near_av)
         left, right = call(pack_z, [edge, edge], (), 8)(
-            place, c, v, ac, av, b, held[12:], end_a, forwarded[12:]
+            place, c, v, ac, av, b, held[RELAYED:], end_a, forwarded[RELAYED:]
         )
         zl = send(right, z_up)
         zr = send(left, z_down)

time: 96.6 us -> 96.6 us (level)
  transfers between devices with their start and end apart: 11 -> 11, of which waited for: 5 -> 4; matrix products, arithmetic and copies ran while one was open for 0% -> 0% of each run, Pallas kernels for 0% -> 0%
where the time goes in v6:
time: 96.6 us; the launch traced here: 94.8 us
  starting transfers between devices  67.3 us (70%)
  Pallas kernels  12.9 us (13%)
  waiting for transfers between devices  12.4 us (13%)
  local copies, waits for them, and re-layouts  1.88 us (2%)
    ppermute x11, starting transfers between devices, send(): return lax.ppermute(value, AXES, pairs)  67.3 us
    ppermute x11, waiting for transfers between devices, send(): return lax.ppermute(value, AXES, pairs)  12.4 us
    pallas_call x1, Pallas kernels, local(): call(compute, [(3, 8, 16, 128)], scratch, 9)  9.38 us
  transfers between devices with their start and end apart: 11, of which 4 were waited for; matrix products, arithmetic and copies ran while one was open for 0% of the time, Pallas kernels for 0%

profile of v6, /device:TPU:6, one launch (start us, length us, event | category | flops | bytes accessed | tf_op | source)
XLA Modules:
  0.0 94.8 jit_solution(4385930063001208725)
XLA Ops:
  0.0 0.1 pad_add_fusion.place_ref
  0.1 0.0 copy-start
  0.1 0.9 copy-done
  1.0 0.0 copy-start.2
  1.0 0.9 copy-done.2
  1.9 1.6 %shard_map.28 = (f32[18,16,128]{2,1,0:T(8,128)S(1)}, f32[8,16,128]{2,1,0:T(8,128)S(1)}, f32[6,4,16,128]{3,2,1,0:T(8,128)S(1)}, f32[4,16,128]{2,1,0:T(8,128)}) custom-call(s32[4]{0:T(128)S(1)} %pad_add_fusion.place_ref, f32[3,8,16,128]{3,2,1,0:T(8,128)S(1)} %copy-done, f32[3,8,16,128]{3,2,1,0:T(8,128)S(1)} %copy-done.2), custom_call_target="tpu_custom_call" | custom-call | tf_op jit(solution)/shard_map/pallas_call | solution.py:367
  3.5 2.7 %collective-permute-start.1 = (f32[8,16,128]{2,1,0:T(8,128)S(1)}, f32[8,16,128]{2,1,0:T(8,128)S(1)}, u32[]{:S(2)}, u32[]{:S(2)}) collective-permute-start(f32[8,16,128]{2,1,0:T(8,128)S(1)} %get-tuple-element.13), channel_id=1, source_target_pairs={{0,128},{1,129},{2,130},{3,131},{4,132},{5,133},{6,134},{7,135},{8... | collective-permute-start | bytes 196616 | tf_op jit(solution)/shard_map/ppermute | solution.py:357
  6.2 29.6 %collective-permute-start = (f32[18,16,128]{2,1,0:T(8,128)S(1)}, f32[18,16,128]{2,1,0:T(8,128)S(1)}, u32[]{:S(2)}, u32[]{:S(2)}) collective-permute-start(f32[18,16,128]{2,1,0:T(8,128)S(1)} %get-tuple-element.12), channel_id=1, source_target_pairs={{0,896},{1,897},{2,898},{3,899},{4,900},{5,901},{6,902},{7,903},{8... | collective-permute-start | bytes 442376 | tf_op jit(solution)/shard_map/ppermute | solution.py:357
  35.8 0.0 collective-permute-done.1
  35.8 0.7 collective-permute-start.2
  36.5 0.7 collective-permute-start.4
  37.2 7.6 %collective-permute-start.5 = (f32[6,4,16,128]{3,2,1,0:T(8,128)S(1)}, f32[6,4,16,128]{3,2,1,0:T(8,128)S(1)}, u32[]{:S(2)}, u32[]{:S(2)}) collective-permute-start(f32[6,4,16,128]{3,2,1,0:T(8,128)S(1)} %get-tuple-element.14), channel_id=1, source_target_pairs={{0,128},{1,129},{2,130},{3,131},{4,132},{5,133},{6,134},{7,135},{8... | collective-permute-start | bytes 589832 | tf_op jit(solution)/shard_map/ppermute | solution.py:357
  44.8 0.0 collective-permute-done.2
  44.8 0.7 collective-permute-start.6
  45.4 0.0 collective-permute-done.ac_ref
  45.5 0.0 copy-start.3
  45.5 0.0 copy-start.1
  45.5 8.6 %collective-permute-start.3 = (f32[10,16,128]{2,1,0:T(8,128)S(1)}, f32[10,16,128]{2,1,0:T(8,128)S(1)}, u32[]{:S(2)}, u32[]{:S(2)}) collective-permute-start(f32[10,16,128]{2,1,0:T(8,128)S(1)} %slice_select_fusion), channel_id=1, source_target_pairs={{0,128},{1,129},{2,130},{3,131},{4,132},{5,133},{6,134},{7,135},{8... | collective-permute-start | bytes 245768 | tf_op jit(solution)/shard_map/ppermute | solution.py:357
  54.1 0.0 collective-permute-done.6
  54.1 2.4 %collective-permute-done.3 = f32[10,16,128]{2,1,0:T(8,128)S(1)} collective-permute-done((f32[10,16,128]{2,1,0:T(8,128)S(1)}, f32[10,16,128]{2,1,0:T(8,128)S(1)}, u32[]{:S(2)}, u32[]{:S(2)}) %collective-permute-start.3) | collective-permute-done | bytes 81952 | tf_op jit(solution)/shard_map/ppermute | solution.py:357
  56.5 0.0 collective-permute-done.4
  56.5 0.0 collective-permute-done.5.b_ref
  56.5 0.0 copy-done.3
  56.5 0.0 copy-done.1
  56.5 1.3 %shard_map.29 = (f32[4,16,128]{2,1,0:T(8,128)S(1)}, f32[4,16,128]{2,1,0:T(8,128)S(1)}) custom-call(s32[4]{0:T(128)S(1)} %pad_add_fusion.place_ref, f32[3,8,16,128]{3,2,1,0:T(8,128)S(1)} %copy-done.1, f32[3,8,16,128]{3,2,1,0:T(8,128)S(1)} %copy-done.3, f32[18,16,128]{2,1,0:T(8,128)S(1)} %collective-permute-done.ac_ref, ...), custom_call_target="tpu_custom_call" | custom-call | tf_op jit(solution)/shard_map/pallas_call | solution.py:378
  57.9 14.5 %collective-permute-start.7 = (f32[4,16,128]{2,1,0:T(8,128)S(1)}, f32[4,16,128]{2,1,0:T(8,128)S(1)}, u32[]{:S(2)}, u32[]{:S(2)}) collective-permute-start(f32[4,16,128]{2,1,0:T(8,128)S(1)} %get-tuple-element.15), channel_id=1, source_target_pairs={{0,1},{1,2},{2,3},{3,4},{4,5},{5,6},{6,7},{7,8},{8,9},{9,10},{10,1... | collective-permute-start | bytes 98312 | tf_op jit(solution)/shard_map/ppermute | solution.py:357
  72.3 1.9 %collective-permute-start.8 = (f32[4,16,128]{2,1,0:T(8,128)S(1)}, f32[4,16,128]{2,1,0:T(8,128)S(1)}, u32[]{:S(2)}, u32[]{:S(2)}) collective-permute-start(f32[4,16,128]{2,1,0:T(8,128)S(1)} %get-tuple-element.16), channel_id=1, source_target_pairs={{0,911},{1,0},{2,1},{3,2},{4,3},{5,4},{6,5},{7,6},{8,7},{9,8},{10,... | collective-permute-start | bytes 98312 | tf_op jit(solution)/shard_map/ppermute | solution.py:357
  74.3 0.0 collective-permute-done.7.zl_ref
  74.3 3.9 %collective-permute-done.8.zr_ref = f32[4,16,128]{2,1,0:T(8,128)S(1)} collective-permute-done((f32[4,16,128]{2,1,0:T(8,128)S(1)}, f32[4,16,128]{2,1,0:T(8,128)S(1)}, u32[]{:S(2)}, u32[]{:S(2)}) %collective-permute-start.8) | collective-permute-done | bytes 32800 | tf_op jit(solution)/shard_map/ppermute | solution.py:357
  78.1 0.6 shard_map.30
  78.8 0.0 collective-permute-start.9
  78.8 0.5 collective-permute-start.10
  79.3 2.9 %collective-permute-done.9.above_ref = f32[52,8,128]{2,1,0:T(8,128)S(1)} collective-permute-done((f32[52,8,128]{2,1,0:T(8,128)S(1)}, f32[52,8,128]{2,1,0:T(8,128)S(1)}, u32[]{:S(2)}, u32[]{:S(2)}) %collective-permute-start.9) | collective-permute-done | bytes 213024 | tf_op jit(solution)/shard_map/ppermute | solution.py:357
  82.2 3.3 %collective-permute-done.10.below_ref = f32[52,8,128]{2,1,0:T(8,128)S(1)} collective-permute-done((f32[52,8,128]{2,1,0:T(8,128)S(1)}, f32[52,8,128]{2,1,0:T(8,128)S(1)}, u32[]{:S(2)}, u32[]{:S(2)}) %collective-permute-start.10) | collective-permute-done | bytes 213024 | tf_op jit(solution)/shard_map/ppermute | solution.py:357
  85.4 9.4 %shard_map.31 = f32[3,8,16,128]{3,2,1,0:T(8,128)} custom-call(s32[4]{0:T(128)S(1)} %pad_add_fusion.place_ref, f32[3,8,16,128]{3,2,1,0:T(8,128)S(1)} %copy-done.1, f32[3,8,16,128]{3,2,1,0:T(8,128)S(1)} %copy-done.3, f32[18,16,128]{2,1,0:T(8,128)S(1)} %collective-permute-done.ac_ref, f32[8,16,128]{2,1,0:T(8,128)S(1)} %slice_select_fusion.1.av_ref, ...), custom_call_target="tpu_custom_call" | custom-call | tf_op jit(solution)/shard_map/pallas_call | solution.py:390
  (8 shorter events, 0.0 us)
Async XLA Ops:
  0.1 0.9 copy-start
  1.0 0.9 copy-start.2
  3.5 32.3 %collective-permute-start.1 = (f32[8,16,128]{2,1,0:T(8,128)S(1)}, f32[8,16,128]{2,1,0:T(8,128)S(1)}, u32[]{:S(2)}, u32[]{:S(2)}) collective-permute-start(f32[8,16,128]{2,1,0:T(8,128)S(1)} %get-tuple-element.13), channel_id=1, source_target_pairs={{0,128},{1,129},{2,130},{3,131},{4,132},{5,133},{6,134},{7,135},{8... | collective-permute-start | bytes 196616 | tf_op jit(solution)/shard_map/ppermute | solution.py:357
  6.2 39.2 %collective-permute-start = (f32[18,16,128]{2,1,0:T(8,128)S(1)}, f32[18,16,128]{2,1,0:T(8,128)S(1)}, u32[]{:S(2)}, u32[]{:S(2)}) collective-permute-start(f32[18,16,128]{2,1,0:T(8,128)S(1)} %get-tuple-element.12), channel_id=1, source_target_pairs={{0,896},{1,897},{2,898},{3,899},{4,900},{5,901},{6,902},{7,903},{8... | collective-permute-start | bytes 442376 | tf_op jit(solution)/shard_map/ppermute | solution.py:357
  35.8 8.9 %collective-permute-start.2 = (f32[10,16,128]{2,1,0:T(8,128)S(1)}, f32[10,16,128]{2,1,0:T(8,128)S(1)}, u32[]{:S(2)}, u32[]{:S(2)}) collective-permute-start(f32[10,16,128]{2,1,0:T(8,128)S(1)} %pad_maximum_fusion), channel_id=1, source_target_pairs={{128,768},{129,769},{130,770},{131,771},{132,772},{133,773},{134,7... | collective-permute-start | bytes 245768 | tf_op jit(solution)/shard_map/ppermute | solution.py:357
  36.5 20.0 %collective-permute-start.4 = (f32[8,16,128]{2,1,0:T(8,128)S(1)}, f32[8,16,128]{2,1,0:T(8,128)S(1)}, u32[]{:S(2)}, u32[]{:S(2)}) collective-permute-start(f32[8,16,128]{2,1,0:T(8,128)S(1)} %get-tuple-element.13), channel_id=1, source_target_pairs={{128,256},{129,257},{130,258},{131,259},{132,260},{133,261},{134,2... | collective-permute-start | bytes 196616 | tf_op jit(solution)/shard_map/ppermute | solution.py:357
  37.2 19.3 %collective-permute-start.5 = (f32[6,4,16,128]{3,2,1,0:T(8,128)S(1)}, f32[6,4,16,128]{3,2,1,0:T(8,128)S(1)}, u32[]{:S(2)}, u32[]{:S(2)}) collective-permute-start(f32[6,4,16,128]{3,2,1,0:T(8,128)S(1)} %get-tuple-element.14), channel_id=1, source_target_pairs={{0,128},{1,129},{2,130},{3,131},{4,132},{5,133},{6,134},{7,135},{8... | collective-permute-start | bytes 589832 | tf_op jit(solution)/shard_map/ppermute | solution.py:357
  44.8 9.3 %collective-permute-start.6 = (f32[2,16,128]{2,1,0:T(8,128)S(1)}, f32[2,16,128]{2,1,0:T(8,128)S(1)}, u32[]{:S(2)}, u32[]{:S(2)}) collective-permute-start(f32[2,16,128]{2,1,0:T(8,128)S(1)} %slice.27), channel_id=1, source_target_pairs={{128,256},{129,257},{130,258},{131,259},{132,260},{133,261},{134,2... | collective-permute-start | bytes 49160 | tf_op jit(solution)/shard_map/ppermute | solution.py:357
  45.5 11.1 %copy-start.3 = (f32[3,8,16,128]{3,2,1,0:T(8,128)S(1)}, f32[3,8,16,128]{3,2,1,0:T(8,128)}, u32[]{:S(2)}) copy-start(f32[3,8,16,128]{3,2,1,0:T(8,128)} %v_ref.7) | copy-start | bytes 589828
  45.5 11.0 %copy-start.1 = (f32[3,8,16,128]{3,2,1,0:T(8,128)S(1)}, f32[3,8,16,128]{3,2,1,0:T(8,128)}, u32[]{:S(2)}) copy-start(f32[3,8,16,128]{3,2,1,0:T(8,128)} %c_ref.7) | copy-start | bytes 589828
  45.5 11.0 %collective-permute-start.3 = (f32[10,16,128]{2,1,0:T(8,128)S(1)}, f32[10,16,128]{2,1,0:T(8,128)S(1)}, u32[]{:S(2)}, u32[]{:S(2)}) collective-permute-start(f32[10,16,128]{2,1,0:T(8,128)S(1)} %slice_select_fusion), channel_id=1, source_target_pairs={{0,128},{1,129},{2,130},{3,131},{4,132},{5,133},{6,134},{7,135},{8... | collective-permute-start | bytes 245768 | tf_op jit(solution)/shard_map/ppermute | solution.py:357
  57.9 16.4 %collective-permute-start.7 = (f32[4,16,128]{2,1,0:T(8,128)S(1)}, f32[4,16,128]{2,1,0:T(8,128)S(1)}, u32[]{:S(2)}, u32[]{:S(2)}) collective-permute-start(f32[4,16,128]{2,1,0:T(8,128)S(1)} %get-tuple-element.15), channel_id=1, source_target_pairs={{0,1},{1,2},{2,3},{3,4},{4,5},{5,6},{6,7},{7,8},{8,9},{9,10},{10,1... | collective-permute-start | bytes 98312 | tf_op jit(solution)/shard_map/ppermute | solution.py:357
  72.3 5.8 %collective-permute-start.8 = (f32[4,16,128]{2,1,0:T(8,128)S(1)}, f32[4,16,128]{2,1,0:T(8,128)S(1)}, u32[]{:S(2)}, u32[]{:S(2)}) collective-permute-start(f32[4,16,128]{2,1,0:T(8,128)S(1)} %get-tuple-element.16), channel_id=1, source_target_pairs={{0,911},{1,0},{2,1},{3,2},{4,3},{5,4},{6,5},{7,6},{8,7},{9,8},{10,... | collective-permute-start | bytes 98312 | tf_op jit(solution)/shard_map/ppermute | solution.py:357
  78.8 3.4 %collective-permute-start.9 = (f32[52,8,128]{2,1,0:T(8,128)S(1)}, f32[52,8,128]{2,1,0:T(8,128)S(1)}, u32[]{:S(2)}, u32[]{:S(2)}) collective-permute-start(f32[52,8,128]{2,1,0:T(8,128)S(1)} %get-tuple-element.17), channel_id=1, source_target_pairs={{0,112},{1,113},{2,114},{3,115},{4,116},{5,117},{6,118},{7,119},{8... | collective-permute-start | bytes 638984 | tf_op jit(solution)/shard_map/ppermute | solution.py:357
  78.8 6.6 %collective-permute-start.10 = (f32[52,8,128]{2,1,0:T(8,128)S(1)}, f32[52,8,128]{2,1,0:T(8,128)S(1)}, u32[]{:S(2)}, u32[]{:S(2)}) collective-permute-start(f32[52,8,128]{2,1,0:T(8,128)S(1)} %get-tuple-element.18), channel_id=1, source_target_pairs={{0,16},{1,17},{2,18},{3,19},{4,20},{5,21},{6,22},{7,23},{8,24},{9,... | collective-permute-start | bytes 638984 | tf_op jit(solution)/shard_map/ppermute | solution.py:357

commit v7 on v5

--- a/solution.py
+++ b/solution.py
@@ -116,26 +116,44 @@
     loop(0, 4, pack)
 
 
-def pack_y(
-    place_ref, c_ref, v_ref, ac_ref, av_ref, b_ref, zl_ref, zr_ref, down_ref, up_ref
-):
-    odd = place_ref[0] == 1
+def join(down_ref, up_ref, entry, first, second):
     upper = rows_of((8, 128)) < 4
-
-    def join(entry, first, second):
-        down_ref[entry] = jnp.where(upper, first[0:8], roll(second[0:8], 4, 0))
-        up_ref[entry] = jnp.where(upper, roll(first[8:16], 4, 0), second[8:16])
-
-    def pack(q):
-        for field in range(6):
-            ref, i = field_of(c_ref, v_ref, field)
-            lo, hi = lower_upper(odd, ac_ref, av_ref, b_ref, field, q)
-            near, far = ref[i, q], ref[i, 4 + q]
-            join(8 * field + q, lo, far)
-            join(8 * field + 4 + q, near, hi)
-        join(48 + q, zl_ref[q], zr_ref[q])
-
-    loop(0, 4, pack)
+    down_ref[entry] = jnp.where(upper, first[0:8], roll(second[0:8], 4, 0))
+    up_ref[entry] = jnp.where(upper, roll(first[8:16], 4, 0), second[8:16])
+
+
+def halo(above_ref, below_ref, entry):
+    upper = rows_of((8, 128)) < 4
+    above, below = above_ref[entry], below_ref[entry]
+    first = jnp.where(upper, above, roll(below, 4, 0))
+    return first, jnp.where(upper, roll(above, 4, 0), below)
+
+
+def pack_y_early(place_ref, c_ref, v_ref, b_ref, down_ref, up_ref):
+    for field in range(6):
+        ref, i = field_of(c_ref, v_ref, field)
+
+        def own(q):
+            join(down_ref, up_ref, 6 * field + q, ref[i, q], ref[i, 4 + q])
+
+        def side(q):
+            join(down_ref, up_ref, 6 * field + 4 + q, b_ref[field, q], b_ref[field, 2 + q])
+
+        loop(0, 4, own)
+        loop(0, 2, side)
+
+
+def pack_y_late(place_ref, ac_ref, av_ref, zl_ref, zr_ref, down_ref, up_ref):
+    def side(q):
+        for field in range(6):
+            ref, i = field_of(ac_ref, av_ref, field)
+            join(down_ref, up_ref, 2 * field + q, ref[4 * i + q], ref[4 * i + 2 + q])
+
+    def strip(q):
+        join(down_ref, up_ref, 12 + q, zl_ref[q], zr_ref[q])
+
+    loop(0, 2, side)
+    loop(0, 4, strip)
 
 
 def weights(v):
@@ -183,35 +201,128 @@
     )
 
 
-def compute(
-    place_ref, c_ref, v_ref, ac_ref, av_ref, b_ref, zl_ref, zr_ref, above_ref, below_ref, out_ref,
-    m_ref, ec_ref, ev_ref, ed_ref, x_ref, ex_ref, s_ref, es_ref,
+def along_x(sources, v_of, stores, rows, base, count):
+    open_sums = {}
+    for p in range(-2, count + 2):
+        w = weights(v_of(base + p, rows))
+        cs = [source(base + p, rows) for source in sources]
+        for a in range(-2, 3):
+            to = p + a
+            if 0 <= to < count:
+                terms = [w[a + 2] * c for c in cs]
+                had = open_sums.get(to)
+                open_sums[to] = terms if had is None else [h + t for h, t in zip(had, terms)]
+        done = open_sums.pop(p - 2, None)
+        if done is not None:
+            for store, value in zip(stores, done):
+                store(base + p - 2, rows, value)
+
+
+def put(ref, *lead):
+    def store(p, rows, value):
+        ref[(*lead, p, rows)] = value
+
+    return store
+
+
+def get(ref, *lead):
+    return lambda p, rows: ref[(*lead, p, rows)]
+
+
+def over_tiles(body):
+    loop(0, 3, lambda tile: body(pl.ds(pl.multiple_of(8 * tile, 8), 8)))
+
+
+def main_along_x(from_ref, m_ref, x_ref, base, count):
+    sources = [get(from_ref, i) for i in range(3)]
+    stores = [put(x_ref, i) for i in range(3)]
+    over_tiles(lambda rows: along_x(sources, get(m_ref, 3), stores, rows, base, count))
+
+
+def main_along_yz(m_ref, x_ref, s_ref, slot, rows):
+    w = weights(m_ref[4, slot])
+    cs = [spread(x_ref[i, slot], w, 0)[0:rows] for i in range(3)]
+    w = weights(m_ref[5, slot, 0:rows])
+    cs = [spread(c, w, 1) for c in cs]
+    return [c + HALF * sum(cs[j] * s_ref[j, i, slot, 0:rows] for j in range(3)) for i, c in enumerate(cs)]
+
+
+def main_slopes(m_ref, s_ref, slot):
+    for i in range(3):
+        v = m_ref[3 + i, slot]
+        s_ref[0, i, slot] = slope_of(*[m_ref[3 + i, slot + k] for k in (-2, -1, 1, 2)])
+        s_ref[1, i, slot] = slope_roll(v, 0)
+        s_ref[2, i, slot] = slope_roll(v, 1)
+
+
+def compute_early(
+    place_ref, c_ref, v_ref, b_ref, above_ref, below_ref, m_ref, n_ref, s_ref, o_ref, x_ref
 ):
-    odd = place_ref[0] == 1
-    upper = rows_of((8, 128)) < 4
-
-    def halo(entry):
-        above, below = above_ref[entry], below_ref[entry]
-        first = jnp.where(upper, above, roll(below, 4, 0))
-        return first, jnp.where(upper, roll(above, 4, 0), below)
-
-    def widen(q):
+    odd = place_ref[0]
+    side = 12 - 12 * odd
+    first = 4 - 4 * odd
+
+    def own(q):
         for field in range(6):
             ref, i = field_of(c_ref, v_ref, field)
-            lo, hi = lower_upper(odd, ac_ref, av_ref, b_ref, field, q)
-            m_ref[field, q, 0:16] = lo
             m_ref[field, 4 + q, 0:16] = ref[i, q]
             m_ref[field, 8 + q, 0:16] = ref[i, 4 + q]
-            m_ref[field, 12 + q, 0:16] = hi
-            m_ref[field, q, 16:24], m_ref[field, 8 + q, 16:24] = halo(8 * field + q)
-            m_ref[field, 4 + q, 16:24], m_ref[field, 12 + q, 16:24] = halo(8 * field + 4 + q)
-
-    loop(0, 4, widen)
+            m_ref[field, 4 + q, 16:24], m_ref[field, 8 + q, 16:24] = halo(
+                above_ref, below_ref, 6 * field + q
+            )
+
+    def beyond(q):
+        for field in range(6):
+            m_ref[field, side + q, 0:16] = b_ref[field, q]
+            m_ref[field, side + 2 + q, 0:16] = b_ref[field, 2 + q]
+            m_ref[field, side + q, 16:24], m_ref[field, side + 2 + q, 16:24] = halo(
+                above_ref, below_ref, 6 * field + 4 + q
+            )
+
+    loop(0, 4, own)
+    loop(0, 2, beyond)
+    loop(0, 8, lambda k: main_slopes(m_ref, s_ref, first + 2 + k), 2)
+    main_along_x(m_ref, m_ref, x_ref, first + 2, 8)
+
+    def substep_one(k):
+        slot = first + 2 + k
+        for i, value in enumerate(main_along_yz(m_ref, x_ref, s_ref, slot, 24)):
+            n_ref[i, slot] = value
+
+    def substep_two(k):
+        slot = first + 4 + k
+        for i, value in enumerate(main_along_yz(m_ref, x_ref, s_ref, slot, 16)):
+            o_ref[i, slot - 4] = value
+
+    loop(0, 8, substep_one, 2)
+    main_along_x(n_ref, m_ref, x_ref, first + 4, 4)
+    loop(0, 4, substep_two, 2)
+
+
+def compute_late(
+    place_ref, ac_ref, av_ref, zl_ref, zr_ref, above_ref, below_ref, m_in, n_in, s_in, o_in,
+    m_ref, n_ref, s_ref, o_ref, out_ref, x_ref, ec_ref, ev_ref, ed_ref, ex_ref, es_ref,
+):
+    odd = place_ref[0]
+    side = 12 * odd
+    first = 2 + 8 * odd
+    second = 4 + 4 * odd
+
+    def beyond(q):
+        for field in range(6):
+            ref, i = field_of(ac_ref, av_ref, field)
+            m_ref[field, side + q, 0:16] = ref[4 * i + q]
+            m_ref[field, side + 2 + q, 0:16] = ref[4 * i + 2 + q]
+            m_ref[field, side + q, 16:24], m_ref[field, side + 2 + q, 16:24] = halo(
+                above_ref, below_ref, 2 * field + q
+            )
+
+    loop(0, 2, beyond)
 
     def edges(s):
         lane = lanes_of((24, 128))
         g, q = lax.shift_right_logical(s, 2), lax.bitwise_and(s, 3)
-        zl_halo, zr_halo = halo(48 + q)
+        zl_halo, zr_halo = halo(above_ref, below_ref, 12 + q)
         zl = jnp.concatenate([zl_ref[q], zl_halo], axis=0)
         zr = jnp.concatenate([zr_ref[q], zr_halo], axis=0)
         back = 128 - 32 * g
@@ -231,82 +342,55 @@
             ed_ref[k, s] = d
 
     loop(0, 16, edges, 2)
-
-    def slopes(s):
-        for i in range(3):
-            v = m_ref[3 + i, s]
-            s_ref[0, i, s] = slope_of(*[m_ref[3 + i, s + k] for k in (-2, -1, 1, 2)])
-            s_ref[1, i, s] = slope_roll(v, 0)
-            s_ref[2, i, s] = slope_roll(v, 1)
+    loop(0, 4, lambda k: main_slopes(m_ref, s_ref, first + k), 2)
+
+    def edge_slopes(s):
         v = ev_ref[s]
         es_ref[0, s] = slope_of(*[ev_ref[s + k] for k in (-2, -1, 1, 2)])
         es_ref[1, s] = slope_roll(v, 0)
         es_ref[2, s] = slope_roll(v, 1)
 
-    loop(2, 14, slopes, 2)
-
-    def along_x(sources, v_of, stores, rows):
-        open_sums = {}
-        for p in range(16):
-            w = weights(v_of(p, rows))
-            cs = [source(p, rows) for source in sources]
-            for a in range(-2, 3):
-                to = p + a
-                if 2 <= to < 14:
-                    terms = [w[a + 2] * c for c in cs]
-                    had = open_sums.get(to)
-                    open_sums[to] = terms if had is None else [h + t for h, t in zip(had, terms)]
-            done = open_sums.pop(p - 2, None)
-            if done is not None:
-                for store, value in zip(stores, done):
-                    store(p - 2, rows, value)
-
-    def put(ref, *lead):
-        def store(p, rows, value):
-            ref[(*lead, p, rows)] = value
-
-        return store
-
-    def get(ref, *lead):
-        return lambda p, rows: ref[(*lead, p, rows)]
-
-    def tile_along_x(tile):
-        rows = pl.ds(pl.multiple_of(8 * tile, 8), 8)
-        along_x(
-            [get(m_ref, i) for i in range(3)], get(m_ref, 3), [put(x_ref, i) for i in range(3)], rows
-        )
-        along_x([get(ec_ref)], get(ed_ref, 0), [put(ex_ref)], rows)
-
-    def along_yz(s):
-        w = weights(m_ref[4, s])
-        cs = [spread(x_ref[i, s], w, 0) for i in range(3)]
-        w = weights(m_ref[5, s])
-        cs = [spread(c, w, 1) for c in cs]
+    loop(2, 14, edge_slopes, 4)
+
+    def edge_along_yz(s):
         e = spread(ex_ref[s], weights(ed_ref[1, s]), 0)
         e = spread(e, weights(ed_ref[2, s]), 1)
-        for i in range(3):
-            stretch = sum(cs[j] * s_ref[j, i, s] for j in range(3))
-            m_ref[i, s] = cs[i] + HALF * stretch
         parts = replicate(e)
         ec_ref[s] = e + HALF * sum(parts[j] * es_ref[j, s] for j in range(3))
 
-    def substep(n):
-        loop(0, 3, tile_along_x)
-        loop(2, 14, along_yz, 2)
-
-    loop(0, 2, substep)
+    def edge_substep(n):
+        over_tiles(lambda rows: along_x([get(ec_ref)], get(ed_ref, 0), [put(ex_ref)], rows, 2, 12))
+        loop(2, 14, edge_along_yz, 4)
+
+    loop(0, 2, edge_substep)
+
+    main_along_x(m_ref, m_ref, x_ref, first, 4)
+
+    def substep_one(k):
+        slot = first + k
+        for i, value in enumerate(main_along_yz(m_ref, x_ref, s_ref, slot, 24)):
+            n_ref[i, slot] = value
+
+    def substep_two(k):
+        slot = second + k
+        for i, value in enumerate(main_along_yz(m_ref, x_ref, s_ref, slot, 16)):
+            o_ref[i, slot - 4] = value
+
+    loop(0, 4, substep_one, 2)
+    main_along_x(n_ref, m_ref, x_ref, second, 4)
+    loop(0, 4, substep_two, 2)
 
     def finish(s):
         lane = lanes_of((16, 128))
         e = ec_ref[s + 4, 0:16]
         for i in range(3):
-            value = jnp.where(lane < 4, roll(e, -(32 * i + 4), 1), m_ref[i, s + 4, 0:16])
+            value = jnp.where(lane < 4, roll(e, -(32 * i + 4), 1), o_ref[i, s])
             out_ref[i, s] = jnp.where(lane >= 124, roll(e, 100 - 32 * i, 1), value)
 
     loop(0, 8, finish, 2)
 
 
-def call(kernel, outs, scratch=(), operands=0):
+def call(kernel, outs, scratch=(), operands=0, aliases=()):
     smem = pl.BlockSpec(memory_space=pltpu.SMEM)
     vmem = pl.BlockSpec(memory_space=pltpu.VMEM)
     shapes = [jax.ShapeDtypeStruct(o, jnp.float32) for o in outs]
@@ -316,6 +400,7 @@
         in_specs=[smem] + [vmem] * operands,
         out_specs=[vmem] * len(outs),
         scratch_shapes=[pltpu.VMEM(s, jnp.float32) for s in scratch],
+        input_output_aliases=dict(aliases),
         compiler_params=pltpu.CompilerParams(vmem_limit_bytes=16 * 1024 * 1024),
     )
 
@@ -363,6 +448,9 @@
         passed = send(jnp.concatenate([passed, own_end]), relay)
         near_av = send(av, beside)
         b = send(b, other)
+        down, up = call(pack_y_early, [(36, 8, 128)] * 2, (), 3)(place, c, v, b)
+        early_above = send(down, y_down)
+        early_below = send(up, y_up)
         held = jnp.where(far, ac, passed)
         forwarded = send(held, other)
         end_a = jnp.where(far, own_end, send(passed[12:], beside))
@@ -372,14 +460,18 @@
         )
         zl = send(right, z_up)
         zr = send(left, z_down)
-        down, up = call(pack_y, [(52, 8, 128)] * 2, (), 7)(place, c, v, ac, av, b, zl, zr)
+        down, up = call(pack_y_late, [(16, 8, 128)] * 2, (), 4)(place, ac, av, zl, zr)
         above = send(down, y_down)
         below = send(up, y_up)
         block = (16, 24, 128)
-        scratch = [
-            (6, *block), block, block, (3, *block), (3, *block), block, (3, 3, *block), (3, *block),
-        ]
-        (out,) = call(compute, [(3, 8, 16, 128)], scratch, 9)(place, c, v, ac, av, b, zl, zr, above, below)
+        state = [(6, *block), (3, *block), (3, 3, *block), (3, 8, 16, 128)]
+        m, n, s, o = call(compute_early, state, [(3, *block)], 5)(
+            place, c, v, b, early_above, early_below
+        )
+        scratch = [(3, *block), block, block, (3, *block), block, (3, *block)]
+        *_, out = call(
+            compute_late, state + [(3, 8, 16, 128)], scratch, 10, {7 + k: k for k in range(4)}
+        )(place, ac, av, zl, zr, above, below, m, n, s, o)
         return out
 
     placed = P(None, *AXES)

time: 96.6 us -> 93.5 us (0.968)
  waiting for transfers between devices: 13 us -> 7.54 us
  local copies, waits for them, and re-layouts: 1.88 us -> 3.72 us
  starting transfers between devices: 67.3 us -> 65.6 us
  Pallas kernels: 12.9 us -> 14.5 us
    ppermute x11 -> x13, waiting for transfers between devices: 13 us -> 7.54 us  [send(): return lax.ppermute(value, AXES, pairs)]
    unnamed x8 -> x12, local copies, waits for them, and re-layouts: 1.87 us -> 3.71 us
    ppermute x11 -> x13, starting transfers between devices: 67.3 us -> 65.6 us  [send(): return lax.ppermute(value, AXES, pairs)]
    pallas_call x2 -> x4, Pallas kernels: 10 us -> 11.6 us  [the longest x1 7.63 us: local(): call(compute_late, state + [(3, 8, 16, 128)], scratch, 10, {7 + k: k for...]
  transfers between devices with their start and end apart: 11 -> 13, of which waited for: 5 -> 5; matrix products, arithmetic and copies ran while one was open for 0% -> 0% of each run, Pallas kernels for 0% -> 6%
where the time goes in v7:
time: 93.5 us; the launch traced here: 91.7 us
  starting transfers between devices  65.6 us (70%)
  Pallas kernels  14.5 us (16%)
  waiting for transfers between devices  7.54 us (8%)
  local copies, waits for them, and re-layouts  3.72 us (4%)
    ppermute x13, starting transfers between devices, send(): return lax.ppermute(value, AXES, pairs)  65.6 us
    pallas_call x1, Pallas kernels, local(): call(compute_late, state + [(3, 8, 16, 128)], scratch, 10, {7 + k: k for...  7.63 us
    ppermute x13, waiting for transfers between devices, send(): return lax.ppermute(value, AXES, pairs)  7.54 us
    unnamed x12, local copies, waits for them, and re-layouts  3.71 us
    pallas_call x1, Pallas kernels, local(): call(compute_early, state, [(3, *block)], 5)  2.62 us
  transfers between devices with their start and end apart: 13, of which 5 were waited for; matrix products, arithmetic and copies ran while one was open for 0% of the time, Pallas kernels for 6%

profile of v7, /device:TPU:6, one launch (start us, length us, event | category | flops | bytes accessed | tf_op | source)
XLA Modules:
  0.0 91.7 jit_solution(10075357040444658742)
XLA Ops:
  0.0 0.1 pad_add_fusion.place_ref
  0.1 0.0 copy-start
  0.1 0.9 %copy-done = f32[3,8,16,128]{3,2,1,0:T(8,128)S(1)} copy-done((f32[3,8,16,128]{3,2,1,0:T(8,128)S(1)}, f32[3,8,16,128]{3,2,1,0:T(8,128)}, u32[]{:S(2)}) %copy-start) | copy-done | bytes 196632
  1.0 0.0 copy-start.3
  1.0 0.9 %copy-done.3 = f32[3,8,16,128]{3,2,1,0:T(8,128)S(1)} copy-done((f32[3,8,16,128]{3,2,1,0:T(8,128)S(1)}, f32[3,8,16,128]{3,2,1,0:T(8,128)}, u32[]{:S(2)}) %copy-start.3) | copy-done | bytes 196632
  1.9 0.0 copy-start.2
  1.9 0.0 copy-start.5
  1.9 1.6 %shard_map.28 = (f32[14,16,128]{2,1,0:T(8,128)S(1)}, f32[12,16,128]{2,1,0:T(8,128)S(1)}, f32[6,4,16,128]{3,2,1,0:T(8,128)S(1)}, f32[4,16,128]{2,1,0:T(8,128)}) custom-call(s32[4]{0:T(128)S(1)} %pad_add_fusion.place_ref, f32[3,8,16,128]{3,2,1,0:T(8,128)S(1)} %copy-done, f32[3,8,16,128]{3,2,1,0:T(8,128)S(1)} %copy-done.3), custom_call_target="tpu_custom_call" | custom-call | tf_op jit(solution)/shard_map/pallas_call | solution.py:444
  3.5 2.7 %collective-permute-start.1 = (f32[12,16,128]{2,1,0:T(8,128)S(1)}, f32[12,16,128]{2,1,0:T(8,128)S(1)}, u32[]{:S(2)}, u32[]{:S(2)}) collective-permute-start(f32[12,16,128]{2,1,0:T(8,128)S(1)} %get-tuple-element.20), channel_id=1, source_target_pairs={{0,128},{1,129},{2,130},{3,131},{4,132},{5,133},{6,134},{7,135},{8... | collective-permute-start | bytes 294920 | tf_op jit(solution)/shard_map/ppermute | solution.py:435
  6.2 1.9 %collective-permute-start.5 = (f32[6,4,16,128]{3,2,1,0:T(8,128)S(1)}, f32[6,4,16,128]{3,2,1,0:T(8,128)S(1)}, u32[]{:S(2)}, u32[]{:S(2)}) collective-permute-start(f32[6,4,16,128]{3,2,1,0:T(8,128)S(1)} %get-tuple-element.21), channel_id=1, source_target_pairs={{0,128},{1,129},{2,130},{3,131},{4,132},{5,133},{6,134},{7,135},{8... | collective-permute-start | bytes 589832 | tf_op jit(solution)/shard_map/ppermute | solution.py:435
  8.2 0.4 collective-permute-done.1
  8.6 0.7 collective-permute-start.2
  9.3 29.6 %collective-permute-start = (f32[14,16,128]{2,1,0:T(8,128)S(1)}, f32[14,16,128]{2,1,0:T(8,128)S(1)}, u32[]{:S(2)}, u32[]{:S(2)}) collective-permute-start(f32[14,16,128]{2,1,0:T(8,128)S(1)} %get-tuple-element.19), channel_id=1, source_target_pairs={{0,896},{1,897},{2,898},{3,899},{4,900},{5,901},{6,902},{7,903},{8... | collective-permute-start | bytes 344072 | tf_op jit(solution)/shard_map/ppermute | solution.py:435
  38.8 0.7 collective-permute-start.4
  39.5 0.0 collective-permute-done.5.b_ref
  39.5 0.0 copy-start.1
  39.6 0.9 %copy-done.1 = f32[3,8,16,128]{3,2,1,0:T(8,128)S(1)} copy-done((f32[3,8,16,128]{3,2,1,0:T(8,128)S(1)}, f32[3,8,16,128]{3,2,1,0:T(8,128)}, u32[]{:S(2)}) %copy-start.1) | copy-done | bytes 196632
  40.5 0.0 copy-start.4
  40.5 0.9 %copy-done.4 = f32[3,8,16,128]{3,2,1,0:T(8,128)S(1)} copy-done((f32[3,8,16,128]{3,2,1,0:T(8,128)S(1)}, f32[3,8,16,128]{3,2,1,0:T(8,128)}, u32[]{:S(2)}) %copy-start.4) | copy-done | bytes 196632
  41.4 0.8 shard_map.31
  42.2 1.5 %collective-permute-start.11 = (f32[36,8,128]{2,1,0:T(8,128)S(1)}, f32[36,8,128]{2,1,0:T(8,128)S(1)}, u32[]{:S(2)}, u32[]{:S(2)}) collective-permute-start(f32[36,8,128]{2,1,0:T(8,128)S(1)} %get-tuple-element.26), channel_id=1, source_target_pairs={{0,112},{1,113},{2,114},{3,115},{4,116},{5,117},{6,118},{7,119},{8... | collective-permute-start | bytes 442376 | tf_op jit(solution)/shard_map/ppermute | solution.py:435
  43.7 0.0 collective-permute-start.12
  43.7 0.0 collective-permute-done.2
  43.7 0.7 collective-permute-start.6
  44.4 0.6 collective-permute-done.ac_ref
  45.0 14.9 %collective-permute-start.3 = (f32[14,16,128]{2,1,0:T(8,128)S(1)}, f32[14,16,128]{2,1,0:T(8,128)S(1)}, u32[]{:S(2)}, u32[]{:S(2)}) collective-permute-start(f32[14,16,128]{2,1,0:T(8,128)S(1)} %broadcast_select_fusion), channel_id=1, source_target_pairs={{0,128},{1,129},{2,130},{3,131},{4,132},{5,133},{6,134},{7,135},{8... | collective-permute-start | bytes 344072 | tf_op jit(solution)/shard_map/ppermute | solution.py:435
  59.8 0.0 collective-permute-done.6
  59.8 0.0 collective-permute-done.4
  59.9 2.7 %collective-permute-done.3 = f32[14,16,128]{2,1,0:T(8,128)S(1)} collective-permute-done((f32[14,16,128]{2,1,0:T(8,128)S(1)}, f32[14,16,128]{2,1,0:T(8,128)S(1)}, u32[]{:S(2)}, u32[]{:S(2)}) %collective-permute-start.3) | collective-permute-done | bytes 114720 | tf_op jit(solution)/shard_map/ppermute | solution.py:435
  62.6 1.3 %shard_map.29 = (f32[4,16,128]{2,1,0:T(8,128)S(1)}, f32[4,16,128]{2,1,0:T(8,128)S(1)}) custom-call(s32[4]{0:T(128)S(1)} %pad_add_fusion.place_ref, f32[3,8,16,128]{3,2,1,0:T(8,128)S(1)} %copy-done.1, f32[3,8,16,128]{3,2,1,0:T(8,128)S(1)} %copy-done.4, f32[14,16,128]{2,1,0:T(8,128)S(1)} %collective-permute-done.ac_ref, ...), custom_call_target="tpu_custom_call" | custom-call | tf_op jit(solution)/shard_map/pallas_call | solution.py:458
  63.9 4.2 %collective-permute-start.7 = (f32[4,16,128]{2,1,0:T(8,128)S(1)}, f32[4,16,128]{2,1,0:T(8,128)S(1)}, u32[]{:S(2)}, u32[]{:S(2)}) collective-permute-start(f32[4,16,128]{2,1,0:T(8,128)S(1)} %get-tuple-element.22), channel_id=1, source_target_pairs={{0,1},{1,2},{2,3},{3,4},{4,5},{5,6},{6,7},{7,8},{8,9},{9,10},{10,1... | collective-permute-start | bytes 98312 | tf_op jit(solution)/shard_map/ppermute | solution.py:435
  68.1 7.9 %collective-permute-start.8 = (f32[4,16,128]{2,1,0:T(8,128)S(1)}, f32[4,16,128]{2,1,0:T(8,128)S(1)}, u32[]{:S(2)}, u32[]{:S(2)}) collective-permute-start(f32[4,16,128]{2,1,0:T(8,128)S(1)} %get-tuple-element.23), channel_id=1, source_target_pairs={{0,911},{1,0},{2,1},{3,2},{4,3},{5,4},{6,5},{7,6},{8,7},{9,8},{10,... | collective-permute-start | bytes 98312 | tf_op jit(solution)/shard_map/ppermute | solution.py:435
  76.0 0.0 collective-permute-done.7.zl_ref
  76.0 1.6 %collective-permute-done.8.zr_ref = f32[4,16,128]{2,1,0:T(8,128)S(1)} collective-permute-done((f32[4,16,128]{2,1,0:T(8,128)S(1)}, f32[4,16,128]{2,1,0:T(8,128)S(1)}, u32[]{:S(2)}, u32[]{:S(2)}) %collective-permute-start.8) | collective-permute-done | bytes 32800 | tf_op jit(solution)/shard_map/ppermute | solution.py:435
  77.6 0.6 shard_map.30
  78.2 0.9 %collective-permute-start.9 = (f32[16,8,128]{2,1,0:T(8,128)S(1)}, f32[16,8,128]{2,1,0:T(8,128)S(1)}, u32[]{:S(2)}, u32[]{:S(2)}) collective-permute-start(f32[16,8,128]{2,1,0:T(8,128)S(1)} %get-tuple-element.24), channel_id=1, source_target_pairs={{0,112},{1,113},{2,114},{3,115},{4,116},{5,117},{6,118},{7,119},{8... | collective-permute-start | bytes 196616 | tf_op jit(solution)/shard_map/ppermute | solution.py:435
  79.1 0.0 collective-permute-start.10
  79.1 0.0 collective-permute-done.11.above_ref
  79.1 0.0 collective-permute-done.12.below_ref
  79.1 0.0 copy-done.2
  79.1 0.0 copy-done.5
  79.2 2.6 %shard_map.32 = (f32[6,16,24,128]{3,2,1,0:T(8,128)S(1)}, f32[3,16,24,128]{3,2,1,0:T(8,128)S(1)}, f32[3,3,16,24,128]{4,3,2,1,0:T(8,128)S(1)}, f32[3,8,16,128]{3,2,1,0:T(8,128)S(1)}) custom-call(s32[4]{0:T(128)S(1)} %pad_add_fusion.place_ref, f32[3,8,16,128]{3,2,1,0:T(8,128)S(1)} %copy-done.2, f32[3,8,16,128]{3,2,1,0:T(8,128)S(1)} %copy-done.5, ...), custom_call_target="tpu_custom_call" | custom-call | tf_op jit(solution)/shard_map/pallas_call | solution.py:468
  81.8 0.0 collective-permute-done.9.above_ref
  81.8 2.2 %collective-permute-done.10.below_ref = f32[16,8,128]{2,1,0:T(8,128)S(1)} collective-permute-done((f32[16,8,128]{2,1,0:T(8,128)S(1)}, f32[16,8,128]{2,1,0:T(8,128)S(1)}, u32[]{:S(2)}, u32[]{:S(2)}) %collective-permute-start.10) | collective-permute-done | bytes 65568 | tf_op jit(solution)/shard_map/ppermute | solution.py:435
  84.0 7.6 %shard_map.33 = (f32[6,16,24,128]{3,2,1,0:T(8,128)S(1)}, f32[3,16,24,128]{3,2,1,0:T(8,128)S(1)}, f32[3,3,16,24,128]{4,3,2,1,0:T(8,128)S(1)}, f32[3,8,16,128]{3,2,1,0:T(8,128)S(1)}, f32[3,8,16,128]{3,2,1,0:T(8,128)}) custom-call(s32[4]{0:T(128)S(1)} %pad_add_fusion.place_ref, ...), custom_call_target="tpu_custom_call", output_to_operand_aliasing={{0}: (7, {}), {1}: (8, {}), {2}: (9, {}), {3}: (10, {})} | custom-call | tf_op jit(solution)/shard_map/pallas_call | solution.py:472
  (8 shorter events, 0.1 us)
Async XLA Ops:
  0.1 0.9 %copy-start = (f32[3,8,16,128]{3,2,1,0:T(8,128)S(1)}, f32[3,8,16,128]{3,2,1,0:T(8,128)}, u32[]{:S(2)}) copy-start(f32[3,8,16,128]{3,2,1,0:T(8,128)} %c_ref.7) | copy-start | bytes 589828
  1.0 0.9 %copy-start.3 = (f32[3,8,16,128]{3,2,1,0:T(8,128)S(1)}, f32[3,8,16,128]{3,2,1,0:T(8,128)}, u32[]{:S(2)}) copy-start(f32[3,8,16,128]{3,2,1,0:T(8,128)} %v_ref.7) | copy-start | bytes 589828
  1.9 77.2 %copy-start.2 = (f32[3,8,16,128]{3,2,1,0:T(8,128)S(1)}, f32[3,8,16,128]{3,2,1,0:T(8,128)}, u32[]{:S(2)}) copy-start(f32[3,8,16,128]{3,2,1,0:T(8,128)} %c_ref.7) | copy-start | bytes 589828
  1.9 77.2 %copy-start.5 = (f32[3,8,16,128]{3,2,1,0:T(8,128)S(1)}, f32[3,8,16,128]{3,2,1,0:T(8,128)}, u32[]{:S(2)}) copy-start(f32[3,8,16,128]{3,2,1,0:T(8,128)} %v_ref.7) | copy-start | bytes 589828
  3.5 5.1 %collective-permute-start.1 = (f32[12,16,128]{2,1,0:T(8,128)S(1)}, f32[12,16,128]{2,1,0:T(8,128)S(1)}, u32[]{:S(2)}, u32[]{:S(2)}) collective-permute-start(f32[12,16,128]{2,1,0:T(8,128)S(1)} %get-tuple-element.20), channel_id=1, source_target_pairs={{0,128},{1,129},{2,130},{3,131},{4,132},{5,133},{6,134},{7,135},{8... | collective-permute-start | bytes 294920 | tf_op jit(solution)/shard_map/ppermute | solution.py:435
  6.2 33.3 %collective-permute-start.5 = (f32[6,4,16,128]{3,2,1,0:T(8,128)S(1)}, f32[6,4,16,128]{3,2,1,0:T(8,128)S(1)}, u32[]{:S(2)}, u32[]{:S(2)}) collective-permute-start(f32[6,4,16,128]{3,2,1,0:T(8,128)S(1)} %get-tuple-element.21), channel_id=1, source_target_pairs={{0,128},{1,129},{2,130},{3,131},{4,132},{5,133},{6,134},{7,135},{8... | collective-permute-start | bytes 589832 | tf_op jit(solution)/shard_map/ppermute | solution.py:435
  8.6 35.1 %collective-permute-start.2 = (f32[14,16,128]{2,1,0:T(8,128)S(1)}, f32[14,16,128]{2,1,0:T(8,128)S(1)}, u32[]{:S(2)}, u32[]{:S(2)}) collective-permute-start(f32[14,16,128]{2,1,0:T(8,128)S(1)} %pad_maximum_fusion), channel_id=1, source_target_pairs={{128,768},{129,769},{130,770},{131,771},{132,772},{133,773},{134,7... | collective-permute-start | bytes 344072 | tf_op jit(solution)/shard_map/ppermute | solution.py:435
  9.3 35.6 %collective-permute-start = (f32[14,16,128]{2,1,0:T(8,128)S(1)}, f32[14,16,128]{2,1,0:T(8,128)S(1)}, u32[]{:S(2)}, u32[]{:S(2)}) collective-permute-start(f32[14,16,128]{2,1,0:T(8,128)S(1)} %get-tuple-element.19), channel_id=1, source_target_pairs={{0,896},{1,897},{2,898},{3,899},{4,900},{5,901},{6,902},{7,903},{8... | collective-permute-start | bytes 344072 | tf_op jit(solution)/shard_map/ppermute | solution.py:435
  38.8 21.0 %collective-permute-start.4 = (f32[12,16,128]{2,1,0:T(8,128)S(1)}, f32[12,16,128]{2,1,0:T(8,128)S(1)}, u32[]{:S(2)}, u32[]{:S(2)}) collective-permute-start(f32[12,16,128]{2,1,0:T(8,128)S(1)} %get-tuple-element.20), channel_id=1, source_target_pairs={{128,256},{129,257},{130,258},{131,259},{132,260},{133,261},{134,2... | collective-permute-start | bytes 294920 | tf_op jit(solution)/shard_map/ppermute | solution.py:435
  39.5 0.9 %copy-start.1 = (f32[3,8,16,128]{3,2,1,0:T(8,128)S(1)}, f32[3,8,16,128]{3,2,1,0:T(8,128)}, u32[]{:S(2)}) copy-start(f32[3,8,16,128]{3,2,1,0:T(8,128)} %c_ref.7) | copy-start | bytes 589828
  40.5 0.9 %copy-start.4 = (f32[3,8,16,128]{3,2,1,0:T(8,128)S(1)}, f32[3,8,16,128]{3,2,1,0:T(8,128)}, u32[]{:S(2)}) copy-start(f32[3,8,16,128]{3,2,1,0:T(8,128)} %v_ref.7) | copy-start | bytes 589828
  42.2 36.9 %collective-permute-start.11 = (f32[36,8,128]{2,1,0:T(8,128)S(1)}, f32[36,8,128]{2,1,0:T(8,128)S(1)}, u32[]{:S(2)}, u32[]{:S(2)}) collective-permute-start(f32[36,8,128]{2,1,0:T(8,128)S(1)} %get-tuple-element.26), channel_id=1, source_target_pairs={{0,112},{1,113},{2,114},{3,115},{4,116},{5,117},{6,118},{7,119},{8... | collective-permute-start | bytes 442376 | tf_op jit(solution)/shard_map/ppermute | solution.py:435
  43.7 35.5 %collective-permute-start.12 = (f32[36,8,128]{2,1,0:T(8,128)S(1)}, f32[36,8,128]{2,1,0:T(8,128)S(1)}, u32[]{:S(2)}, u32[]{:S(2)}) collective-permute-start(f32[36,8,128]{2,1,0:T(8,128)S(1)} %get-tuple-element.27), channel_id=1, source_target_pairs={{0,16},{1,17},{2,18},{3,19},{4,20},{5,21},{6,22},{7,23},{8,24},{9,... | collective-permute-start | bytes 442376 | tf_op jit(solution)/shard_map/ppermute | solution.py:435
  43.7 16.1 %collective-permute-start.6 = (f32[2,16,128]{2,1,0:T(8,128)S(1)}, f32[2,16,128]{2,1,0:T(8,128)S(1)}, u32[]{:S(2)}, u32[]{:S(2)}) collective-permute-start(f32[2,16,128]{2,1,0:T(8,128)S(1)} %slice.22), channel_id=1, source_target_pairs={{128,256},{129,257},{130,258},{131,259},{132,260},{133,261},{134,2... | collective-permute-start | bytes 49160 | tf_op jit(solution)/shard_map/ppermute | solution.py:435
  45.0 17.6 %collective-permute-start.3 = (f32[14,16,128]{2,1,0:T(8,128)S(1)}, f32[14,16,128]{2,1,0:T(8,128)S(1)}, u32[]{:S(2)}, u32[]{:S(2)}) collective-permute-start(f32[14,16,128]{2,1,0:T(8,128)S(1)} %broadcast_select_fusion), channel_id=1, source_target_pairs={{0,128},{1,129},{2,130},{3,131},{4,132},{5,133},{6,134},{7,135},{8... | collective-permute-start | bytes 344072 | tf_op jit(solution)/shard_map/ppermute | solution.py:435
  63.9 12.1 %collective-permute-start.7 = (f32[4,16,128]{2,1,0:T(8,128)S(1)}, f32[4,16,128]{2,1,0:T(8,128)S(1)}, u32[]{:S(2)}, u32[]{:S(2)}) collective-permute-start(f32[4,16,128]{2,1,0:T(8,128)S(1)} %get-tuple-element.22), channel_id=1, source_target_pairs={{0,1},{1,2},{2,3},{3,4},{4,5},{5,6},{6,7},{7,8},{8,9},{9,10},{10,1... | collective-permute-start | bytes 98312 | tf_op jit(solution)/shard_map/ppermute | solution.py:435
  68.1 9.5 %collective-permute-start.8 = (f32[4,16,128]{2,1,0:T(8,128)S(1)}, f32[4,16,128]{2,1,0:T(8,128)S(1)}, u32[]{:S(2)}, u32[]{:S(2)}) collective-permute-start(f32[4,16,128]{2,1,0:T(8,128)S(1)} %get-tuple-element.23), channel_id=1, source_target_pairs={{0,911},{1,0},{2,1},{3,2},{4,3},{5,4},{6,5},{7,6},{8,7},{9,8},{10,... | collective-permute-start | bytes 98312 | tf_op jit(solution)/shard_map/ppermute | solution.py:435
  78.2 3.6 %collective-permute-start.9 = (f32[16,8,128]{2,1,0:T(8,128)S(1)}, f32[16,8,128]{2,1,0:T(8,128)S(1)}, u32[]{:S(2)}, u32[]{:S(2)}) collective-permute-start(f32[16,8,128]{2,1,0:T(8,128)S(1)} %get-tuple-element.24), channel_id=1, source_target_pairs={{0,112},{1,113},{2,114},{3,115},{4,116},{5,117},{6,118},{7,119},{8... | collective-permute-start | bytes 196616 | tf_op jit(solution)/shard_map/ppermute | solution.py:435
  79.1 4.9 %collective-permute-start.10 = (f32[16,8,128]{2,1,0:T(8,128)S(1)}, f32[16,8,128]{2,1,0:T(8,128)S(1)}, u32[]{:S(2)}, u32[]{:S(2)}) collective-permute-start(f32[16,8,128]{2,1,0:T(8,128)S(1)} %get-tuple-element.25), channel_id=1, source_target_pairs={{0,16},{1,17},{2,18},{3,19},{4,20},{5,21},{6,22},{7,23},{8,24},{9,... | collective-permute-start | bytes 196616 | tf_op jit(solution)/shard_map/ppermute | solution.py:435

commit v8 on v7

--- a/solution.py
+++ b/solution.py
@@ -52,7 +52,7 @@
     return (c_ref, field) if field < 3 else (v_ref, field - 3)
 
 
-def pack_x(place_ref, c_ref, v_ref, ac_ref, av_ref, b_ref, edge_ref):
+def pack_x(place_ref, c_ref, v_ref, ac_ref, av_ref, b_ref, edge_ref, c_out, v_out):
     high = 4 * place_ref[0]
     low = 4 - high
     shift = 4 * place_ref[1]
@@ -63,6 +63,8 @@
             to, j = field_of(ac_ref, av_ref, field)
             to[4 * j + q] = ref[i, high + q]
             b_ref[field, q] = ref[i, low + q]
+            kept = c_out if field < 3 else v_out
+            kept[i, q], kept[i, 4 + q] = ref[i, q], ref[i, 4 + q]
         lane = lanes_of((16, 128))
         edge = jnp.zeros((16, 128), jnp.float32)
         for g in (1, 2):
@@ -233,30 +235,35 @@
     loop(0, 3, lambda tile: body(pl.ds(pl.multiple_of(8 * tile, 8), 8)))
 
 
-def main_along_x(from_ref, m_ref, x_ref, base, count):
-    sources = [get(from_ref, i) for i in range(3)]
+def main_along_x(t_ref, v_ref, x_ref, stage, base, count):
+    sources = [get(t_ref, stage, i) for i in range(3)]
     stores = [put(x_ref, i) for i in range(3)]
-    over_tiles(lambda rows: along_x(sources, get(m_ref, 3), stores, rows, base, count))
-
-
-def main_along_yz(m_ref, x_ref, s_ref, slot, rows):
-    w = weights(m_ref[4, slot])
-    cs = [spread(x_ref[i, slot], w, 0)[0:rows] for i in range(3)]
-    w = weights(m_ref[5, slot, 0:rows])
+    over_tiles(lambda rows: along_x(sources, get(v_ref, 0), stores, rows, base, count))
+
+
+def main_along_yz(t_ref, v_ref, x_ref, s_ref, stage, slot):
+    w = weights(v_ref[1, slot])
+    cs = [spread(x_ref[i, slot], w, 0) for i in range(3)]
+    w = weights(v_ref[2, slot])
     cs = [spread(c, w, 1) for c in cs]
-    return [c + HALF * sum(cs[j] * s_ref[j, i, slot, 0:rows] for j in range(3)) for i, c in enumerate(cs)]
-
-
-def main_slopes(m_ref, s_ref, slot):
+    for i, c in enumerate(cs):
+        t_ref[stage + 1, i, slot] = c + HALF * sum(cs[j] * s_ref[j, i, slot] for j in range(3))
+
+
+def main_slopes(v_ref, s_ref, slot):
     for i in range(3):
-        v = m_ref[3 + i, slot]
-        s_ref[0, i, slot] = slope_of(*[m_ref[3 + i, slot + k] for k in (-2, -1, 1, 2)])
+        v = v_ref[i, slot]
+        s_ref[0, i, slot] = slope_of(*[v_ref[i, slot + k] for k in (-2, -1, 1, 2)])
         s_ref[1, i, slot] = slope_roll(v, 0)
         s_ref[2, i, slot] = slope_roll(v, 1)
 
 
+def widened(t_ref, w_ref, field):
+    return (t_ref, (0, field)) if field < 3 else (w_ref, (field - 3,))
+
+
 def compute_early(
-    place_ref, c_ref, v_ref, b_ref, above_ref, below_ref, m_ref, n_ref, s_ref, o_ref, x_ref
+    place_ref, c_ref, v_ref, b_ref, above_ref, below_ref, t_ref, w_ref, s_ref, x_ref
 ):
     odd = place_ref[0]
     side = 12 - 12 * odd
@@ -265,57 +272,56 @@
     def own(q):
         for field in range(6):
             ref, i = field_of(c_ref, v_ref, field)
-            m_ref[field, 4 + q, 0:16] = ref[i, q]
-            m_ref[field, 8 + q, 0:16] = ref[i, 4 + q]
-            m_ref[field, 4 + q, 16:24], m_ref[field, 8 + q, 16:24] = halo(
-                above_ref, below_ref, 6 * field + q
-            )
+            to, at = widened(t_ref, w_ref, field)
+            to[(*at, 4 + q, slice(0, 16))] = ref[i, q]
+            to[(*at, 8 + q, slice(0, 16))] = ref[i, 4 + q]
+            near, far = halo(above_ref, below_ref, 6 * field + q)
+            to[(*at, 4 + q, slice(16, 24))] = near
+            to[(*at, 8 + q, slice(16, 24))] = far
 
     def beyond(q):
         for field in range(6):
-            m_ref[field, side + q, 0:16] = b_ref[field, q]
-            m_ref[field, side + 2 + q, 0:16] = b_ref[field, 2 + q]
-            m_ref[field, side + q, 16:24], m_ref[field, side + 2 + q, 16:24] = halo(
-                above_ref, below_ref, 6 * field + 4 + q
-            )
+            to, at = widened(t_ref, w_ref, field)
+            to[(*at, side + q, slice(0, 16))] = b_ref[field, q]
+            to[(*at, side + 2 + q, slice(0, 16))] = b_ref[field, 2 + q]
+            near, far = halo(above_ref, below_ref, 6 * field + 4 + q)
+            to[(*at, side + q, slice(16, 24))] = near
+            to[(*at, side + 2 + q, slice(16, 24))] = far
 
     loop(0, 4, own)
     loop(0, 2, beyond)
-    loop(0, 8, lambda k: main_slopes(m_ref, s_ref, first + 2 + k), 2)
-    main_along_x(m_ref, m_ref, x_ref, first + 2, 8)
-
-    def substep_one(k):
-        slot = first + 2 + k
-        for i, value in enumerate(main_along_yz(m_ref, x_ref, s_ref, slot, 24)):
-            n_ref[i, slot] = value
-
-    def substep_two(k):
-        slot = first + 4 + k
-        for i, value in enumerate(main_along_yz(m_ref, x_ref, s_ref, slot, 16)):
-            o_ref[i, slot - 4] = value
-
-    loop(0, 8, substep_one, 2)
-    main_along_x(n_ref, m_ref, x_ref, first + 4, 4)
-    loop(0, 4, substep_two, 2)
+    loop(0, 8, lambda k: main_slopes(w_ref, s_ref, first + 2 + k))
+
+    def substep(n):
+        main_along_x(t_ref, w_ref, x_ref, n, first + 2, 8)
+
+        def pair(k):
+            for j in range(2):
+                main_along_yz(t_ref, w_ref, x_ref, s_ref, n, first + 2 + 2 * n + 2 * k + j)
+
+        loop(0, 4 - 2 * n, pair)
+
+    loop(0, 2, substep)
 
 
 def compute_late(
-    place_ref, ac_ref, av_ref, zl_ref, zr_ref, above_ref, below_ref, m_in, n_in, s_in, o_in,
-    m_ref, n_ref, s_ref, o_ref, out_ref, x_ref, ec_ref, ev_ref, ed_ref, ex_ref, es_ref,
+    place_ref, ac_ref, av_ref, zl_ref, zr_ref, above_ref, below_ref, t_in, w_in, s_in,
+    t_ref, w_ref, s_ref, out_ref, x_ref, ec_ref, ev_ref, ed_ref, ex_ref, es_ref,
 ):
     odd = place_ref[0]
     side = 12 * odd
     first = 2 + 8 * odd
-    second = 4 + 4 * odd
+    step = 2 - 4 * odd
 
     def beyond(q):
         for field in range(6):
             ref, i = field_of(ac_ref, av_ref, field)
-            m_ref[field, side + q, 0:16] = ref[4 * i + q]
-            m_ref[field, side + 2 + q, 0:16] = ref[4 * i + 2 + q]
-            m_ref[field, side + q, 16:24], m_ref[field, side + 2 + q, 16:24] = halo(
-                above_ref, below_ref, 2 * field + q
-            )
+            to, at = widened(t_ref, w_ref, field)
+            to[(*at, side + q, slice(0, 16))] = ref[4 * i + q]
+            to[(*at, side + 2 + q, slice(0, 16))] = ref[4 * i + 2 + q]
+            near, far = halo(above_ref, below_ref, 2 * field + q)
+            to[(*at, side + q, slice(16, 24))] = near
+            to[(*at, side + 2 + q, slice(16, 24))] = far
 
     loop(0, 2, beyond)
 
@@ -332,7 +338,8 @@
             for i in range(3):
                 field = 3 * kind + i
                 at = 32 * i
-                x = m_ref[field, s]
+                source, where = widened(t_ref, w_ref, field)
+                x = source[(*where, s)]
                 e = jnp.where(between(lane, at, at + 4), roll(zl, at - 4 * field, 1), e)
                 e = jnp.where(between(lane, at + 4, at + 16), roll(x, at + 4, 1), e)
                 e = jnp.where(between(lane, at + 16, at + 28), roll(x, at + 28, 1), e)
@@ -342,7 +349,7 @@
             ed_ref[k, s] = d
 
     loop(0, 16, edges, 2)
-    loop(0, 4, lambda k: main_slopes(m_ref, s_ref, first + k), 2)
+    loop(0, 4, lambda k: main_slopes(w_ref, s_ref, first + k))
 
     def edge_slopes(s):
         v = ev_ref[s]
@@ -360,34 +367,35 @@
 
     def edge_substep(n):
         over_tiles(lambda rows: along_x([get(ec_ref)], get(ed_ref, 0), [put(ex_ref)], rows, 2, 12))
-        loop(2, 14, edge_along_yz, 4)
+
+        def four(k):
+            for j in range(4):
+                edge_along_yz(2 + 2 * n + 4 * k + j)
+
+        loop(0, 3 - n, four)
 
     loop(0, 2, edge_substep)
 
-    main_along_x(m_ref, m_ref, x_ref, first, 4)
-
-    def substep_one(k):
-        slot = first + k
-        for i, value in enumerate(main_along_yz(m_ref, x_ref, s_ref, slot, 24)):
-            n_ref[i, slot] = value
-
-    def substep_two(k):
-        slot = second + k
-        for i, value in enumerate(main_along_yz(m_ref, x_ref, s_ref, slot, 16)):
-            o_ref[i, slot - 4] = value
-
-    loop(0, 4, substep_one, 2)
-    main_along_x(n_ref, m_ref, x_ref, second, 4)
-    loop(0, 4, substep_two, 2)
+    def substep(n):
+        base = first + step * n
+        main_along_x(t_ref, w_ref, x_ref, n, base, 4)
+
+        def pair(k):
+            for j in range(2):
+                main_along_yz(t_ref, w_ref, x_ref, s_ref, n, base + 2 * k + j)
+
+        loop(0, 2, pair)
+
+    loop(0, 2, substep)
 
     def finish(s):
         lane = lanes_of((16, 128))
         e = ec_ref[s + 4, 0:16]
         for i in range(3):
-            value = jnp.where(lane < 4, roll(e, -(32 * i + 4), 1), o_ref[i, s])
+            value = jnp.where(lane < 4, roll(e, -(32 * i + 4), 1), t_ref[2, i, s + 4, 0:16])
             out_ref[i, s] = jnp.where(lane >= 124, roll(e, 100 - 32 * i, 1), value)
 
-    loop(0, 8, finish, 2)
+    loop(0, 8, finish)
 
 
 def call(kernel, outs, scratch=(), operands=0, aliases=()):
@@ -441,7 +449,9 @@
         far = (x % 4 == 0) | (x % 4 == 3)
         layers = (6, 4, 16, 128)
         edge = (4, 16, 128)
-        ac, av, b, _ = call(pack_x, [(14, 16, 128), (12, 16, 128), layers, edge], (), 2)(place, c, v)
+        block = (3, 8, 16, 128)
+        shapes = [(14, 16, 128), (12, 16, 128), layers, edge, block, block]
+        ac, av, b, _, c, v = call(pack_x, shapes, (), 2)(place, c, v)
         own_end = ac[12:]
         passed = send(av, aside)
         ac = send(ac, across)
@@ -464,14 +474,15 @@
         above = send(down, y_down)
         below = send(up, y_up)
         block = (16, 24, 128)
-        state = [(6, *block), (3, *block), (3, 3, *block), (3, 8, 16, 128)]
-        m, n, s, o = call(compute_early, state, [(3, *block)], 5)(
+        state = [(3, 3, *block), (3, *block), (3, 3, *block)]
+        state = call(compute_early, state, [(3, *block)], 5)(
             place, c, v, b, early_above, early_below
         )
         scratch = [(3, *block), block, block, (3, *block), block, (3, *block)]
-        *_, out = call(
-            compute_late, state + [(3, 8, 16, 128)], scratch, 10, {7 + k: k for k in range(4)}
-        )(place, ac, av, zl, zr, above, below, m, n, s, o)
+        shapes = [a.shape for a in state] + [(3, 8, 16, 128)]
+        *_, out = call(compute_late, shapes, scratch, 9, {7 + k: k for k in range(3)})(
+            place, ac, av, zl, zr, above, below, *state
+        )
         return out
 
     placed = P(None, *AXES)

time: 93.5 us -> 94 us (level)
  the two profiles are of different devices: /device:TPU:6 before, /device:TPU:1 now
where the time goes in v8:
time: 94 us; the launch traced here: 93.7 us
  starting transfers between devices  73.2 us (78%)
  Pallas kernels  15.1 us (16%)
  waiting for transfers between devices  3.15 us (3%)
  local copies, waits for them, and re-layouts  1.87 us (2%)
    ppermute x13, starting transfers between devices, send(): return lax.ppermute(value, AXES, pairs)  73.2 us
    pallas_call x1, Pallas kernels, local(): call(compute_late, shapes, scratch, 9, {7 + k: k for k in range(3)})  7.82 us
    ppermute x13, waiting for transfers between devices, send(): return lax.ppermute(value, AXES, pairs)  3.15 us
    pallas_call x1, Pallas kernels, local(): call(compute_early, state, [(3, *block)], 5)  3.03 us
  transfers between devices with their start and end apart: 13, of which 2 were waited for; matrix products, arithmetic and copies ran while one was open for 0% of the time, Pallas kernels for 6%

profile of v8, /device:TPU:1, one launch (start us, length us, event | category | flops | bytes accessed | tf_op | source)
XLA Modules:
  0.0 93.7 jit_solution(12338398552873651534)
XLA Ops:
  0.0 0.1 pad_add_fusion.place_ref
  0.1 0.0 copy-start
  0.1 0.9 copy-done
  1.0 0.0 copy-start.1
  1.0 0.9 copy-done.1
  1.9 1.6 %shard_map.28 = (f32[14,16,128]{2,1,0:T(8,128)S(1)}, f32[12,16,128]{2,1,0:T(8,128)S(1)}, f32[6,4,16,128]{3,2,1,0:T(8,128)S(1)}, f32[4,16,128]{2,1,0:T(8,128)}, f...) custom-call(s32[4]{0:T(128)S(1)} %pad_add_fusion.place_ref, f32[3,8,16,128]{3,2,1,0:T(8,128)S(1)} %copy-done, ...), custom_call_target="tpu_custom_call" | custom-call | tf_op jit(solution)/shard_map/pallas_call | solution.py:454
  3.5 3.9 %collective-permute-start.1 = (f32[12,16,128]{2,1,0:T(8,128)S(1)}, f32[12,16,128]{2,1,0:T(8,128)S(1)}, u32[]{:S(2)}, u32[]{:S(2)}) collective-permute-start(f32[12,16,128]{2,1,0:T(8,128)S(1)} %get-tuple-element.21), channel_id=1, source_target_pairs={{0,128},{1,129},{2,130},{3,131},{4,132},{5,133},{6,134},{7,135},{8... | collective-permute-start | bytes 294920 | tf_op jit(solution)/shard_map/ppermute | solution.py:443
  7.4 1.9 %collective-permute-start.5 = (f32[6,4,16,128]{3,2,1,0:T(8,128)S(1)}, f32[6,4,16,128]{3,2,1,0:T(8,128)S(1)}, u32[]{:S(2)}, u32[]{:S(2)}) collective-permute-start(f32[6,4,16,128]{3,2,1,0:T(8,128)S(1)} %get-tuple-element.24), channel_id=1, source_target_pairs={{0,128},{1,129},{2,130},{3,131},{4,132},{5,133},{6,134},{7,135},{8... | collective-permute-start | bytes 589832 | tf_op jit(solution)/shard_map/ppermute | solution.py:443
  9.4 0.0 collective-permute-done.1
  9.4 0.7 collective-permute-start.2
  10.1 30.2 %collective-permute-start = (f32[14,16,128]{2,1,0:T(8,128)S(1)}, f32[14,16,128]{2,1,0:T(8,128)S(1)}, u32[]{:S(2)}, u32[]{:S(2)}) collective-permute-start(f32[14,16,128]{2,1,0:T(8,128)S(1)} %get-tuple-element.20), channel_id=1, source_target_pairs={{0,896},{1,897},{2,898},{3,899},{4,900},{5,901},{6,902},{7,903},{8... | collective-permute-start | bytes 344072 | tf_op jit(solution)/shard_map/ppermute | solution.py:443
  40.3 0.7 collective-permute-start.4
  41.0 0.0 collective-permute-done.5.b_ref
  41.0 0.8 shard_map.31
  41.8 1.7 %collective-permute-start.11 = (f32[36,8,128]{2,1,0:T(8,128)S(1)}, f32[36,8,128]{2,1,0:T(8,128)S(1)}, u32[]{:S(2)}, u32[]{:S(2)}) collective-permute-start(f32[36,8,128]{2,1,0:T(8,128)S(1)} %get-tuple-element.29), channel_id=1, source_target_pairs={{0,112},{1,113},{2,114},{3,115},{4,116},{5,117},{6,118},{7,119},{8... | collective-permute-start | bytes 442376 | tf_op jit(solution)/shard_map/ppermute | solution.py:443
  43.5 1.2 %collective-permute-start.12 = (f32[36,8,128]{2,1,0:T(8,128)S(1)}, f32[36,8,128]{2,1,0:T(8,128)S(1)}, u32[]{:S(2)}, u32[]{:S(2)}) collective-permute-start(f32[36,8,128]{2,1,0:T(8,128)S(1)} %get-tuple-element.30), channel_id=1, source_target_pairs={{0,16},{1,17},{2,18},{3,19},{4,20},{5,21},{6,22},{7,23},{8,24},{9,... | collective-permute-start | bytes 442376 | tf_op jit(solution)/shard_map/ppermute | solution.py:443
  44.7 0.0 collective-permute-done.2
  44.7 0.7 collective-permute-start.6
  45.3 0.0 collective-permute-done.ac_ref
  45.4 9.5 %collective-permute-start.3 = (f32[14,16,128]{2,1,0:T(8,128)S(1)}, f32[14,16,128]{2,1,0:T(8,128)S(1)}, u32[]{:S(2)}, u32[]{:S(2)}) collective-permute-start(f32[14,16,128]{2,1,0:T(8,128)S(1)} %broadcast_select_fusion), channel_id=1, source_target_pairs={{0,128},{1,129},{2,130},{3,131},{4,132},{5,133},{6,134},{7,135},{8... | collective-permute-start | bytes 344072 | tf_op jit(solution)/shard_map/ppermute | solution.py:443
  54.9 0.0 collective-permute-done.6
  54.9 0.0 collective-permute-done.4
  54.9 2.1 %collective-permute-done.3 = f32[14,16,128]{2,1,0:T(8,128)S(1)} collective-permute-done((f32[14,16,128]{2,1,0:T(8,128)S(1)}, f32[14,16,128]{2,1,0:T(8,128)S(1)}, u32[]{:S(2)}, u32[]{:S(2)}) %collective-permute-start.3) | collective-permute-done | bytes 114720 | tf_op jit(solution)/shard_map/ppermute | solution.py:443
  57.1 1.3 %shard_map.29 = (f32[4,16,128]{2,1,0:T(8,128)S(1)}, f32[4,16,128]{2,1,0:T(8,128)S(1)}) custom-call(s32[4]{0:T(128)S(1)} %pad_add_fusion.place_ref, f32[3,8,16,128]{3,2,1,0:T(8,128)S(1)} %get-tuple-element.22.c_ref, f32[3,8,16,128]{3,2,1,0:T(8,128)S(1)} %get-tuple-element.23.v_ref, f32[14,16,128]{2,1,0:T(8,128)S(1)} %collective-permute-done.ac_ref, ...), custom_call_target="tpu_custom_call" | custom-call | tf_op jit(solution)/shard_map/pallas_call | solution.py:468
  58.4 7.2 %collective-permute-start.7 = (f32[4,16,128]{2,1,0:T(8,128)S(1)}, f32[4,16,128]{2,1,0:T(8,128)S(1)}, u32[]{:S(2)}, u32[]{:S(2)}) collective-permute-start(f32[4,16,128]{2,1,0:T(8,128)S(1)} %get-tuple-element.25), channel_id=1, source_target_pairs={{0,1},{1,2},{2,3},{3,4},{4,5},{5,6},{6,7},{7,8},{8,9},{9,10},{10,1... | collective-permute-start | bytes 98312 | tf_op jit(solution)/shard_map/ppermute | solution.py:443
  65.6 11.6 %collective-permute-start.8 = (f32[4,16,128]{2,1,0:T(8,128)S(1)}, f32[4,16,128]{2,1,0:T(8,128)S(1)}, u32[]{:S(2)}, u32[]{:S(2)}) collective-permute-start(f32[4,16,128]{2,1,0:T(8,128)S(1)} %get-tuple-element.26), channel_id=1, source_target_pairs={{0,911},{1,0},{2,1},{3,2},{4,3},{5,4},{6,5},{7,6},{8,7},{9,8},{10,... | collective-permute-start | bytes 98312 | tf_op jit(solution)/shard_map/ppermute | solution.py:443
  77.2 0.0 collective-permute-done.7.zl_ref
  77.2 1.0 %collective-permute-done.8.zr_ref = f32[4,16,128]{2,1,0:T(8,128)S(1)} collective-permute-done((f32[4,16,128]{2,1,0:T(8,128)S(1)}, f32[4,16,128]{2,1,0:T(8,128)S(1)}, u32[]{:S(2)}, u32[]{:S(2)}) %collective-permute-start.8) | collective-permute-done | bytes 32800 | tf_op jit(solution)/shard_map/ppermute | solution.py:443
  78.2 0.6 shard_map.30
  78.8 2.8 %collective-permute-start.9 = (f32[16,8,128]{2,1,0:T(8,128)S(1)}, f32[16,8,128]{2,1,0:T(8,128)S(1)}, u32[]{:S(2)}, u32[]{:S(2)}) collective-permute-start(f32[16,8,128]{2,1,0:T(8,128)S(1)} %get-tuple-element.27), channel_id=1, source_target_pairs={{0,112},{1,113},{2,114},{3,115},{4,116},{5,117},{6,118},{7,119},{8... | collective-permute-start | bytes 196616 | tf_op jit(solution)/shard_map/ppermute | solution.py:443
  81.6 1.2 %collective-permute-start.10 = (f32[16,8,128]{2,1,0:T(8,128)S(1)}, f32[16,8,128]{2,1,0:T(8,128)S(1)}, u32[]{:S(2)}, u32[]{:S(2)}) collective-permute-start(f32[16,8,128]{2,1,0:T(8,128)S(1)} %get-tuple-element.28), channel_id=1, source_target_pairs={{0,16},{1,17},{2,18},{3,19},{4,20},{5,21},{6,22},{7,23},{8,24},{9,... | collective-permute-start | bytes 196616 | tf_op jit(solution)/shard_map/ppermute | solution.py:443
  82.8 0.0 collective-permute-done.11.above_ref
  82.8 0.0 collective-permute-done.12.below_ref
  82.8 3.0 %shard_map.32 = (f32[3,3,16,24,128]{4,3,2,1,0:T(8,128)S(1)}, f32[3,16,24,128]{3,2,1,0:T(8,128)S(1)}, f32[3,3,16,24,128]{4,3,2,1,0:T(8,128)S(1)}) custom-call(s32[4]{0:T(128)S(1)} %pad_add_fusion.place_ref, f32[3,8,16,128]{3,2,1,0:T(8,128)S(1)} %get-tuple-element.22.c_ref, f32[3,8,16,128]{3,2,1,0:T(8,128)S(1)} %get-tuple-element.23.v_ref, ...), custom_call_target="tpu_custom_call" | custom-call | tf_op jit(solution)/shard_map/pallas_call | solution.py:478
  85.8 0.0 collective-permute-done.9.above_ref
  85.8 0.0 collective-permute-done.10.below_ref
  85.9 7.8 %shard_map.33 = (f32[3,3,16,24,128]{4,3,2,1,0:T(8,128)S(1)}, f32[3,16,24,128]{3,2,1,0:T(8,128)S(1)}, f32[3,3,16,24,128]{4,3,2,1,0:T(8,128)S(1)}, f32[3,8,16,128]{3,2,1,0:T(8,128)}) custom-call(s32[4]{0:T(128)S(1)} %pad_add_fusion.place_ref, ...), custom_call_target="tpu_custom_call", output_to_operand_aliasing={{0}: (7, {}), {1}: (8, {}), {2}: (9, {})} | custom-call | tf_op jit(solution)/shard_map/pallas_call | solution.py:483
  (8 shorter events, 0.1 us)
Async XLA Ops:
  0.1 0.9 copy-start
  1.0 0.9 copy-start.1
  3.5 5.9 %collective-permute-start.1 = (f32[12,16,128]{2,1,0:T(8,128)S(1)}, f32[12,16,128]{2,1,0:T(8,128)S(1)}, u32[]{:S(2)}, u32[]{:S(2)}) collective-permute-start(f32[12,16,128]{2,1,0:T(8,128)S(1)} %get-tuple-element.21), channel_id=1, source_target_pairs={{0,128},{1,129},{2,130},{3,131},{4,132},{5,133},{6,134},{7,135},{8... | collective-permute-start | bytes 294920 | tf_op jit(solution)/shard_map/ppermute | solution.py:443
  7.4 33.6 %collective-permute-start.5 = (f32[6,4,16,128]{3,2,1,0:T(8,128)S(1)}, f32[6,4,16,128]{3,2,1,0:T(8,128)S(1)}, u32[]{:S(2)}, u32[]{:S(2)}) collective-permute-start(f32[6,4,16,128]{3,2,1,0:T(8,128)S(1)} %get-tuple-element.24), channel_id=1, source_target_pairs={{0,128},{1,129},{2,130},{3,131},{4,132},{5,133},{6,134},{7,135},{8... | collective-permute-start | bytes 589832 | tf_op jit(solution)/shard_map/ppermute | solution.py:443
  9.4 35.3 %collective-permute-start.2 = (f32[14,16,128]{2,1,0:T(8,128)S(1)}, f32[14,16,128]{2,1,0:T(8,128)S(1)}, u32[]{:S(2)}, u32[]{:S(2)}) collective-permute-start(f32[14,16,128]{2,1,0:T(8,128)S(1)} %pad_maximum_fusion), channel_id=1, source_target_pairs={{128,768},{129,769},{130,770},{131,771},{132,772},{133,773},{134,7... | collective-permute-start | bytes 344072 | tf_op jit(solution)/shard_map/ppermute | solution.py:443
  10.1 35.3 %collective-permute-start = (f32[14,16,128]{2,1,0:T(8,128)S(1)}, f32[14,16,128]{2,1,0:T(8,128)S(1)}, u32[]{:S(2)}, u32[]{:S(2)}) collective-permute-start(f32[14,16,128]{2,1,0:T(8,128)S(1)} %get-tuple-element.20), channel_id=1, source_target_pairs={{0,896},{1,897},{2,898},{3,899},{4,900},{5,901},{6,902},{7,903},{8... | collective-permute-start | bytes 344072 | tf_op jit(solution)/shard_map/ppermute | solution.py:443
  40.3 14.6 %collective-permute-start.4 = (f32[12,16,128]{2,1,0:T(8,128)S(1)}, f32[12,16,128]{2,1,0:T(8,128)S(1)}, u32[]{:S(2)}, u32[]{:S(2)}) collective-permute-start(f32[12,16,128]{2,1,0:T(8,128)S(1)} %get-tuple-element.21), channel_id=1, source_target_pairs={{128,256},{129,257},{130,258},{131,259},{132,260},{133,261},{134,2... | collective-permute-start | bytes 294920 | tf_op jit(solution)/shard_map/ppermute | solution.py:443
  41.8 41.0 %collective-permute-start.11 = (f32[36,8,128]{2,1,0:T(8,128)S(1)}, f32[36,8,128]{2,1,0:T(8,128)S(1)}, u32[]{:S(2)}, u32[]{:S(2)}) collective-permute-start(f32[36,8,128]{2,1,0:T(8,128)S(1)} %get-tuple-element.29), channel_id=1, source_target_pairs={{0,112},{1,113},{2,114},{3,115},{4,116},{5,117},{6,118},{7,119},{8... | collective-permute-start | bytes 442376 | tf_op jit(solution)/shard_map/ppermute | solution.py:443
  43.5 39.3 %collective-permute-start.12 = (f32[36,8,128]{2,1,0:T(8,128)S(1)}, f32[36,8,128]{2,1,0:T(8,128)S(1)}, u32[]{:S(2)}, u32[]{:S(2)}) collective-permute-start(f32[36,8,128]{2,1,0:T(8,128)S(1)} %get-tuple-element.30), channel_id=1, source_target_pairs={{0,16},{1,17},{2,18},{3,19},{4,20},{5,21},{6,22},{7,23},{8,24},{9,... | collective-permute-start | bytes 442376 | tf_op jit(solution)/shard_map/ppermute | solution.py:443
  44.7 10.2 %collective-permute-start.6 = (f32[2,16,128]{2,1,0:T(8,128)S(1)}, f32[2,16,128]{2,1,0:T(8,128)S(1)}, u32[]{:S(2)}, u32[]{:S(2)}) collective-permute-start(f32[2,16,128]{2,1,0:T(8,128)S(1)} %slice.22), channel_id=1, source_target_pairs={{128,256},{129,257},{130,258},{131,259},{132,260},{133,261},{134,2... | collective-permute-start | bytes 49160 | tf_op jit(solution)/shard_map/ppermute | solution.py:443
  45.4 11.7 %collective-permute-start.3 = (f32[14,16,128]{2,1,0:T(8,128)S(1)}, f32[14,16,128]{2,1,0:T(8,128)S(1)}, u32[]{:S(2)}, u32[]{:S(2)}) collective-permute-start(f32[14,16,128]{2,1,0:T(8,128)S(1)} %broadcast_select_fusion), channel_id=1, source_target_pairs={{0,128},{1,129},{2,130},{3,131},{4,132},{5,133},{6,134},{7,135},{8... | collective-permute-start | bytes 344072 | tf_op jit(solution)/shard_map/ppermute | solution.py:443
  58.4 18.8 %collective-permute-start.7 = (f32[4,16,128]{2,1,0:T(8,128)S(1)}, f32[4,16,128]{2,1,0:T(8,128)S(1)}, u32[]{:S(2)}, u32[]{:S(2)}) collective-permute-start(f32[4,16,128]{2,1,0:T(8,128)S(1)} %get-tuple-element.25), channel_id=1, source_target_pairs={{0,1},{1,2},{2,3},{3,4},{4,5},{5,6},{6,7},{7,8},{8,9},{9,10},{10,1... | collective-permute-start | bytes 98312 | tf_op jit(solution)/shard_map/ppermute | solution.py:443
  65.6 12.6 %collective-permute-start.8 = (f32[4,16,128]{2,1,0:T(8,128)S(1)}, f32[4,16,128]{2,1,0:T(8,128)S(1)}, u32[]{:S(2)}, u32[]{:S(2)}) collective-permute-start(f32[4,16,128]{2,1,0:T(8,128)S(1)} %get-tuple-element.26), channel_id=1, source_target_pairs={{0,911},{1,0},{2,1},{3,2},{4,3},{5,4},{6,5},{7,6},{8,7},{9,8},{10,... | collective-permute-start | bytes 98312 | tf_op jit(solution)/shard_map/ppermute | solution.py:443
  78.8 7.1 %collective-permute-start.9 = (f32[16,8,128]{2,1,0:T(8,128)S(1)}, f32[16,8,128]{2,1,0:T(8,128)S(1)}, u32[]{:S(2)}, u32[]{:S(2)}) collective-permute-start(f32[16,8,128]{2,1,0:T(8,128)S(1)} %get-tuple-element.27), channel_id=1, source_target_pairs={{0,112},{1,113},{2,114},{3,115},{4,116},{5,117},{6,118},{7,119},{8... | collective-permute-start | bytes 196616 | tf_op jit(solution)/shard_map/ppermute | solution.py:443
  81.6 4.3 %collective-permute-start.10 = (f32[16,8,128]{2,1,0:T(8,128)S(1)}, f32[16,8,128]{2,1,0:T(8,128)S(1)}, u32[]{:S(2)}, u32[]{:S(2)}) collective-permute-start(f32[16,8,128]{2,1,0:T(8,128)S(1)} %get-tuple-element.28), channel_id=1, source_target_pairs={{0,16},{1,17},{2,18},{3,19},{4,20},{5,21},{6,22},{7,23},{8,24},{9,... | collective-permute-start | bytes 196616 | tf_op jit(solution)/shard_map/ppermute | solution.py:443

commit v9 on v8

--- a/solution.py
+++ b/solution.py
@@ -52,7 +52,15 @@
     return (c_ref, field) if field < 3 else (v_ref, field - 3)
 
 
-def pack_x(place_ref, c_ref, v_ref, ac_ref, av_ref, b_ref, edge_ref, c_out, v_out):
+def pack_aside(place_ref, v_ref, av_ref, v_out):
+    high = 4 * place_ref[0]
+    for i in range(3):
+        for q in range(4):
+            av_ref[4 * i + q] = v_ref[i, high + q]
+    v_out[...] = v_ref[...]
+
+
+def pack_x(place_ref, c_ref, v_ref, ac_ref, b_ref, edge_ref, c_out):
     high = 4 * place_ref[0]
     low = 4 - high
     shift = 4 * place_ref[1]
@@ -60,11 +68,10 @@
     def copy(q):
         for field in range(6):
             ref, i = field_of(c_ref, v_ref, field)
-            to, j = field_of(ac_ref, av_ref, field)
-            to[4 * j + q] = ref[i, high + q]
+            if field < 3:
+                ac_ref[4 * field + q] = ref[i, high + q]
+                c_out[i, q], c_out[i, 4 + q] = ref[i, q], ref[i, 4 + q]
             b_ref[field, q] = ref[i, low + q]
-            kept = c_out if field < 3 else v_out
-            kept[i, q], kept[i, 4 + q] = ref[i, q], ref[i, 4 + q]
         lane = lanes_of((16, 128))
         edge = jnp.zeros((16, 128), jnp.float32)
         for g in (1, 2):
@@ -433,6 +440,10 @@
         mesh, lambda x, y, z: None if is_far(x) else (other_of(across_of(other_of(x))), y, z)
     )
     beside = flat_pairs(mesh, lambda x, y, z: None if is_far(x) else (across_of(x), y, z))
+    turn = flat_pairs(
+        mesh,
+        lambda x, y, z: None if is_far(x) or z not in (0, end) else (across_of(x), y, z),
+    )
     y_up = flat_pairs(mesh, lambda x, y, z: (x, y + 1, z))
     y_down = flat_pairs(mesh, lambda x, y, z: (x, y - 1, z))
     last_x = mesh.shape["gx"] - 1
@@ -450,10 +461,11 @@
         layers = (6, 4, 16, 128)
         edge = (4, 16, 128)
         block = (3, 8, 16, 128)
-        shapes = [(14, 16, 128), (12, 16, 128), layers, edge, block, block]
-        ac, av, b, _, c, v = call(pack_x, shapes, (), 2)(place, c, v)
+        av, v = call(pack_aside, [(12, 16, 128), block], (), 1)(place, v)
+        passed = send(av, aside)
+        shapes = [(14, 16, 128), layers, edge, block]
+        ac, b, _, c = call(pack_x, shapes, (), 2)(place, c, v)
         own_end = ac[12:]
-        passed = send(av, aside)
         ac = send(ac, across)
         passed = send(jnp.concatenate([passed, own_end]), relay)
         near_av = send(av, beside)
@@ -463,7 +475,7 @@
         early_below = send(up, y_up)
         held = jnp.where(far, ac, passed)
         forwarded = send(held, other)
-        end_a = jnp.where(far, own_end, send(passed[12:], beside))
+        end_a = jnp.where(far, own_end, send(passed[12:], turn))
         av = jnp.where(far, forwarded[:12], near_av)
         left, right = call(pack_z, [edge, edge], (), 8)(
             place, c, v, ac, av, b, held[12:], end_a, forwarded[12:]

time: 94 us -> 94.3 us (level)
  the two profiles are of different devices: /device:TPU:1 before, /device:TPU:6 now
where the time goes in v9:
time: 94.3 us; the launch traced here: 92.5 us
  starting transfers between devices  66.4 us (70%)
  Pallas kernels  15.7 us (17%)
  waiting for transfers between devices  8.26 us (9%)
  local copies, waits for them, and re-layouts  1.86 us (2%)
    ppermute x13, starting transfers between devices, send(): return lax.ppermute(value, AXES, pairs)  66.4 us
    ppermute x13, waiting for transfers between devices, send(): return lax.ppermute(value, AXES, pairs)  8.26 us
    pallas_call x1, Pallas kernels, local(): call(compute_late, shapes, scratch, 9, {7 + k: k for k in range(3)})  7.82 us
    pallas_call x1, Pallas kernels, local(): call(compute_early, state, [(3, *block)], 5)  3.04 us
  transfers between devices with their start and end apart: 13, of which 4 were waited for; matrix products, arithmetic and copies ran while one was open for 0% of the time, Pallas kernels for 8%

profile of v9, /device:TPU:6, one launch (start us, length us, event | category | flops | bytes accessed | tf_op | source)
XLA Modules:
  0.0 92.5 jit_solution(5783166891675897623)
XLA Ops:
  0.0 0.1 pad_add_fusion.place_ref
  0.1 0.0 copy-start
  0.1 0.9 %copy-done = f32[3,8,16,128]{3,2,1,0:T(8,128)S(1)} copy-done((f32[3,8,16,128]{3,2,1,0:T(8,128)S(1)}, f32[3,8,16,128]{3,2,1,0:T(8,128)}, u32[]{:S(2)}) %copy-start) | copy-done | bytes 196632
  1.0 0.6 shard_map.28
  1.6 2.7 %collective-permute-start.1 = (f32[12,16,128]{2,1,0:T(8,128)S(1)}, f32[12,16,128]{2,1,0:T(8,128)S(1)}, u32[]{:S(2)}, u32[]{:S(2)}) collective-permute-start(f32[12,16,128]{2,1,0:T(8,128)S(1)} %get-tuple-element.22), channel_id=1, source_target_pairs={{0,128},{1,129},{2,130},{3,131},{4,132},{5,133},{6,134},{7,135},{8... | collective-permute-start | bytes 294920 | tf_op jit(solution)/shard_map/ppermute | solution.py:454
  4.3 0.0 copy-start.1
  4.3 0.9 copy-done.1
  5.2 1.6 %shard_map.29 = (f32[14,16,128]{2,1,0:T(8,128)S(1)}, f32[6,4,16,128]{3,2,1,0:T(8,128)S(1)}, f32[4,16,128]{2,1,0:T(8,128)}, f32[3,8,16,128]{3,2,1,0:T(8,128)S(1)}) custom-call(s32[4]{0:T(128)S(1)} %pad_add_fusion.place_ref, f32[3,8,16,128]{3,2,1,0:T(8,128)S(1)} %copy-done.1, f32[3,8,16,128]{3,2,1,0:T(8,128)S(1)} %get-tuple-element.20.v_ref), custom_call_target="tpu_custom_call" | custom-call | tf_op jit(solution)/shard_map/pallas_call | solution.py:467
  6.8 1.9 %collective-permute-start.5 = (f32[6,4,16,128]{3,2,1,0:T(8,128)S(1)}, f32[6,4,16,128]{3,2,1,0:T(8,128)S(1)}, u32[]{:S(2)}, u32[]{:S(2)}) collective-permute-start(f32[6,4,16,128]{3,2,1,0:T(8,128)S(1)} %get-tuple-element.24), channel_id=1, source_target_pairs={{0,128},{1,129},{2,130},{3,131},{4,132},{5,133},{6,134},{7,135},{8... | collective-permute-start | bytes 589832 | tf_op jit(solution)/shard_map/ppermute | solution.py:454
  8.7 0.0 collective-permute-done.1
  8.8 0.7 collective-permute-start.2
  9.4 29.6 %collective-permute-start = (f32[14,16,128]{2,1,0:T(8,128)S(1)}, f32[14,16,128]{2,1,0:T(8,128)S(1)}, u32[]{:S(2)}, u32[]{:S(2)}) collective-permute-start(f32[14,16,128]{2,1,0:T(8,128)S(1)} %get-tuple-element.21), channel_id=1, source_target_pairs={{0,896},{1,897},{2,898},{3,899},{4,900},{5,901},{6,902},{7,903},{8... | collective-permute-start | bytes 344072 | tf_op jit(solution)/shard_map/ppermute | solution.py:454
  39.0 0.7 collective-permute-start.4
  39.7 0.0 collective-permute-done.5.b_ref
  39.7 0.8 shard_map.32
  40.5 1.9 %collective-permute-start.11 = (f32[36,8,128]{2,1,0:T(8,128)S(1)}, f32[36,8,128]{2,1,0:T(8,128)S(1)}, u32[]{:S(2)}, u32[]{:S(2)}) collective-permute-start(f32[36,8,128]{2,1,0:T(8,128)S(1)} %get-tuple-element.29), channel_id=1, source_target_pairs={{0,112},{1,113},{2,114},{3,115},{4,116},{5,117},{6,118},{7,119},{8... | collective-permute-start | bytes 442376 | tf_op jit(solution)/shard_map/ppermute | solution.py:454
  42.4 0.0 collective-permute-start.12
  42.4 0.0 collective-permute-done.2
  42.4 0.7 collective-permute-start.6
  43.1 2.1 %collective-permute-done.ac_ref = f32[14,16,128]{2,1,0:T(8,128)S(1)} collective-permute-done((f32[14,16,128]{2,1,0:T(8,128)S(1)}, f32[14,16,128]{2,1,0:T(8,128)S(1)}, u32[]{:S(2)}, u32[]{:S(2)}) %collective-permute-start) | collective-permute-done | bytes 114720 | tf_op jit(solution)/shard_map/ppermute | solution.py:454
  45.2 15.3 %collective-permute-start.3 = (f32[14,16,128]{2,1,0:T(8,128)S(1)}, f32[14,16,128]{2,1,0:T(8,128)S(1)}, u32[]{:S(2)}, u32[]{:S(2)}) collective-permute-start(f32[14,16,128]{2,1,0:T(8,128)S(1)} %broadcast_select_fusion), channel_id=1, source_target_pairs={{0,128},{1,129},{2,130},{3,131},{4,132},{5,133},{6,134},{7,135},{8... | collective-permute-start | bytes 344072 | tf_op jit(solution)/shard_map/ppermute | solution.py:454
  60.6 0.0 collective-permute-done.6
  60.6 0.0 collective-permute-done.4
  60.6 2.7 %collective-permute-done.3 = f32[14,16,128]{2,1,0:T(8,128)S(1)} collective-permute-done((f32[14,16,128]{2,1,0:T(8,128)S(1)}, f32[14,16,128]{2,1,0:T(8,128)S(1)}, u32[]{:S(2)}, u32[]{:S(2)}) %collective-permute-start.3) | collective-permute-done | bytes 114720 | tf_op jit(solution)/shard_map/ppermute | solution.py:454
  63.3 1.3 %shard_map.30 = (f32[4,16,128]{2,1,0:T(8,128)S(1)}, f32[4,16,128]{2,1,0:T(8,128)S(1)}) custom-call(s32[4]{0:T(128)S(1)} %pad_add_fusion.place_ref, f32[3,8,16,128]{3,2,1,0:T(8,128)S(1)} %get-tuple-element.23.c_ref, f32[3,8,16,128]{3,2,1,0:T(8,128)S(1)} %get-tuple-element.20.v_ref, f32[14,16,128]{2,1,0:T(8,128)S(1)} %collective-permute-done.ac_ref, ...), custom_call_target="tpu_custom_call" | custom-call | tf_op jit(solution)/shard_map/pallas_call | solution.py:480
  64.7 3.7 %collective-permute-start.7 = (f32[4,16,128]{2,1,0:T(8,128)S(1)}, f32[4,16,128]{2,1,0:T(8,128)S(1)}, u32[]{:S(2)}, u32[]{:S(2)}) collective-permute-start(f32[4,16,128]{2,1,0:T(8,128)S(1)} %get-tuple-element.25), channel_id=1, source_target_pairs={{0,1},{1,2},{2,3},{3,4},{4,5},{5,6},{6,7},{7,8},{8,9},{9,10},{10,1... | collective-permute-start | bytes 98312 | tf_op jit(solution)/shard_map/ppermute | solution.py:454
  68.4 8.4 %collective-permute-start.8 = (f32[4,16,128]{2,1,0:T(8,128)S(1)}, f32[4,16,128]{2,1,0:T(8,128)S(1)}, u32[]{:S(2)}, u32[]{:S(2)}) collective-permute-start(f32[4,16,128]{2,1,0:T(8,128)S(1)} %get-tuple-element.26), channel_id=1, source_target_pairs={{0,911},{1,0},{2,1},{3,2},{4,3},{5,4},{6,5},{7,6},{8,7},{9,8},{10,... | collective-permute-start | bytes 98312 | tf_op jit(solution)/shard_map/ppermute | solution.py:454
  76.8 0.0 collective-permute-done.7.zl_ref
  76.8 1.6 %collective-permute-done.8.zr_ref = f32[4,16,128]{2,1,0:T(8,128)S(1)} collective-permute-done((f32[4,16,128]{2,1,0:T(8,128)S(1)}, f32[4,16,128]{2,1,0:T(8,128)S(1)}, u32[]{:S(2)}, u32[]{:S(2)}) %collective-permute-start.8) | collective-permute-done | bytes 32800 | tf_op jit(solution)/shard_map/ppermute | solution.py:454
  78.4 0.6 shard_map.31
  79.0 0.8 collective-permute-start.9
  79.8 0.0 collective-permute-start.10
  79.8 0.0 collective-permute-done.11.above_ref
  79.8 0.0 collective-permute-done.12.below_ref
  79.8 3.0 %shard_map.33 = (f32[3,3,16,24,128]{4,3,2,1,0:T(8,128)S(1)}, f32[3,16,24,128]{3,2,1,0:T(8,128)S(1)}, f32[3,3,16,24,128]{4,3,2,1,0:T(8,128)S(1)}) custom-call(s32[4]{0:T(128)S(1)} %pad_add_fusion.place_ref, f32[3,8,16,128]{3,2,1,0:T(8,128)S(1)} %get-tuple-element.23.c_ref, f32[3,8,16,128]{3,2,1,0:T(8,128)S(1)} %get-tuple-element.20.v_ref, ...), custom_call_target="tpu_custom_call" | custom-call | tf_op jit(solution)/shard_map/pallas_call | solution.py:490
  82.8 0.0 collective-permute-done.9.above_ref
  82.8 1.8 %collective-permute-done.10.below_ref = f32[16,8,128]{2,1,0:T(8,128)S(1)} collective-permute-done((f32[16,8,128]{2,1,0:T(8,128)S(1)}, f32[16,8,128]{2,1,0:T(8,128)S(1)}, u32[]{:S(2)}, u32[]{:S(2)}) %collective-permute-start.10) | collective-permute-done | bytes 65568 | tf_op jit(solution)/shard_map/ppermute | solution.py:454
  84.7 7.8 %shard_map.34 = (f32[3,3,16,24,128]{4,3,2,1,0:T(8,128)S(1)}, f32[3,16,24,128]{3,2,1,0:T(8,128)S(1)}, f32[3,3,16,24,128]{4,3,2,1,0:T(8,128)S(1)}, f32[3,8,16,128]{3,2,1,0:T(8,128)}) custom-call(s32[4]{0:T(128)S(1)} %pad_add_fusion.place_ref, ...), custom_call_target="tpu_custom_call", output_to_operand_aliasing={{0}: (7, {}), {1}: (8, {}), {2}: (9, {})} | custom-call | tf_op jit(solution)/shard_map/pallas_call | solution.py:495
  (8 shorter events, 0.1 us)
Async XLA Ops:
  0.1 0.9 %copy-start = (f32[3,8,16,128]{3,2,1,0:T(8,128)S(1)}, f32[3,8,16,128]{3,2,1,0:T(8,128)}, u32[]{:S(2)}) copy-start(f32[3,8,16,128]{3,2,1,0:T(8,128)} %v_ref.1) | copy-start | bytes 589828
  1.6 7.2 %collective-permute-start.1 = (f32[12,16,128]{2,1,0:T(8,128)S(1)}, f32[12,16,128]{2,1,0:T(8,128)S(1)}, u32[]{:S(2)}, u32[]{:S(2)}) collective-permute-start(f32[12,16,128]{2,1,0:T(8,128)S(1)} %get-tuple-element.22), channel_id=1, source_target_pairs={{0,128},{1,129},{2,130},{3,131},{4,132},{5,133},{6,134},{7,135},{8... | collective-permute-start | bytes 294920 | tf_op jit(solution)/shard_map/ppermute | solution.py:454
  4.3 0.9 %copy-start.1 = (f32[3,8,16,128]{3,2,1,0:T(8,128)S(1)}, f32[3,8,16,128]{3,2,1,0:T(8,128)}, u32[]{:S(2)}) copy-start(f32[3,8,16,128]{3,2,1,0:T(8,128)} %c_ref.1) | copy-start | bytes 589828
  6.8 32.9 %collective-permute-start.5 = (f32[6,4,16,128]{3,2,1,0:T(8,128)S(1)}, f32[6,4,16,128]{3,2,1,0:T(8,128)S(1)}, u32[]{:S(2)}, u32[]{:S(2)}) collective-permute-start(f32[6,4,16,128]{3,2,1,0:T(8,128)S(1)} %get-tuple-element.24), channel_id=1, source_target_pairs={{0,128},{1,129},{2,130},{3,131},{4,132},{5,133},{6,134},{7,135},{8... | collective-permute-start | bytes 589832 | tf_op jit(solution)/shard_map/ppermute | solution.py:454
  8.8 33.6 %collective-permute-start.2 = (f32[14,16,128]{2,1,0:T(8,128)S(1)}, f32[14,16,128]{2,1,0:T(8,128)S(1)}, u32[]{:S(2)}, u32[]{:S(2)}) collective-permute-start(f32[14,16,128]{2,1,0:T(8,128)S(1)} %pad_maximum_fusion), channel_id=1, source_target_pairs={{128,768},{129,769},{130,770},{131,771},{132,772},{133,773},{134,7... | collective-permute-start | bytes 344072 | tf_op jit(solution)/shard_map/ppermute | solution.py:454
  9.4 35.7 %collective-permute-start = (f32[14,16,128]{2,1,0:T(8,128)S(1)}, f32[14,16,128]{2,1,0:T(8,128)S(1)}, u32[]{:S(2)}, u32[]{:S(2)}) collective-permute-start(f32[14,16,128]{2,1,0:T(8,128)S(1)} %get-tuple-element.21), channel_id=1, source_target_pairs={{0,896},{1,897},{2,898},{3,899},{4,900},{5,901},{6,902},{7,903},{8... | collective-permute-start | bytes 344072 | tf_op jit(solution)/shard_map/ppermute | solution.py:454
  39.0 21.6 %collective-permute-start.4 = (f32[12,16,128]{2,1,0:T(8,128)S(1)}, f32[12,16,128]{2,1,0:T(8,128)S(1)}, u32[]{:S(2)}, u32[]{:S(2)}) collective-permute-start(f32[12,16,128]{2,1,0:T(8,128)S(1)} %get-tuple-element.22), channel_id=1, source_target_pairs={{128,256},{129,257},{130,258},{131,259},{132,260},{133,261},{134,2... | collective-permute-start | bytes 294920 | tf_op jit(solution)/shard_map/ppermute | solution.py:454
  40.5 39.3 %collective-permute-start.11 = (f32[36,8,128]{2,1,0:T(8,128)S(1)}, f32[36,8,128]{2,1,0:T(8,128)S(1)}, u32[]{:S(2)}, u32[]{:S(2)}) collective-permute-start(f32[36,8,128]{2,1,0:T(8,128)S(1)} %get-tuple-element.29), channel_id=1, source_target_pairs={{0,112},{1,113},{2,114},{3,115},{4,116},{5,117},{6,118},{7,119},{8... | collective-permute-start | bytes 442376 | tf_op jit(solution)/shard_map/ppermute | solution.py:454
  42.4 37.4 %collective-permute-start.12 = (f32[36,8,128]{2,1,0:T(8,128)S(1)}, f32[36,8,128]{2,1,0:T(8,128)S(1)}, u32[]{:S(2)}, u32[]{:S(2)}) collective-permute-start(f32[36,8,128]{2,1,0:T(8,128)S(1)} %get-tuple-element.30), channel_id=1, source_target_pairs={{0,16},{1,17},{2,18},{3,19},{4,20},{5,21},{6,22},{7,23},{8,24},{9,... | collective-permute-start | bytes 442376 | tf_op jit(solution)/shard_map/ppermute | solution.py:454
  42.4 18.2 %collective-permute-start.6 = (f32[2,16,128]{2,1,0:T(8,128)S(1)}, f32[2,16,128]{2,1,0:T(8,128)S(1)}, u32[]{:S(2)}, u32[]{:S(2)}) collective-permute-start(f32[2,16,128]{2,1,0:T(8,128)S(1)} %slice.22), channel_id=1, source_target_pairs={{128,256},{143,271},{144,272},{159,287},{160,288},{175,303},{176,3... | collective-permute-start | bytes 49160 | tf_op jit(solution)/shard_map/ppermute | solution.py:454
  45.2 18.1 %collective-permute-start.3 = (f32[14,16,128]{2,1,0:T(8,128)S(1)}, f32[14,16,128]{2,1,0:T(8,128)S(1)}, u32[]{:S(2)}, u32[]{:S(2)}) collective-permute-start(f32[14,16,128]{2,1,0:T(8,128)S(1)} %broadcast_select_fusion), channel_id=1, source_target_pairs={{0,128},{1,129},{2,130},{3,131},{4,132},{5,133},{6,134},{7,135},{8... | collective-permute-start | bytes 344072 | tf_op jit(solution)/shard_map/ppermute | solution.py:454
  64.7 12.1 %collective-permute-start.7 = (f32[4,16,128]{2,1,0:T(8,128)S(1)}, f32[4,16,128]{2,1,0:T(8,128)S(1)}, u32[]{:S(2)}, u32[]{:S(2)}) collective-permute-start(f32[4,16,128]{2,1,0:T(8,128)S(1)} %get-tuple-element.25), channel_id=1, source_target_pairs={{0,1},{1,2},{2,3},{3,4},{4,5},{5,6},{6,7},{7,8},{8,9},{9,10},{10,1... | collective-permute-start | bytes 98312 | tf_op jit(solution)/shard_map/ppermute | solution.py:454
  68.4 10.0 %collective-permute-start.8 = (f32[4,16,128]{2,1,0:T(8,128)S(1)}, f32[4,16,128]{2,1,0:T(8,128)S(1)}, u32[]{:S(2)}, u32[]{:S(2)}) collective-permute-start(f32[4,16,128]{2,1,0:T(8,128)S(1)} %get-tuple-element.26), channel_id=1, source_target_pairs={{0,911},{1,0},{2,1},{3,2},{4,3},{5,4},{6,5},{7,6},{8,7},{9,8},{10,... | collective-permute-start | bytes 98312 | tf_op jit(solution)/shard_map/ppermute | solution.py:454
  79.0 3.9 %collective-permute-start.9 = (f32[16,8,128]{2,1,0:T(8,128)S(1)}, f32[16,8,128]{2,1,0:T(8,128)S(1)}, u32[]{:S(2)}, u32[]{:S(2)}) collective-permute-start(f32[16,8,128]{2,1,0:T(8,128)S(1)} %get-tuple-element.27), channel_id=1, source_target_pairs={{0,112},{1,113},{2,114},{3,115},{4,116},{5,117},{6,118},{7,119},{8... | collective-permute-start | bytes 196616 | tf_op jit(solution)/shard_map/ppermute | solution.py:454
  79.8 4.9 %collective-permute-start.10 = (f32[16,8,128]{2,1,0:T(8,128)S(1)}, f32[16,8,128]{2,1,0:T(8,128)S(1)}, u32[]{:S(2)}, u32[]{:S(2)}) collective-permute-start(f32[16,8,128]{2,1,0:T(8,128)S(1)} %get-tuple-element.28), channel_id=1, source_target_pairs={{0,16},{1,17},{2,18},{3,19},{4,20},{5,21},{6,22},{7,23},{8,24},{9,... | collective-permute-start | bytes 196616 | tf_op jit(solution)/shard_map/ppermute | solution.py:454

commit v10 on v9

--- a/solution.py
+++ b/solution.py
@@ -269,8 +269,29 @@
     return (t_ref, (0, field)) if field < 3 else (w_ref, (field - 3,))
 
 
+def edge_rows(t_ref, w_ref, ec_ref, ev_ref, ed_ref, zl, zr, s, rows):
+    lane = lanes_of(zl.shape)
+    back = 128 - 32 * lax.shift_right_logical(s, 2)
+    zl, zr = pltpu.roll(zl, back, 1), pltpu.roll(zr, back, 1)
+    for kind, e_ref in ((0, ec_ref), (1, ev_ref)):
+        e = jnp.zeros(zl.shape, jnp.float32)
+        for i in range(3):
+            field = 3 * kind + i
+            at = 32 * i
+            source, where = widened(t_ref, w_ref, field)
+            x = source[(*where, s, rows)]
+            e = jnp.where(between(lane, at, at + 4), roll(zl, at - 4 * field, 1), e)
+            e = jnp.where(between(lane, at + 4, at + 16), roll(x, at + 4, 1), e)
+            e = jnp.where(between(lane, at + 16, at + 28), roll(x, at + 28, 1), e)
+            e = jnp.where(between(lane, at + 28, at + 32), roll(zr, at + 28 - 4 * field, 1), e)
+        e_ref[s, rows] = e
+    for k, d in enumerate(replicate(e)):
+        ed_ref[k, s, rows] = d
+
+
 def compute_early(
-    place_ref, c_ref, v_ref, b_ref, above_ref, below_ref, t_ref, w_ref, s_ref, x_ref
+    place_ref, c_ref, v_ref, b_ref, above_ref, below_ref, ac_ref, av_ref, zl_ref, zr_ref,
+    t_ref, w_ref, s_ref, ec_ref, ev_ref, ed_ref, x_ref,
 ):
     odd = place_ref[0]
     side = 12 - 12 * odd
@@ -295,8 +316,20 @@
             to[(*at, side + q, slice(16, 24))] = near
             to[(*at, side + 2 + q, slice(16, 24))] = far
 
+    def across(q):
+        for field in range(6):
+            ref, i = field_of(ac_ref, av_ref, field)
+            to, at = widened(t_ref, w_ref, field)
+            to[(*at, 12 - side + q, slice(0, 16))] = ref[4 * i + q]
+
+    def edges(s):
+        q = lax.bitwise_and(s, 3)
+        edge_rows(t_ref, w_ref, ec_ref, ev_ref, ed_ref, zl_ref[q], zr_ref[q], s, slice(0, 16))
+
     loop(0, 4, own)
     loop(0, 2, beyond)
+    loop(0, 4, across)
+    loop(0, 16, edges, 2)
     loop(0, 8, lambda k: main_slopes(w_ref, s_ref, first + 2 + k))
 
     def substep(n):
@@ -312,8 +345,8 @@
 
 
 def compute_late(
-    place_ref, ac_ref, av_ref, zl_ref, zr_ref, above_ref, below_ref, t_in, w_in, s_in,
-    t_ref, w_ref, s_ref, out_ref, x_ref, ec_ref, ev_ref, ed_ref, ex_ref, es_ref,
+    place_ref, above_ref, below_ref, t_in, w_in, s_in, ec_in, ev_in, ed_in,
+    t_ref, w_ref, s_ref, ec_ref, ev_ref, ed_ref, out_ref, x_ref, ex_ref, es_ref,
 ):
     odd = place_ref[0]
     side = 12 * odd
@@ -322,10 +355,7 @@
 
     def beyond(q):
         for field in range(6):
-            ref, i = field_of(ac_ref, av_ref, field)
             to, at = widened(t_ref, w_ref, field)
-            to[(*at, side + q, slice(0, 16))] = ref[4 * i + q]
-            to[(*at, side + 2 + q, slice(0, 16))] = ref[4 * i + 2 + q]
             near, far = halo(above_ref, below_ref, 2 * field + q)
             to[(*at, side + q, slice(16, 24))] = near
             to[(*at, side + 2 + q, slice(16, 24))] = far
@@ -333,27 +363,8 @@
     loop(0, 2, beyond)
 
     def edges(s):
-        lane = lanes_of((24, 128))
-        g, q = lax.shift_right_logical(s, 2), lax.bitwise_and(s, 3)
-        zl_halo, zr_halo = halo(above_ref, below_ref, 12 + q)
-        zl = jnp.concatenate([zl_ref[q], zl_halo], axis=0)
-        zr = jnp.concatenate([zr_ref[q], zr_halo], axis=0)
-        back = 128 - 32 * g
-        zl, zr = pltpu.roll(zl, back, 1), pltpu.roll(zr, back, 1)
-        for kind, e_ref in ((0, ec_ref), (1, ev_ref)):
-            e = jnp.zeros((24, 128), jnp.float32)
-            for i in range(3):
-                field = 3 * kind + i
-                at = 32 * i
-                source, where = widened(t_ref, w_ref, field)
-                x = source[(*where, s)]
-                e = jnp.where(between(lane, at, at + 4), roll(zl, at - 4 * field, 1), e)
-                e = jnp.where(between(lane, at + 4, at + 16), roll(x, at + 4, 1), e)
-                e = jnp.where(between(lane, at + 16, at + 28), roll(x, at + 28, 1), e)
-                e = jnp.where(between(lane, at + 28, at + 32), roll(zr, at + 28 - 4 * field, 1), e)
-            e_ref[s] = e
-        for k, d in enumerate(replicate(e)):
-            ed_ref[k, s] = d
+        zl, zr = halo(above_ref, below_ref, 12 + lax.bitwise_and(s, 3))
+        edge_rows(t_ref, w_ref, ec_ref, ev_ref, ed_ref, zl, zr, s, slice(16, 24))
 
     loop(0, 16, edges, 2)
     loop(0, 4, lambda k: main_slopes(w_ref, s_ref, first + k))
@@ -486,14 +497,14 @@
         above = send(down, y_down)
         below = send(up, y_up)
         block = (16, 24, 128)
-        state = [(3, 3, *block), (3, *block), (3, 3, *block)]
-        state = call(compute_early, state, [(3, *block)], 5)(
-            place, c, v, b, early_above, early_below
+        state = [(3, 3, *block), (3, *block), (3, 3, *block), block, block, (3, *block)]
+        state = call(compute_early, state, [(3, *block)], 9)(
+            place, c, v, b, early_above, early_below, ac, av, zl, zr
         )
-        scratch = [(3, *block), block, block, (3, *block), block, (3, *block)]
+        scratch = [(3, *block), block, (3, *block)]
         shapes = [a.shape for a in state] + [(3, 8, 16, 128)]
-        *_, out = call(compute_late, shapes, scratch, 9, {7 + k: k for k in range(3)})(
-            place, ac, av, zl, zr, above, below, *state
+        *_, out = call(compute_late, shapes, scratch, 8, {3 + k: k for k in range(6)})(
+            place, above, below, *state
         )
         return out
 

time: 94.3 us -> 95.8 us (1.016)
  the two profiles are of different devices: /device:TPU:6 before, /device:TPU:1 now
where the time goes in v10:
time: 95.8 us; the launch traced here: 95.4 us
  starting transfers between devices  72.9 us (76%)
  Pallas kernels  17.1 us (18%)
  waiting for transfers between devices  3.15 us (3%)
  local copies, waits for them, and re-layouts  1.86 us (2%)
    ppermute x13, starting transfers between devices, send(): return lax.ppermute(value, AXES, pairs)  72.9 us
    pallas_call x1, Pallas kernels, local(): call(compute_late, shapes, scratch, 8, {3 + k: k for k in range(6)})  7.22 us
    pallas_call x1, Pallas kernels, local(): call(compute_early, state, [(3, *block)], 9)  5.12 us
    ppermute x13, waiting for transfers between devices, send(): return lax.ppermute(value, AXES, pairs)  3.15 us
  transfers between devices with their start and end apart: 13, of which 2 were waited for; matrix products, arithmetic and copies ran while one was open for 0% of the time, Pallas kernels for 10%

profile of v10, /device:TPU:1, one launch (start us, length us, event | category | flops | bytes accessed | tf_op | source)
XLA Modules:
  0.0 95.4 jit_solution(9119461451034669438)
XLA Ops:
  0.0 0.1 pad_add_fusion.place_ref
  0.1 0.0 copy-start
  0.1 0.9 copy-done
  1.0 0.6 shard_map.28
  1.6 3.9 %collective-permute-start.1 = (f32[12,16,128]{2,1,0:T(8,128)S(1)}, f32[12,16,128]{2,1,0:T(8,128)S(1)}, u32[]{:S(2)}, u32[]{:S(2)}) collective-permute-start(f32[12,16,128]{2,1,0:T(8,128)S(1)} %get-tuple-element.25), channel_id=1, source_target_pairs={{0,128},{1,129},{2,130},{3,131},{4,132},{5,133},{6,134},{7,135},{8... | collective-permute-start | bytes 294920 | tf_op jit(solution)/shard_map/ppermute | solution.py:465
  5.5 0.0 copy-start.1
  5.5 0.9 copy-done.1
  6.5 1.6 %shard_map.29 = (f32[14,16,128]{2,1,0:T(8,128)S(1)}, f32[6,4,16,128]{3,2,1,0:T(8,128)S(1)}, f32[4,16,128]{2,1,0:T(8,128)}, f32[3,8,16,128]{3,2,1,0:T(8,128)S(1)}) custom-call(s32[4]{0:T(128)S(1)} %pad_add_fusion.place_ref, f32[3,8,16,128]{3,2,1,0:T(8,128)S(1)} %copy-done.1, f32[3,8,16,128]{3,2,1,0:T(8,128)S(1)} %get-tuple-element.23.v_ref), custom_call_target="tpu_custom_call" | custom-call | tf_op jit(solution)/shard_map/pallas_call | solution.py:478
  8.0 1.9 %collective-permute-start.5 = (f32[6,4,16,128]{3,2,1,0:T(8,128)S(1)}, f32[6,4,16,128]{3,2,1,0:T(8,128)S(1)}, u32[]{:S(2)}, u32[]{:S(2)}) collective-permute-start(f32[6,4,16,128]{3,2,1,0:T(8,128)S(1)} %get-tuple-element.27), channel_id=1, source_target_pairs={{0,128},{1,129},{2,130},{3,131},{4,132},{5,133},{6,134},{7,135},{8... | collective-permute-start | bytes 589832 | tf_op jit(solution)/shard_map/ppermute | solution.py:465
  9.9 0.0 collective-permute-done.1
  10.0 0.7 collective-permute-start.2
  10.6 30.2 %collective-permute-start = (f32[14,16,128]{2,1,0:T(8,128)S(1)}, f32[14,16,128]{2,1,0:T(8,128)S(1)}, u32[]{:S(2)}, u32[]{:S(2)}) collective-permute-start(f32[14,16,128]{2,1,0:T(8,128)S(1)} %get-tuple-element.24), channel_id=1, source_target_pairs={{0,896},{1,897},{2,898},{3,899},{4,900},{5,901},{6,902},{7,903},{8... | collective-permute-start | bytes 344072 | tf_op jit(solution)/shard_map/ppermute | solution.py:465
  40.9 0.7 collective-permute-start.4
  41.6 0.0 collective-permute-done.5.b_ref
  41.6 0.8 shard_map.32
  42.4 1.2 %collective-permute-start.11 = (f32[36,8,128]{2,1,0:T(8,128)S(1)}, f32[36,8,128]{2,1,0:T(8,128)S(1)}, u32[]{:S(2)}, u32[]{:S(2)}) collective-permute-start(f32[36,8,128]{2,1,0:T(8,128)S(1)} %get-tuple-element.32), channel_id=1, source_target_pairs={{0,112},{1,113},{2,114},{3,115},{4,116},{5,117},{6,118},{7,119},{8... | collective-permute-start | bytes 442376 | tf_op jit(solution)/shard_map/ppermute | solution.py:465
  43.6 1.2 %collective-permute-start.12 = (f32[36,8,128]{2,1,0:T(8,128)S(1)}, f32[36,8,128]{2,1,0:T(8,128)S(1)}, u32[]{:S(2)}, u32[]{:S(2)}) collective-permute-start(f32[36,8,128]{2,1,0:T(8,128)S(1)} %get-tuple-element.33), channel_id=1, source_target_pairs={{0,16},{1,17},{2,18},{3,19},{4,20},{5,21},{6,22},{7,23},{8,24},{9,... | collective-permute-start | bytes 442376 | tf_op jit(solution)/shard_map/ppermute | solution.py:465
  44.8 0.0 collective-permute-done.2
  44.8 0.7 collective-permute-start.6
  45.5 0.0 collective-permute-done.ac_ref
  45.5 9.0 %collective-permute-start.3 = (f32[14,16,128]{2,1,0:T(8,128)S(1)}, f32[14,16,128]{2,1,0:T(8,128)S(1)}, u32[]{:S(2)}, u32[]{:S(2)}) collective-permute-start(f32[14,16,128]{2,1,0:T(8,128)S(1)} %broadcast_select_fusion), channel_id=1, source_target_pairs={{0,128},{1,129},{2,130},{3,131},{4,132},{5,133},{6,134},{7,135},{8... | collective-permute-start | bytes 344072 | tf_op jit(solution)/shard_map/ppermute | solution.py:465
  54.6 0.0 collective-permute-done.6
  54.6 0.0 collective-permute-done.4
  54.6 2.1 %collective-permute-done.3 = f32[14,16,128]{2,1,0:T(8,128)S(1)} collective-permute-done((f32[14,16,128]{2,1,0:T(8,128)S(1)}, f32[14,16,128]{2,1,0:T(8,128)S(1)}, u32[]{:S(2)}, u32[]{:S(2)}) %collective-permute-start.3) | collective-permute-done | bytes 114720 | tf_op jit(solution)/shard_map/ppermute | solution.py:465
  56.8 1.3 %shard_map.30 = (f32[4,16,128]{2,1,0:T(8,128)S(1)}, f32[4,16,128]{2,1,0:T(8,128)S(1)}) custom-call(s32[4]{0:T(128)S(1)} %pad_add_fusion.place_ref, f32[3,8,16,128]{3,2,1,0:T(8,128)S(1)} %get-tuple-element.26.c_ref, f32[3,8,16,128]{3,2,1,0:T(8,128)S(1)} %get-tuple-element.23.v_ref, f32[14,16,128]{2,1,0:T(8,128)S(1)} %collective-permute-done.ac_ref, ...), custom_call_target="tpu_custom_call" | custom-call | tf_op jit(solution)/shard_map/pallas_call | solution.py:491
  58.1 7.3 %collective-permute-start.7 = (f32[4,16,128]{2,1,0:T(8,128)S(1)}, f32[4,16,128]{2,1,0:T(8,128)S(1)}, u32[]{:S(2)}, u32[]{:S(2)}) collective-permute-start(f32[4,16,128]{2,1,0:T(8,128)S(1)} %get-tuple-element.28), channel_id=1, source_target_pairs={{0,1},{1,2},{2,3},{3,4},{4,5},{5,6},{6,7},{7,8},{8,9},{9,10},{10,1... | collective-permute-start | bytes 98312 | tf_op jit(solution)/shard_map/ppermute | solution.py:465
  65.4 12.5 %collective-permute-start.8 = (f32[4,16,128]{2,1,0:T(8,128)S(1)}, f32[4,16,128]{2,1,0:T(8,128)S(1)}, u32[]{:S(2)}, u32[]{:S(2)}) collective-permute-start(f32[4,16,128]{2,1,0:T(8,128)S(1)} %get-tuple-element.29), channel_id=1, source_target_pairs={{0,911},{1,0},{2,1},{3,2},{4,3},{5,4},{6,5},{7,6},{8,7},{9,8},{10,... | collective-permute-start | bytes 98312 | tf_op jit(solution)/shard_map/ppermute | solution.py:465
  77.9 0.0 collective-permute-done.7.zl_ref
  77.9 1.0 %collective-permute-done.8.zr_ref = f32[4,16,128]{2,1,0:T(8,128)S(1)} collective-permute-done((f32[4,16,128]{2,1,0:T(8,128)S(1)}, f32[4,16,128]{2,1,0:T(8,128)S(1)}, u32[]{:S(2)}, u32[]{:S(2)}) %collective-permute-start.8) | collective-permute-done | bytes 32800 | tf_op jit(solution)/shard_map/ppermute | solution.py:465
  78.9 0.6 shard_map.31
  79.5 2.3 %collective-permute-start.9 = (f32[16,8,128]{2,1,0:T(8,128)S(1)}, f32[16,8,128]{2,1,0:T(8,128)S(1)}, u32[]{:S(2)}, u32[]{:S(2)}) collective-permute-start(f32[16,8,128]{2,1,0:T(8,128)S(1)} %get-tuple-element.30), channel_id=1, source_target_pairs={{0,112},{1,113},{2,114},{3,115},{4,116},{5,117},{6,118},{7,119},{8... | collective-permute-start | bytes 196616 | tf_op jit(solution)/shard_map/ppermute | solution.py:465
  81.8 1.2 %collective-permute-start.10 = (f32[16,8,128]{2,1,0:T(8,128)S(1)}, f32[16,8,128]{2,1,0:T(8,128)S(1)}, u32[]{:S(2)}, u32[]{:S(2)}) collective-permute-start(f32[16,8,128]{2,1,0:T(8,128)S(1)} %get-tuple-element.31), channel_id=1, source_target_pairs={{0,16},{1,17},{2,18},{3,19},{4,20},{5,21},{6,22},{7,23},{8,24},{9,... | collective-permute-start | bytes 196616 | tf_op jit(solution)/shard_map/ppermute | solution.py:465
  83.0 0.0 collective-permute-done.11.above_ref
  83.1 0.0 collective-permute-done.12.below_ref
  83.1 5.1 %shard_map.33 = (f32[3,3,16,24,128]{4,3,2,1,0:T(8,128)S(1)}, f32[3,16,24,128]{3,2,1,0:T(8,128)S(1)}, f32[3,3,16,24,128]{4,3,2,1,0:T(8,128)S(1)}, f32[16,24,128]{...) custom-call(s32[4]{0:T(128)S(1)} %pad_add_fusion.place_ref, ...), custom_call_target="tpu_custom_call" | custom-call | tf_op jit(solution)/shard_map/pallas_call | solution.py:501
  88.2 0.0 collective-permute-done.9.above_ref
  88.2 0.0 collective-permute-done.10.below_ref
  88.2 7.2 %shard_map.34 = (f32[3,3,16,24,128]{4,3,2,1,0:T(8,128)S(1)}, f32[3,16,24,128]{3,2,1,0:T(8,128)S(1)}, f32[3,3,16,24,128]{4,3,2,1,0:T(8,128)S(1)}, f32[16,24,128]{...) custom-call(s32[4]{0:T(128)S(1)} %pad_add_fusion.place_ref, ...), custom_call_target="tpu_custom_call", output_to_operand_aliasing={{0}: (3, {}), {1}: (4, {}), {2}: (5, {}), {3}: (6, {}), {4}... | custom-call | tf_op jit(solution)/shard_map/pallas_call | solution.py:506
  (8 shorter events, 0.1 us)
Async XLA Ops:
  0.1 0.9 copy-start
  1.6 8.4 %collective-permute-start.1 = (f32[12,16,128]{2,1,0:T(8,128)S(1)}, f32[12,16,128]{2,1,0:T(8,128)S(1)}, u32[]{:S(2)}, u32[]{:S(2)}) collective-permute-start(f32[12,16,128]{2,1,0:T(8,128)S(1)} %get-tuple-element.25), channel_id=1, source_target_pairs={{0,128},{1,129},{2,130},{3,131},{4,132},{5,133},{6,134},{7,135},{8... | collective-permute-start | bytes 294920 | tf_op jit(solution)/shard_map/ppermute | solution.py:465
  5.5 0.9 copy-start.1
  8.0 33.6 %collective-permute-start.5 = (f32[6,4,16,128]{3,2,1,0:T(8,128)S(1)}, f32[6,4,16,128]{3,2,1,0:T(8,128)S(1)}, u32[]{:S(2)}, u32[]{:S(2)}) collective-permute-start(f32[6,4,16,128]{3,2,1,0:T(8,128)S(1)} %get-tuple-element.27), channel_id=1, source_target_pairs={{0,128},{1,129},{2,130},{3,131},{4,132},{5,133},{6,134},{7,135},{8... | collective-permute-start | bytes 589832 | tf_op jit(solution)/shard_map/ppermute | solution.py:465
  10.0 34.8 %collective-permute-start.2 = (f32[14,16,128]{2,1,0:T(8,128)S(1)}, f32[14,16,128]{2,1,0:T(8,128)S(1)}, u32[]{:S(2)}, u32[]{:S(2)}) collective-permute-start(f32[14,16,128]{2,1,0:T(8,128)S(1)} %pad_maximum_fusion), channel_id=1, source_target_pairs={{128,768},{129,769},{130,770},{131,771},{132,772},{133,773},{134,7... | collective-permute-start | bytes 344072 | tf_op jit(solution)/shard_map/ppermute | solution.py:465
  10.6 34.8 %collective-permute-start = (f32[14,16,128]{2,1,0:T(8,128)S(1)}, f32[14,16,128]{2,1,0:T(8,128)S(1)}, u32[]{:S(2)}, u32[]{:S(2)}) collective-permute-start(f32[14,16,128]{2,1,0:T(8,128)S(1)} %get-tuple-element.24), channel_id=1, source_target_pairs={{0,896},{1,897},{2,898},{3,899},{4,900},{5,901},{6,902},{7,903},{8... | collective-permute-start | bytes 344072 | tf_op jit(solution)/shard_map/ppermute | solution.py:465
  40.9 13.7 %collective-permute-start.4 = (f32[12,16,128]{2,1,0:T(8,128)S(1)}, f32[12,16,128]{2,1,0:T(8,128)S(1)}, u32[]{:S(2)}, u32[]{:S(2)}) collective-permute-start(f32[12,16,128]{2,1,0:T(8,128)S(1)} %get-tuple-element.25), channel_id=1, source_target_pairs={{128,256},{129,257},{130,258},{131,259},{132,260},{133,261},{134,2... | collective-permute-start | bytes 294920 | tf_op jit(solution)/shard_map/ppermute | solution.py:465
  42.4 40.7 %collective-permute-start.11 = (f32[36,8,128]{2,1,0:T(8,128)S(1)}, f32[36,8,128]{2,1,0:T(8,128)S(1)}, u32[]{:S(2)}, u32[]{:S(2)}) collective-permute-start(f32[36,8,128]{2,1,0:T(8,128)S(1)} %get-tuple-element.32), channel_id=1, source_target_pairs={{0,112},{1,113},{2,114},{3,115},{4,116},{5,117},{6,118},{7,119},{8... | collective-permute-start | bytes 442376 | tf_op jit(solution)/shard_map/ppermute | solution.py:465
  43.6 39.4 %collective-permute-start.12 = (f32[36,8,128]{2,1,0:T(8,128)S(1)}, f32[36,8,128]{2,1,0:T(8,128)S(1)}, u32[]{:S(2)}, u32[]{:S(2)}) collective-permute-start(f32[36,8,128]{2,1,0:T(8,128)S(1)} %get-tuple-element.33), channel_id=1, source_target_pairs={{0,16},{1,17},{2,18},{3,19},{4,20},{5,21},{6,22},{7,23},{8,24},{9,... | collective-permute-start | bytes 442376 | tf_op jit(solution)/shard_map/ppermute | solution.py:465
  44.8 9.8 %collective-permute-start.6 = (f32[2,16,128]{2,1,0:T(8,128)S(1)}, f32[2,16,128]{2,1,0:T(8,128)S(1)}, u32[]{:S(2)}, u32[]{:S(2)}) collective-permute-start(f32[2,16,128]{2,1,0:T(8,128)S(1)} %slice.22), channel_id=1, source_target_pairs={{128,256},{143,271},{144,272},{159,287},{160,288},{175,303},{176,3... | collective-permute-start | bytes 49160 | tf_op jit(solution)/shard_map/ppermute | solution.py:465
  45.5 11.2 %collective-permute-start.3 = (f32[14,16,128]{2,1,0:T(8,128)S(1)}, f32[14,16,128]{2,1,0:T(8,128)S(1)}, u32[]{:S(2)}, u32[]{:S(2)}) collective-permute-start(f32[14,16,128]{2,1,0:T(8,128)S(1)} %broadcast_select_fusion), channel_id=1, source_target_pairs={{0,128},{1,129},{2,130},{3,131},{4,132},{5,133},{6,134},{7,135},{8... | collective-permute-start | bytes 344072 | tf_op jit(solution)/shard_map/ppermute | solution.py:465
  58.1 19.8 %collective-permute-start.7 = (f32[4,16,128]{2,1,0:T(8,128)S(1)}, f32[4,16,128]{2,1,0:T(8,128)S(1)}, u32[]{:S(2)}, u32[]{:S(2)}) collective-permute-start(f32[4,16,128]{2,1,0:T(8,128)S(1)} %get-tuple-element.28), channel_id=1, source_target_pairs={{0,1},{1,2},{2,3},{3,4},{4,5},{5,6},{6,7},{7,8},{8,9},{9,10},{10,1... | collective-permute-start | bytes 98312 | tf_op jit(solution)/shard_map/ppermute | solution.py:465
  65.4 13.5 %collective-permute-start.8 = (f32[4,16,128]{2,1,0:T(8,128)S(1)}, f32[4,16,128]{2,1,0:T(8,128)S(1)}, u32[]{:S(2)}, u32[]{:S(2)}) collective-permute-start(f32[4,16,128]{2,1,0:T(8,128)S(1)} %get-tuple-element.29), channel_id=1, source_target_pairs={{0,911},{1,0},{2,1},{3,2},{4,3},{5,4},{6,5},{7,6},{8,7},{9,8},{10,... | collective-permute-start | bytes 98312 | tf_op jit(solution)/shard_map/ppermute | solution.py:465
  79.5 8.7 %collective-permute-start.9 = (f32[16,8,128]{2,1,0:T(8,128)S(1)}, f32[16,8,128]{2,1,0:T(8,128)S(1)}, u32[]{:S(2)}, u32[]{:S(2)}) collective-permute-start(f32[16,8,128]{2,1,0:T(8,128)S(1)} %get-tuple-element.30), channel_id=1, source_target_pairs={{0,112},{1,113},{2,114},{3,115},{4,116},{5,117},{6,118},{7,119},{8... | collective-permute-start | bytes 196616 | tf_op jit(solution)/shard_map/ppermute | solution.py:465
  81.8 6.4 %collective-permute-start.10 = (f32[16,8,128]{2,1,0:T(8,128)S(1)}, f32[16,8,128]{2,1,0:T(8,128)S(1)}, u32[]{:S(2)}, u32[]{:S(2)}) collective-permute-start(f32[16,8,128]{2,1,0:T(8,128)S(1)} %get-tuple-element.31), channel_id=1, source_target_pairs={{0,16},{1,17},{2,18},{3,19},{4,20},{5,21},{6,22},{7,23},{8,24},{9,... | collective-permute-start | bytes 196616 | tf_op jit(solution)/shard_map/ppermute | solution.py:465

commit v11 on v10

--- a/solution.py
+++ b/solution.py
@@ -290,8 +290,7 @@
 
 
 def compute_early(
-    place_ref, c_ref, v_ref, b_ref, above_ref, below_ref, ac_ref, av_ref, zl_ref, zr_ref,
-    t_ref, w_ref, s_ref, ec_ref, ev_ref, ed_ref, x_ref,
+    place_ref, c_ref, v_ref, b_ref, above_ref, below_ref, t_ref, w_ref, s_ref, x_ref
 ):
     odd = place_ref[0]
     side = 12 - 12 * odd
@@ -316,32 +315,39 @@
             to[(*at, side + q, slice(16, 24))] = near
             to[(*at, side + 2 + q, slice(16, 24))] = far
 
+    loop(0, 4, own)
+    loop(0, 2, beyond)
+    loop(0, 8, lambda k: main_slopes(w_ref, s_ref, first + 2 + k))
+
+    def substep(n):
+        main_along_x(t_ref, w_ref, x_ref, n, first + 2, 8)
+
+        def pair(k):
+            for j in range(2):
+                main_along_yz(t_ref, w_ref, x_ref, s_ref, n, first + 2 + 2 * n + 2 * k + j)
+
+        loop(0, 4 - 2 * n, pair)
+
+    loop(0, 2, substep)
+
+
+def own_edges(
+    place_ref, ac_ref, av_ref, zl_ref, zr_ref, t_in, w_in, t_ref, w_ref, ec_ref, ev_ref, ed_ref
+):
+    side = 12 * place_ref[0]
+
     def across(q):
         for field in range(6):
             ref, i = field_of(ac_ref, av_ref, field)
             to, at = widened(t_ref, w_ref, field)
-            to[(*at, 12 - side + q, slice(0, 16))] = ref[4 * i + q]
+            to[(*at, side + q, slice(0, 16))] = ref[4 * i + q]
 
     def edges(s):
         q = lax.bitwise_and(s, 3)
         edge_rows(t_ref, w_ref, ec_ref, ev_ref, ed_ref, zl_ref[q], zr_ref[q], s, slice(0, 16))
 
-    loop(0, 4, own)
-    loop(0, 2, beyond)
     loop(0, 4, across)
     loop(0, 16, edges, 2)
-    loop(0, 8, lambda k: main_slopes(w_ref, s_ref, first + 2 + k))
-
-    def substep(n):
-        main_along_x(t_ref, w_ref, x_ref, n, first + 2, 8)
-
-        def pair(k):
-            for j in range(2):
-                main_along_yz(t_ref, w_ref, x_ref, s_ref, n, first + 2 + 2 * n + 2 * k + j)
-
-        loop(0, 4 - 2 * n, pair)
-
-    loop(0, 2, substep)
 
 
 def compute_late(
@@ -497,10 +503,15 @@
         above = send(down, y_down)
         below = send(up, y_up)
         block = (16, 24, 128)
-        state = [(3, 3, *block), (3, *block), (3, 3, *block), block, block, (3, *block)]
-        state = call(compute_early, state, [(3, *block)], 9)(
-            place, c, v, b, early_above, early_below, ac, av, zl, zr
+        state = [(3, 3, *block), (3, *block), (3, 3, *block)]
+        t, w, slopes = call(compute_early, state, [(3, *block)], 5)(
+            place, c, v, b, early_above, early_below
         )
+        state = [(3, 3, *block), (3, *block), block, block, (3, *block)]
+        t, w, *edges = call(own_edges, state, (), 6, {5: 0, 6: 1})(
+            place, ac, av, zl, zr, t, w
+        )
+        state = [t, w, slopes, *edges]
         scratch = [(3, *block), block, (3, *block)]
         shapes = [a.shape for a in state] + [(3, 8, 16, 128)]
         *_, out = call(compute_late, shapes, scratch, 8, {3 + k: k for k in range(6)})(

time: 95.8 us -> 96.3 us (level)
    pallas_call x1 -> x2, Pallas kernels: 5.12 us -> 5.66 us  [the longest x1 3.03 us: local(): call(compute_early, state, [(3, *block)], 5)]
where the time goes in v11:
time: 96.3 us; the launch traced here: 96 us
  starting transfers between devices  72.9 us (76%)
  Pallas kernels  17.7 us (18%)
  waiting for transfers between devices  3.15 us (3%)
  local copies, waits for them, and re-layouts  1.86 us (2%)
    ppermute x13, starting transfers between devices, send(): return lax.ppermute(value, AXES, pairs)  72.9 us
    pallas_call x1, Pallas kernels, local(): call(compute_late, shapes, scratch, 8, {3 + k: k for k in range(6)})  7.22 us
    ppermute x13, waiting for transfers between devices, send(): return lax.ppermute(value, AXES, pairs)  3.15 us
    pallas_call x1, Pallas kernels, local(): call(compute_early, state, [(3, *block)], 5)  3.03 us
    pallas_call x1, Pallas kernels, local(): call(own_edges, state, (), 6, {5: 0, 6: 1})(place, ac, av, zl, zr, t, w)  2.63 us
  transfers between devices with their start and end apart: 13, of which 2 were waited for; matrix products, arithmetic and copies ran while one was open for 0% of the time, Pallas kernels for 10%

profile of v11, /device:TPU:1, one launch (start us, length us, event | category | flops | bytes accessed | tf_op | source)
XLA Modules:
  0.0 96.0 jit_solution(6239357085407501639)
XLA Ops:
  0.0 0.1 pad_add_fusion.place_ref
  0.1 0.0 copy-start
  0.1 0.9 copy-done
  1.0 0.6 shard_map.28
  1.6 3.9 %collective-permute-start.1 = (f32[12,16,128]{2,1,0:T(8,128)S(1)}, f32[12,16,128]{2,1,0:T(8,128)S(1)}, u32[]{:S(2)}, u32[]{:S(2)}) collective-permute-start(f32[12,16,128]{2,1,0:T(8,128)S(1)} %get-tuple-element.27), channel_id=1, source_target_pairs={{0,128},{1,129},{2,130},{3,131},{4,132},{5,133},{6,134},{7,135},{8... | collective-permute-start | bytes 294920 | tf_op jit(solution)/shard_map/ppermute | solution.py:471
  5.5 0.0 copy-start.1
  5.5 0.9 copy-done.1
  6.5 1.6 %shard_map.29 = (f32[14,16,128]{2,1,0:T(8,128)S(1)}, f32[6,4,16,128]{3,2,1,0:T(8,128)S(1)}, f32[4,16,128]{2,1,0:T(8,128)}, f32[3,8,16,128]{3,2,1,0:T(8,128)S(1)}) custom-call(s32[4]{0:T(128)S(1)} %pad_add_fusion.place_ref, f32[3,8,16,128]{3,2,1,0:T(8,128)S(1)} %copy-done.1, f32[3,8,16,128]{3,2,1,0:T(8,128)S(1)} %get-tuple-element.25.v_ref), custom_call_target="tpu_custom_call" | custom-call | tf_op jit(solution)/shard_map/pallas_call | solution.py:484
  8.0 1.9 %collective-permute-start.5 = (f32[6,4,16,128]{3,2,1,0:T(8,128)S(1)}, f32[6,4,16,128]{3,2,1,0:T(8,128)S(1)}, u32[]{:S(2)}, u32[]{:S(2)}) collective-permute-start(f32[6,4,16,128]{3,2,1,0:T(8,128)S(1)} %get-tuple-element.29), channel_id=1, source_target_pairs={{0,128},{1,129},{2,130},{3,131},{4,132},{5,133},{6,134},{7,135},{8... | collective-permute-start | bytes 589832 | tf_op jit(solution)/shard_map/ppermute | solution.py:471
  9.9 0.0 collective-permute-done.1
  10.0 0.7 collective-permute-start.2
  10.6 30.2 %collective-permute-start = (f32[14,16,128]{2,1,0:T(8,128)S(1)}, f32[14,16,128]{2,1,0:T(8,128)S(1)}, u32[]{:S(2)}, u32[]{:S(2)}) collective-permute-start(f32[14,16,128]{2,1,0:T(8,128)S(1)} %get-tuple-element.26), channel_id=1, source_target_pairs={{0,896},{1,897},{2,898},{3,899},{4,900},{5,901},{6,902},{7,903},{8... | collective-permute-start | bytes 344072 | tf_op jit(solution)/shard_map/ppermute | solution.py:471
  40.9 0.7 collective-permute-start.4
  41.6 0.0 collective-permute-done.5.b_ref
  41.6 0.8 shard_map.32
  42.4 1.2 %collective-permute-start.11 = (f32[36,8,128]{2,1,0:T(8,128)S(1)}, f32[36,8,128]{2,1,0:T(8,128)S(1)}, u32[]{:S(2)}, u32[]{:S(2)}) collective-permute-start(f32[36,8,128]{2,1,0:T(8,128)S(1)} %get-tuple-element.34), channel_id=1, source_target_pairs={{0,112},{1,113},{2,114},{3,115},{4,116},{5,117},{6,118},{7,119},{8... | collective-permute-start | bytes 442376 | tf_op jit(solution)/shard_map/ppermute | solution.py:471
  43.6 1.2 %collective-permute-start.12 = (f32[36,8,128]{2,1,0:T(8,128)S(1)}, f32[36,8,128]{2,1,0:T(8,128)S(1)}, u32[]{:S(2)}, u32[]{:S(2)}) collective-permute-start(f32[36,8,128]{2,1,0:T(8,128)S(1)} %get-tuple-element.35), channel_id=1, source_target_pairs={{0,16},{1,17},{2,18},{3,19},{4,20},{5,21},{6,22},{7,23},{8,24},{9,... | collective-permute-start | bytes 442376 | tf_op jit(solution)/shard_map/ppermute | solution.py:471
  44.8 0.0 collective-permute-done.2
  44.8 0.7 collective-permute-start.6
  45.5 0.0 collective-permute-done.ac_ref
  45.5 9.0 %collective-permute-start.3 = (f32[14,16,128]{2,1,0:T(8,128)S(1)}, f32[14,16,128]{2,1,0:T(8,128)S(1)}, u32[]{:S(2)}, u32[]{:S(2)}) collective-permute-start(f32[14,16,128]{2,1,0:T(8,128)S(1)} %broadcast_select_fusion), channel_id=1, source_target_pairs={{0,128},{1,129},{2,130},{3,131},{4,132},{5,133},{6,134},{7,135},{8... | collective-permute-start | bytes 344072 | tf_op jit(solution)/shard_map/ppermute | solution.py:471
  54.6 0.0 collective-permute-done.6
  54.6 0.0 collective-permute-done.4
  54.6 2.1 %collective-permute-done.3 = f32[14,16,128]{2,1,0:T(8,128)S(1)} collective-permute-done((f32[14,16,128]{2,1,0:T(8,128)S(1)}, f32[14,16,128]{2,1,0:T(8,128)S(1)}, u32[]{:S(2)}, u32[]{:S(2)}) %collective-permute-start.3) | collective-permute-done | bytes 114720 | tf_op jit(solution)/shard_map/ppermute | solution.py:471
  56.8 1.3 %shard_map.30 = (f32[4,16,128]{2,1,0:T(8,128)S(1)}, f32[4,16,128]{2,1,0:T(8,128)S(1)}) custom-call(s32[4]{0:T(128)S(1)} %pad_add_fusion.place_ref, f32[3,8,16,128]{3,2,1,0:T(8,128)S(1)} %get-tuple-element.28.c_ref, f32[3,8,16,128]{3,2,1,0:T(8,128)S(1)} %get-tuple-element.25.v_ref, f32[14,16,128]{2,1,0:T(8,128)S(1)} %collective-permute-done.ac_ref, ...), custom_call_target="tpu_custom_call" | custom-call | tf_op jit(solution)/shard_map/pallas_call | solution.py:497
  58.1 7.3 %collective-permute-start.7 = (f32[4,16,128]{2,1,0:T(8,128)S(1)}, f32[4,16,128]{2,1,0:T(8,128)S(1)}, u32[]{:S(2)}, u32[]{:S(2)}) collective-permute-start(f32[4,16,128]{2,1,0:T(8,128)S(1)} %get-tuple-element.30), channel_id=1, source_target_pairs={{0,1},{1,2},{2,3},{3,4},{4,5},{5,6},{6,7},{7,8},{8,9},{9,10},{10,1... | collective-permute-start | bytes 98312 | tf_op jit(solution)/shard_map/ppermute | solution.py:471
  65.4 12.5 %collective-permute-start.8 = (f32[4,16,128]{2,1,0:T(8,128)S(1)}, f32[4,16,128]{2,1,0:T(8,128)S(1)}, u32[]{:S(2)}, u32[]{:S(2)}) collective-permute-start(f32[4,16,128]{2,1,0:T(8,128)S(1)} %get-tuple-element.31), channel_id=1, source_target_pairs={{0,911},{1,0},{2,1},{3,2},{4,3},{5,4},{6,5},{7,6},{8,7},{9,8},{10,... | collective-permute-start | bytes 98312 | tf_op jit(solution)/shard_map/ppermute | solution.py:471
  77.9 0.0 collective-permute-done.7.zl_ref
  77.9 1.0 %collective-permute-done.8.zr_ref = f32[4,16,128]{2,1,0:T(8,128)S(1)} collective-permute-done((f32[4,16,128]{2,1,0:T(8,128)S(1)}, f32[4,16,128]{2,1,0:T(8,128)S(1)}, u32[]{:S(2)}, u32[]{:S(2)}) %collective-permute-start.8) | collective-permute-done | bytes 32800 | tf_op jit(solution)/shard_map/ppermute | solution.py:471
  78.9 0.6 shard_map.31
  79.5 2.3 %collective-permute-start.9 = (f32[16,8,128]{2,1,0:T(8,128)S(1)}, f32[16,8,128]{2,1,0:T(8,128)S(1)}, u32[]{:S(2)}, u32[]{:S(2)}) collective-permute-start(f32[16,8,128]{2,1,0:T(8,128)S(1)} %get-tuple-element.32), channel_id=1, source_target_pairs={{0,112},{1,113},{2,114},{3,115},{4,116},{5,117},{6,118},{7,119},{8... | collective-permute-start | bytes 196616 | tf_op jit(solution)/shard_map/ppermute | solution.py:471
  81.8 1.2 %collective-permute-start.10 = (f32[16,8,128]{2,1,0:T(8,128)S(1)}, f32[16,8,128]{2,1,0:T(8,128)S(1)}, u32[]{:S(2)}, u32[]{:S(2)}) collective-permute-start(f32[16,8,128]{2,1,0:T(8,128)S(1)} %get-tuple-element.33), channel_id=1, source_target_pairs={{0,16},{1,17},{2,18},{3,19},{4,20},{5,21},{6,22},{7,23},{8,24},{9,... | collective-permute-start | bytes 196616 | tf_op jit(solution)/shard_map/ppermute | solution.py:471
  83.0 0.0 collective-permute-done.11.above_ref
  83.1 0.0 collective-permute-done.12.below_ref
  83.1 3.0 %shard_map.33 = (f32[3,3,16,24,128]{4,3,2,1,0:T(8,128)S(1)}, f32[3,16,24,128]{3,2,1,0:T(8,128)S(1)}, f32[3,3,16,24,128]{4,3,2,1,0:T(8,128)S(1)}) custom-call(s32[4]{0:T(128)S(1)} %pad_add_fusion.place_ref, f32[3,8,16,128]{3,2,1,0:T(8,128)S(1)} %get-tuple-element.28.c_ref, f32[3,8,16,128]{3,2,1,0:T(8,128)S(1)} %get-tuple-element.25.v_ref, ...), custom_call_target="tpu_custom_call" | custom-call | tf_op jit(solution)/shard_map/pallas_call | solution.py:507
  86.1 2.6 %shard_map.34 = (f32[3,3,16,24,128]{4,3,2,1,0:T(8,128)S(1)}, f32[3,16,24,128]{3,2,1,0:T(8,128)S(1)}, f32[16,24,128]{2,1,0:T(8,128)S(1)}, f32[16,24,128]{2,1,0:T(8,128)S(1)}, f32[3,16,24,128]{3,2,1,0:T(8,128)S(1)}) custom-call(s32[4]{0:T(128)S(1)} %pad_add_fusion.place_ref, ...), custom_call_target="tpu_custom_call", output_to_operand_aliasing={{0}: (5, {}), {1}: (6, {})} | custom-call | tf_op jit(solution)/shard_map/pallas_call | solution.py:511
  88.7 0.0 collective-permute-done.9.above_ref
  88.7 0.0 collective-permute-done.10.below_ref
  88.8 7.2 %shard_map.35 = (f32[3,3,16,24,128]{4,3,2,1,0:T(8,128)S(1)}, f32[3,16,24,128]{3,2,1,0:T(8,128)S(1)}, f32[3,3,16,24,128]{4,3,2,1,0:T(8,128)S(1)}, f32[16,24,128]{...) custom-call(s32[4]{0:T(128)S(1)} %pad_add_fusion.place_ref, ...), custom_call_target="tpu_custom_call", output_to_operand_aliasing={{0}: (3, {}), {1}: (4, {}), {2}: (5, {}), {3}: (6, {}), {4}... | custom-call | tf_op jit(solution)/shard_map/pallas_call | solution.py:517
  (8 shorter events, 0.1 us)
Async XLA Ops:
  0.1 0.9 copy-start
  1.6 8.4 %collective-permute-start.1 = (f32[12,16,128]{2,1,0:T(8,128)S(1)}, f32[12,16,128]{2,1,0:T(8,128)S(1)}, u32[]{:S(2)}, u32[]{:S(2)}) collective-permute-start(f32[12,16,128]{2,1,0:T(8,128)S(1)} %get-tuple-element.27), channel_id=1, source_target_pairs={{0,128},{1,129},{2,130},{3,131},{4,132},{5,133},{6,134},{7,135},{8... | collective-permute-start | bytes 294920 | tf_op jit(solution)/shard_map/ppermute | solution.py:471
  5.5 0.9 copy-start.1
  8.0 33.6 %collective-permute-start.5 = (f32[6,4,16,128]{3,2,1,0:T(8,128)S(1)}, f32[6,4,16,128]{3,2,1,0:T(8,128)S(1)}, u32[]{:S(2)}, u32[]{:S(2)}) collective-permute-start(f32[6,4,16,128]{3,2,1,0:T(8,128)S(1)} %get-tuple-element.29), channel_id=1, source_target_pairs={{0,128},{1,129},{2,130},{3,131},{4,132},{5,133},{6,134},{7,135},{8... | collective-permute-start | bytes 589832 | tf_op jit(solution)/shard_map/ppermute | solution.py:471
  10.0 34.8 %collective-permute-start.2 = (f32[14,16,128]{2,1,0:T(8,128)S(1)}, f32[14,16,128]{2,1,0:T(8,128)S(1)}, u32[]{:S(2)}, u32[]{:S(2)}) collective-permute-start(f32[14,16,128]{2,1,0:T(8,128)S(1)} %pad_maximum_fusion), channel_id=1, source_target_pairs={{128,768},{129,769},{130,770},{131,771},{132,772},{133,773},{134,7... | collective-permute-start | bytes 344072 | tf_op jit(solution)/shard_map/ppermute | solution.py:471
  10.6 34.8 %collective-permute-start = (f32[14,16,128]{2,1,0:T(8,128)S(1)}, f32[14,16,128]{2,1,0:T(8,128)S(1)}, u32[]{:S(2)}, u32[]{:S(2)}) collective-permute-start(f32[14,16,128]{2,1,0:T(8,128)S(1)} %get-tuple-element.26), channel_id=1, source_target_pairs={{0,896},{1,897},{2,898},{3,899},{4,900},{5,901},{6,902},{7,903},{8... | collective-permute-start | bytes 344072 | tf_op jit(solution)/shard_map/ppermute | solution.py:471
  40.9 13.7 %collective-permute-start.4 = (f32[12,16,128]{2,1,0:T(8,128)S(1)}, f32[12,16,128]{2,1,0:T(8,128)S(1)}, u32[]{:S(2)}, u32[]{:S(2)}) collective-permute-start(f32[12,16,128]{2,1,0:T(8,128)S(1)} %get-tuple-element.27), channel_id=1, source_target_pairs={{128,256},{129,257},{130,258},{131,259},{132,260},{133,261},{134,2... | collective-permute-start | bytes 294920 | tf_op jit(solution)/shard_map/ppermute | solution.py:471
  42.4 40.7 %collective-permute-start.11 = (f32[36,8,128]{2,1,0:T(8,128)S(1)}, f32[36,8,128]{2,1,0:T(8,128)S(1)}, u32[]{:S(2)}, u32[]{:S(2)}) collective-permute-start(f32[36,8,128]{2,1,0:T(8,128)S(1)} %get-tuple-element.34), channel_id=1, source_target_pairs={{0,112},{1,113},{2,114},{3,115},{4,116},{5,117},{6,118},{7,119},{8... | collective-permute-start | bytes 442376 | tf_op jit(solution)/shard_map/ppermute | solution.py:471
  43.6 39.4 %collective-permute-start.12 = (f32[36,8,128]{2,1,0:T(8,128)S(1)}, f32[36,8,128]{2,1,0:T(8,128)S(1)}, u32[]{:S(2)}, u32[]{:S(2)}) collective-permute-start(f32[36,8,128]{2,1,0:T(8,128)S(1)} %get-tuple-element.35), channel_id=1, source_target_pairs={{0,16},{1,17},{2,18},{3,19},{4,20},{5,21},{6,22},{7,23},{8,24},{9,... | collective-permute-start | bytes 442376 | tf_op jit(solution)/shard_map/ppermute | solution.py:471
  44.8 9.8 %collective-permute-start.6 = (f32[2,16,128]{2,1,0:T(8,128)S(1)}, f32[2,16,128]{2,1,0:T(8,128)S(1)}, u32[]{:S(2)}, u32[]{:S(2)}) collective-permute-start(f32[2,16,128]{2,1,0:T(8,128)S(1)} %slice.22), channel_id=1, source_target_pairs={{128,256},{143,271},{144,272},{159,287},{160,288},{175,303},{176,3... | collective-permute-start | bytes 49160 | tf_op jit(solution)/shard_map/ppermute | solution.py:471
  45.5 11.2 %collective-permute-start.3 = (f32[14,16,128]{2,1,0:T(8,128)S(1)}, f32[14,16,128]{2,1,0:T(8,128)S(1)}, u32[]{:S(2)}, u32[]{:S(2)}) collective-permute-start(f32[14,16,128]{2,1,0:T(8,128)S(1)} %broadcast_select_fusion), channel_id=1, source_target_pairs={{0,128},{1,129},{2,130},{3,131},{4,132},{5,133},{6,134},{7,135},{8... | collective-permute-start | bytes 344072 | tf_op jit(solution)/shard_map/ppermute | solution.py:471
  58.1 19.8 %collective-permute-start.7 = (f32[4,16,128]{2,1,0:T(8,128)S(1)}, f32[4,16,128]{2,1,0:T(8,128)S(1)}, u32[]{:S(2)}, u32[]{:S(2)}) collective-permute-start(f32[4,16,128]{2,1,0:T(8,128)S(1)} %get-tuple-element.30), channel_id=1, source_target_pairs={{0,1},{1,2},{2,3},{3,4},{4,5},{5,6},{6,7},{7,8},{8,9},{9,10},{10,1... | collective-permute-start | bytes 98312 | tf_op jit(solution)/shard_map/ppermute | solution.py:471
  65.4 13.5 %collective-permute-start.8 = (f32[4,16,128]{2,1,0:T(8,128)S(1)}, f32[4,16,128]{2,1,0:T(8,128)S(1)}, u32[]{:S(2)}, u32[]{:S(2)}) collective-permute-start(f32[4,16,128]{2,1,0:T(8,128)S(1)} %get-tuple-element.31), channel_id=1, source_target_pairs={{0,911},{1,0},{2,1},{3,2},{4,3},{5,4},{6,5},{7,6},{8,7},{9,8},{10,... | collective-permute-start | bytes 98312 | tf_op jit(solution)/shard_map/ppermute | solution.py:471
  79.5 9.2 %collective-permute-start.9 = (f32[16,8,128]{2,1,0:T(8,128)S(1)}, f32[16,8,128]{2,1,0:T(8,128)S(1)}, u32[]{:S(2)}, u32[]{:S(2)}) collective-permute-start(f32[16,8,128]{2,1,0:T(8,128)S(1)} %get-tuple-element.32), channel_id=1, source_target_pairs={{0,112},{1,113},{2,114},{3,115},{4,116},{5,117},{6,118},{7,119},{8... | collective-permute-start | bytes 196616 | tf_op jit(solution)/shard_map/ppermute | solution.py:471
  81.8 6.9 %collective-permute-start.10 = (f32[16,8,128]{2,1,0:T(8,128)S(1)}, f32[16,8,128]{2,1,0:T(8,128)S(1)}, u32[]{:S(2)}, u32[]{:S(2)}) collective-permute-start(f32[16,8,128]{2,1,0:T(8,128)S(1)} %get-tuple-element.33), channel_id=1, source_target_pairs={{0,16},{1,17},{2,18},{3,19},{4,20},{5,21},{6,22},{7,23},{8,24},{9,... | collective-permute-start | bytes 196616 | tf_op jit(solution)/shard_map/ppermute | solution.py:471

commit v12 on v11

--- a/solution.py
+++ b/solution.py
@@ -272,7 +272,10 @@
 def edge_rows(t_ref, w_ref, ec_ref, ev_ref, ed_ref, zl, zr, s, rows):
     lane = lanes_of(zl.shape)
     back = 128 - 32 * lax.shift_right_logical(s, 2)
-    zl, zr = pltpu.roll(zl, back, 1), pltpu.roll(zr, back, 1)
+
+    def turned(x, shift):
+        return pltpu.roll(x, lax.bitwise_and(back + shift + 128, 127), 1)
+
     for kind, e_ref in ((0, ec_ref), (1, ev_ref)):
         e = jnp.zeros(zl.shape, jnp.float32)
         for i in range(3):
@@ -280,10 +283,10 @@
             at = 32 * i
             source, where = widened(t_ref, w_ref, field)
             x = source[(*where, s, rows)]
-            e = jnp.where(between(lane, at, at + 4), roll(zl, at - 4 * field, 1), e)
+            e = jnp.where(between(lane, at, at + 4), turned(zl, at - 4 * field), e)
             e = jnp.where(between(lane, at + 4, at + 16), roll(x, at + 4, 1), e)
             e = jnp.where(between(lane, at + 16, at + 28), roll(x, at + 28, 1), e)
-            e = jnp.where(between(lane, at + 28, at + 32), roll(zr, at + 28 - 4 * field, 1), e)
+            e = jnp.where(between(lane, at + 28, at + 32), turned(zr, at + 28 - 4 * field), e)
         e_ref[s, rows] = e
     for k, d in enumerate(replicate(e)):
         ed_ref[k, s, rows] = d

time: 96.3 us -> 95.6 us (level)
  no operation moved by 1% of the time
where the time goes in v12:
time: 95.6 us; the launch traced here: 95.3 us
  starting transfers between devices  72.9 us (76%)
  Pallas kernels  17 us (18%)
  waiting for transfers between devices  3.15 us (3%)
  local copies, waits for them, and re-layouts  1.86 us (2%)
    ppermute x13, starting transfers between devices, send(): return lax.ppermute(value, AXES, pairs)  72.9 us
    pallas_call x1, Pallas kernels, local(): call(compute_late, shapes, scratch, 8, {3 + k: k for k in range(6)})  6.77 us
    ppermute x13, waiting for transfers between devices, send(): return lax.ppermute(value, AXES, pairs)  3.15 us
    pallas_call x1, Pallas kernels, local(): call(compute_early, state, [(3, *block)], 5)  3.03 us
    pallas_call x1, Pallas kernels, local(): call(own_edges, state, (), 6, {5: 0, 6: 1})(place, ac, av, zl, zr, t, w)  2.38 us
  transfers between devices with their start and end apart: 13, of which 2 were waited for; matrix products, arithmetic and copies ran while one was open for 0% of the time, Pallas kernels for 10%

profile of v12, /device:TPU:1, one launch (start us, length us, event | category | flops | bytes accessed | tf_op | source)
XLA Modules:
  0.0 95.3 jit_solution(91595325995929932)
XLA Ops:
  0.0 0.1 pad_add_fusion.place_ref
  0.1 0.0 copy-start
  0.1 0.9 copy-done
  1.0 0.6 shard_map.28
  1.6 3.9 %collective-permute-start.1 = (f32[12,16,128]{2,1,0:T(8,128)S(1)}, f32[12,16,128]{2,1,0:T(8,128)S(1)}, u32[]{:S(2)}, u32[]{:S(2)}) collective-permute-start(f32[12,16,128]{2,1,0:T(8,128)S(1)} %get-tuple-element.27), channel_id=1, source_target_pairs={{0,128},{1,129},{2,130},{3,131},{4,132},{5,133},{6,134},{7,135},{8... | collective-permute-start | bytes 294920 | tf_op jit(solution)/shard_map/ppermute | solution.py:474
  5.5 0.0 copy-start.1
  5.5 0.9 copy-done.1
  6.5 1.6 %shard_map.29 = (f32[14,16,128]{2,1,0:T(8,128)S(1)}, f32[6,4,16,128]{3,2,1,0:T(8,128)S(1)}, f32[4,16,128]{2,1,0:T(8,128)}, f32[3,8,16,128]{3,2,1,0:T(8,128)S(1)}) custom-call(s32[4]{0:T(128)S(1)} %pad_add_fusion.place_ref, f32[3,8,16,128]{3,2,1,0:T(8,128)S(1)} %copy-done.1, f32[3,8,16,128]{3,2,1,0:T(8,128)S(1)} %get-tuple-element.25.v_ref), custom_call_target="tpu_custom_call" | custom-call | tf_op jit(solution)/shard_map/pallas_call | solution.py:487
  8.0 1.9 %collective-permute-start.5 = (f32[6,4,16,128]{3,2,1,0:T(8,128)S(1)}, f32[6,4,16,128]{3,2,1,0:T(8,128)S(1)}, u32[]{:S(2)}, u32[]{:S(2)}) collective-permute-start(f32[6,4,16,128]{3,2,1,0:T(8,128)S(1)} %get-tuple-element.29), channel_id=1, source_target_pairs={{0,128},{1,129},{2,130},{3,131},{4,132},{5,133},{6,134},{7,135},{8... | collective-permute-start | bytes 589832 | tf_op jit(solution)/shard_map/ppermute | solution.py:474
  9.9 0.0 collective-permute-done.1
  10.0 0.7 collective-permute-start.2
  10.6 30.2 %collective-permute-start = (f32[14,16,128]{2,1,0:T(8,128)S(1)}, f32[14,16,128]{2,1,0:T(8,128)S(1)}, u32[]{:S(2)}, u32[]{:S(2)}) collective-permute-start(f32[14,16,128]{2,1,0:T(8,128)S(1)} %get-tuple-element.26), channel_id=1, source_target_pairs={{0,896},{1,897},{2,898},{3,899},{4,900},{5,901},{6,902},{7,903},{8... | collective-permute-start | bytes 344072 | tf_op jit(solution)/shard_map/ppermute | solution.py:474
  40.9 0.7 collective-permute-start.4
  41.6 0.0 collective-permute-done.5.b_ref
  41.6 0.8 shard_map.32
  42.4 1.2 %collective-permute-start.11 = (f32[36,8,128]{2,1,0:T(8,128)S(1)}, f32[36,8,128]{2,1,0:T(8,128)S(1)}, u32[]{:S(2)}, u32[]{:S(2)}) collective-permute-start(f32[36,8,128]{2,1,0:T(8,128)S(1)} %get-tuple-element.34), channel_id=1, source_target_pairs={{0,112},{1,113},{2,114},{3,115},{4,116},{5,117},{6,118},{7,119},{8... | collective-permute-start | bytes 442376 | tf_op jit(solution)/shard_map/ppermute | solution.py:474
  43.6 1.2 %collective-permute-start.12 = (f32[36,8,128]{2,1,0:T(8,128)S(1)}, f32[36,8,128]{2,1,0:T(8,128)S(1)}, u32[]{:S(2)}, u32[]{:S(2)}) collective-permute-start(f32[36,8,128]{2,1,0:T(8,128)S(1)} %get-tuple-element.35), channel_id=1, source_target_pairs={{0,16},{1,17},{2,18},{3,19},{4,20},{5,21},{6,22},{7,23},{8,24},{9,... | collective-permute-start | bytes 442376 | tf_op jit(solution)/shard_map/ppermute | solution.py:474
  44.8 0.0 collective-permute-done.2
  44.8 0.7 collective-permute-start.6
  45.5 0.0 collective-permute-done.ac_ref
  45.5 9.0 %collective-permute-start.3 = (f32[14,16,128]{2,1,0:T(8,128)S(1)}, f32[14,16,128]{2,1,0:T(8,128)S(1)}, u32[]{:S(2)}, u32[]{:S(2)}) collective-permute-start(f32[14,16,128]{2,1,0:T(8,128)S(1)} %broadcast_select_fusion), channel_id=1, source_target_pairs={{0,128},{1,129},{2,130},{3,131},{4,132},{5,133},{6,134},{7,135},{8... | collective-permute-start | bytes 344072 | tf_op jit(solution)/shard_map/ppermute | solution.py:474
  54.6 0.0 collective-permute-done.6
  54.6 0.0 collective-permute-done.4
  54.6 2.1 %collective-permute-done.3 = f32[14,16,128]{2,1,0:T(8,128)S(1)} collective-permute-done((f32[14,16,128]{2,1,0:T(8,128)S(1)}, f32[14,16,128]{2,1,0:T(8,128)S(1)}, u32[]{:S(2)}, u32[]{:S(2)}) %collective-permute-start.3) | collective-permute-done | bytes 114720 | tf_op jit(solution)/shard_map/ppermute | solution.py:474
  56.8 1.3 %shard_map.30 = (f32[4,16,128]{2,1,0:T(8,128)S(1)}, f32[4,16,128]{2,1,0:T(8,128)S(1)}) custom-call(s32[4]{0:T(128)S(1)} %pad_add_fusion.place_ref, f32[3,8,16,128]{3,2,1,0:T(8,128)S(1)} %get-tuple-element.28.c_ref, f32[3,8,16,128]{3,2,1,0:T(8,128)S(1)} %get-tuple-element.25.v_ref, f32[14,16,128]{2,1,0:T(8,128)S(1)} %collective-permute-done.ac_ref, ...), custom_call_target="tpu_custom_call" | custom-call | tf_op jit(solution)/shard_map/pallas_call | solution.py:500
  58.1 7.3 %collective-permute-start.7 = (f32[4,16,128]{2,1,0:T(8,128)S(1)}, f32[4,16,128]{2,1,0:T(8,128)S(1)}, u32[]{:S(2)}, u32[]{:S(2)}) collective-permute-start(f32[4,16,128]{2,1,0:T(8,128)S(1)} %get-tuple-element.30), channel_id=1, source_target_pairs={{0,1},{1,2},{2,3},{3,4},{4,5},{5,6},{6,7},{7,8},{8,9},{9,10},{10,1... | collective-permute-start | bytes 98312 | tf_op jit(solution)/shard_map/ppermute | solution.py:474
  65.4 12.5 %collective-permute-start.8 = (f32[4,16,128]{2,1,0:T(8,128)S(1)}, f32[4,16,128]{2,1,0:T(8,128)S(1)}, u32[]{:S(2)}, u32[]{:S(2)}) collective-permute-start(f32[4,16,128]{2,1,0:T(8,128)S(1)} %get-tuple-element.31), channel_id=1, source_target_pairs={{0,911},{1,0},{2,1},{3,2},{4,3},{5,4},{6,5},{7,6},{8,7},{9,8},{10,... | collective-permute-start | bytes 98312 | tf_op jit(solution)/shard_map/ppermute | solution.py:474
  77.9 0.0 collective-permute-done.7.zl_ref
  77.9 1.0 %collective-permute-done.8.zr_ref = f32[4,16,128]{2,1,0:T(8,128)S(1)} collective-permute-done((f32[4,16,128]{2,1,0:T(8,128)S(1)}, f32[4,16,128]{2,1,0:T(8,128)S(1)}, u32[]{:S(2)}, u32[]{:S(2)}) %collective-permute-start.8) | collective-permute-done | bytes 32800 | tf_op jit(solution)/shard_map/ppermute | solution.py:474
  78.9 0.6 shard_map.31
  79.5 2.3 %collective-permute-start.9 = (f32[16,8,128]{2,1,0:T(8,128)S(1)}, f32[16,8,128]{2,1,0:T(8,128)S(1)}, u32[]{:S(2)}, u32[]{:S(2)}) collective-permute-start(f32[16,8,128]{2,1,0:T(8,128)S(1)} %get-tuple-element.32), channel_id=1, source_target_pairs={{0,112},{1,113},{2,114},{3,115},{4,116},{5,117},{6,118},{7,119},{8... | collective-permute-start | bytes 196616 | tf_op jit(solution)/shard_map/ppermute | solution.py:474
  81.8 1.2 %collective-permute-start.10 = (f32[16,8,128]{2,1,0:T(8,128)S(1)}, f32[16,8,128]{2,1,0:T(8,128)S(1)}, u32[]{:S(2)}, u32[]{:S(2)}) collective-permute-start(f32[16,8,128]{2,1,0:T(8,128)S(1)} %get-tuple-element.33), channel_id=1, source_target_pairs={{0,16},{1,17},{2,18},{3,19},{4,20},{5,21},{6,22},{7,23},{8,24},{9,... | collective-permute-start | bytes 196616 | tf_op jit(solution)/shard_map/ppermute | solution.py:474
  83.0 0.0 collective-permute-done.11.above_ref
  83.1 0.0 collective-permute-done.12.below_ref
  83.1 3.0 %shard_map.33 = (f32[3,3,16,24,128]{4,3,2,1,0:T(8,128)S(1)}, f32[3,16,24,128]{3,2,1,0:T(8,128)S(1)}, f32[3,3,16,24,128]{4,3,2,1,0:T(8,128)S(1)}) custom-call(s32[4]{0:T(128)S(1)} %pad_add_fusion.place_ref, f32[3,8,16,128]{3,2,1,0:T(8,128)S(1)} %get-tuple-element.28.c_ref, f32[3,8,16,128]{3,2,1,0:T(8,128)S(1)} %get-tuple-element.25.v_ref, ...), custom_call_target="tpu_custom_call" | custom-call | tf_op jit(solution)/shard_map/pallas_call | solution.py:510
  86.1 2.4 %shard_map.34 = (f32[3,3,16,24,128]{4,3,2,1,0:T(8,128)S(1)}, f32[3,16,24,128]{3,2,1,0:T(8,128)S(1)}, f32[16,24,128]{2,1,0:T(8,128)S(1)}, f32[16,24,128]{2,1,0:T(8,128)S(1)}, f32[3,16,24,128]{3,2,1,0:T(8,128)S(1)}) custom-call(s32[4]{0:T(128)S(1)} %pad_add_fusion.place_ref, ...), custom_call_target="tpu_custom_call", output_to_operand_aliasing={{0}: (5, {}), {1}: (6, {})} | custom-call | tf_op jit(solution)/shard_map/pallas_call | solution.py:514
  88.5 0.0 collective-permute-done.9.above_ref
  88.5 0.0 collective-permute-done.10.below_ref
  88.5 6.8 %shard_map.35 = (f32[3,3,16,24,128]{4,3,2,1,0:T(8,128)S(1)}, f32[3,16,24,128]{3,2,1,0:T(8,128)S(1)}, f32[3,3,16,24,128]{4,3,2,1,0:T(8,128)S(1)}, f32[16,24,128]{...) custom-call(s32[4]{0:T(128)S(1)} %pad_add_fusion.place_ref, ...), custom_call_target="tpu_custom_call", output_to_operand_aliasing={{0}: (3, {}), {1}: (4, {}), {2}: (5, {}), {3}: (6, {}), {4}... | custom-call | tf_op jit(solution)/shard_map/pallas_call | solution.py:520
  (8 shorter events, 0.1 us)
Async XLA Ops:
  0.1 0.9 copy-start
  1.6 8.4 %collective-permute-start.1 = (f32[12,16,128]{2,1,0:T(8,128)S(1)}, f32[12,16,128]{2,1,0:T(8,128)S(1)}, u32[]{:S(2)}, u32[]{:S(2)}) collective-permute-start(f32[12,16,128]{2,1,0:T(8,128)S(1)} %get-tuple-element.27), channel_id=1, source_target_pairs={{0,128},{1,129},{2,130},{3,131},{4,132},{5,133},{6,134},{7,135},{8... | collective-permute-start | bytes 294920 | tf_op jit(solution)/shard_map/ppermute | solution.py:474
  5.5 0.9 copy-start.1
  8.0 33.6 %collective-permute-start.5 = (f32[6,4,16,128]{3,2,1,0:T(8,128)S(1)}, f32[6,4,16,128]{3,2,1,0:T(8,128)S(1)}, u32[]{:S(2)}, u32[]{:S(2)}) collective-permute-start(f32[6,4,16,128]{3,2,1,0:T(8,128)S(1)} %get-tuple-element.29), channel_id=1, source_target_pairs={{0,128},{1,129},{2,130},{3,131},{4,132},{5,133},{6,134},{7,135},{8... | collective-permute-start | bytes 589832 | tf_op jit(solution)/shard_map/ppermute | solution.py:474
  10.0 34.8 %collective-permute-start.2 = (f32[14,16,128]{2,1,0:T(8,128)S(1)}, f32[14,16,128]{2,1,0:T(8,128)S(1)}, u32[]{:S(2)}, u32[]{:S(2)}) collective-permute-start(f32[14,16,128]{2,1,0:T(8,128)S(1)} %pad_maximum_fusion), channel_id=1, source_target_pairs={{128,768},{129,769},{130,770},{131,771},{132,772},{133,773},{134,7... | collective-permute-start | bytes 344072 | tf_op jit(solution)/shard_map/ppermute | solution.py:474
  10.6 34.8 %collective-permute-start = (f32[14,16,128]{2,1,0:T(8,128)S(1)}, f32[14,16,128]{2,1,0:T(8,128)S(1)}, u32[]{:S(2)}, u32[]{:S(2)}) collective-permute-start(f32[14,16,128]{2,1,0:T(8,128)S(1)} %get-tuple-element.26), channel_id=1, source_target_pairs={{0,896},{1,897},{2,898},{3,899},{4,900},{5,901},{6,902},{7,903},{8... | collective-permute-start | bytes 344072 | tf_op jit(solution)/shard_map/ppermute | solution.py:474
  40.9 13.7 %collective-permute-start.4 = (f32[12,16,128]{2,1,0:T(8,128)S(1)}, f32[12,16,128]{2,1,0:T(8,128)S(1)}, u32[]{:S(2)}, u32[]{:S(2)}) collective-permute-start(f32[12,16,128]{2,1,0:T(8,128)S(1)} %get-tuple-element.27), channel_id=1, source_target_pairs={{128,256},{129,257},{130,258},{131,259},{132,260},{133,261},{134,2... | collective-permute-start | bytes 294920 | tf_op jit(solution)/shard_map/ppermute | solution.py:474
  42.4 40.7 %collective-permute-start.11 = (f32[36,8,128]{2,1,0:T(8,128)S(1)}, f32[36,8,128]{2,1,0:T(8,128)S(1)}, u32[]{:S(2)}, u32[]{:S(2)}) collective-permute-start(f32[36,8,128]{2,1,0:T(8,128)S(1)} %get-tuple-element.34), channel_id=1, source_target_pairs={{0,112},{1,113},{2,114},{3,115},{4,116},{5,117},{6,118},{7,119},{8... | collective-permute-start | bytes 442376 | tf_op jit(solution)/shard_map/ppermute | solution.py:474
  43.6 39.4 %collective-permute-start.12 = (f32[36,8,128]{2,1,0:T(8,128)S(1)}, f32[36,8,128]{2,1,0:T(8,128)S(1)}, u32[]{:S(2)}, u32[]{:S(2)}) collective-permute-start(f32[36,8,128]{2,1,0:T(8,128)S(1)} %get-tuple-element.35), channel_id=1, source_target_pairs={{0,16},{1,17},{2,18},{3,19},{4,20},{5,21},{6,22},{7,23},{8,24},{9,... | collective-permute-start | bytes 442376 | tf_op jit(solution)/shard_map/ppermute | solution.py:474
  44.8 9.8 %collective-permute-start.6 = (f32[2,16,128]{2,1,0:T(8,128)S(1)}, f32[2,16,128]{2,1,0:T(8,128)S(1)}, u32[]{:S(2)}, u32[]{:S(2)}) collective-permute-start(f32[2,16,128]{2,1,0:T(8,128)S(1)} %slice.22), channel_id=1, source_target_pairs={{128,256},{143,271},{144,272},{159,287},{160,288},{175,303},{176,3... | collective-permute-start | bytes 49160 | tf_op jit(solution)/shard_map/ppermute | solution.py:474
  45.5 11.2 %collective-permute-start.3 = (f32[14,16,128]{2,1,0:T(8,128)S(1)}, f32[14,16,128]{2,1,0:T(8,128)S(1)}, u32[]{:S(2)}, u32[]{:S(2)}) collective-permute-start(f32[14,16,128]{2,1,0:T(8,128)S(1)} %broadcast_select_fusion), channel_id=1, source_target_pairs={{0,128},{1,129},{2,130},{3,131},{4,132},{5,133},{6,134},{7,135},{8... | collective-permute-start | bytes 344072 | tf_op jit(solution)/shard_map/ppermute | solution.py:474
  58.1 19.8 %collective-permute-start.7 = (f32[4,16,128]{2,1,0:T(8,128)S(1)}, f32[4,16,128]{2,1,0:T(8,128)S(1)}, u32[]{:S(2)}, u32[]{:S(2)}) collective-permute-start(f32[4,16,128]{2,1,0:T(8,128)S(1)} %get-tuple-element.30), channel_id=1, source_target_pairs={{0,1},{1,2},{2,3},{3,4},{4,5},{5,6},{6,7},{7,8},{8,9},{9,10},{10,1... | collective-permute-start | bytes 98312 | tf_op jit(solution)/shard_map/ppermute | solution.py:474
  65.4 13.5 %collective-permute-start.8 = (f32[4,16,128]{2,1,0:T(8,128)S(1)}, f32[4,16,128]{2,1,0:T(8,128)S(1)}, u32[]{:S(2)}, u32[]{:S(2)}) collective-permute-start(f32[4,16,128]{2,1,0:T(8,128)S(1)} %get-tuple-element.31), channel_id=1, source_target_pairs={{0,911},{1,0},{2,1},{3,2},{4,3},{5,4},{6,5},{7,6},{8,7},{9,8},{10,... | collective-permute-start | bytes 98312 | tf_op jit(solution)/shard_map/ppermute | solution.py:474
  79.5 9.0 %collective-permute-start.9 = (f32[16,8,128]{2,1,0:T(8,128)S(1)}, f32[16,8,128]{2,1,0:T(8,128)S(1)}, u32[]{:S(2)}, u32[]{:S(2)}) collective-permute-start(f32[16,8,128]{2,1,0:T(8,128)S(1)} %get-tuple-element.32), channel_id=1, source_target_pairs={{0,112},{1,113},{2,114},{3,115},{4,116},{5,117},{6,118},{7,119},{8... | collective-permute-start | bytes 196616 | tf_op jit(solution)/shard_map/ppermute | solution.py:474
  81.8 6.7 %collective-permute-start.10 = (f32[16,8,128]{2,1,0:T(8,128)S(1)}, f32[16,8,128]{2,1,0:T(8,128)S(1)}, u32[]{:S(2)}, u32[]{:S(2)}) collective-permute-start(f32[16,8,128]{2,1,0:T(8,128)S(1)} %get-tuple-element.33), channel_id=1, source_target_pairs={{0,16},{1,17},{2,18},{3,19},{4,20},{5,21},{6,22},{7,23},{8,24},{9,... | collective-permute-start | bytes 196616 | tf_op jit(solution)/shard_map/ppermute | solution.py:474
